TPU v7x, 32 devices: a whole 2x2x4 slice. The times are simulated.
32 devices in a mesh: seq: 8 (over z, y), shard: 4 (over x, core).
Axes of the slice: x: 2, y: 2, z: 4, core: 2. Of those that a mesh axis runs over, the one named last changes fastest.
Arguments:
- tokens: bfloat16 [8, 4096, 768], P('shard', 'seq'), may hold values from -6 to 6
- segments: int32 [8, 4096], P('shard'), may hold values from 0 to 20, as said below
- positions: int32 [8, 4096], P('shard', 'seq'), may hold values from 0 to 1999, as said below
- cotangent: bfloat16 [8, 4096, 768], P('shard', 'seq'), may hold values from -6 to 6
- w_qkv: bfloat16 [768, 2304], P('shard'), may hold values from -0.21875 to 0.21875
- w_out: bfloat16 [768, 768], P('shard'), may hold values from -3 to 3
- w_gate: bfloat16 [768, 3072], P('shard'), may hold values from -0.21875 to 0.21875
- w_up: bfloat16 [768, 3072], P('shard'), may hold values from -0.21875 to 0.21875
- w_down: bfloat16 [3072, 768], P('shard'), may hold values from -0.109375 to 0.109375
- ln1_gain: bfloat16 [768], P('shard'), may hold values from 0.099609375 to 1.8984375
- ln1_bias: bfloat16 [768], P('shard'), may hold values from -3 to 3
- ln2_gain: bfloat16 [768], P('shard'), may hold values from 0.099609375 to 1.8984375
- ln2_bias: bfloat16 [768], P('shard'), may hold values from -3 to 3
Outputs:
- output: bfloat16 [8, 4096, 768], P('shard', 'seq')
- input_grad: bfloat16 [8, 4096, 768], P('shard', 'seq')
- grad_w_qkv: float32 [768, 2304], P('shard')
- grad_w_out: float32 [768, 768], P('shard')
- grad_w_gate: float32 [768, 3072], P('shard')
- grad_w_up: float32 [768, 3072], P('shard')
- grad_w_down: float32 [3072, 768], P('shard')
- grad_ln1_gain: float32 [768], P('shard')
- grad_ln1_bias: float32 [768], P('shard')
- grad_ln2_gain: float32 [768], P('shard')
- grad_ln2_bias: float32 [768], P('shard')
Inputs may be any that keep to these rules, and one draw needn't show every extreme that they name: segments[s, t] numbers the documents of sequence s in order from 0 and never falls along t; every document has 200 to 2000 tokens, except that the end of the sequence may cut the last one short. positions[s, t] counts the earlier tokens of the same document of sequence s.
All inputs are finite; a program needn't handle non-finite values.
Results may differ from a plain program's by a relative error of at most 0.025.
Values may be sent and summed in bfloat16 or wider, within the bound.
A program may use at most 256 MiB of HBM per device.

v0:
```python
import math

import jax
import jax.numpy as jnp
from jax import lax
from jax.sharding import PartitionSpec as P

HEADS = 12
HD = 64


EPS = 1e-05
ROPE_BASE = 1000.0


def rope_tables(pos_block):
    half_dim = HD // 2
    freqs = jnp.exp(jnp.arange(half_dim, dtype=jnp.float32) * (-math.log(ROPE_BASE) / half_dim))
    angle = pos_block.astype(jnp.float32)[..., None] * freqs
    return (jnp.cos(angle)[:, :, None, :], jnp.sin(angle)[:, :, None, :])


def rotate(heads, cos_b, sin_b):
    half_dim = heads.shape[-1] // 2
    first = heads[..., :half_dim]
    second = heads[..., half_dim:]
    return jnp.concatenate(
        [first * cos_b - second * sin_b, second * cos_b + first * sin_b], axis=-1
    )


def rotate_back(grads, cos_b, sin_b):
    half_dim = grads.shape[-1] // 2
    first = grads[..., :half_dim]
    second = grads[..., half_dim:]
    return jnp.concatenate(
        [first * cos_b + second * sin_b, second * cos_b - first * sin_b], axis=-1
    )


def norm_fwd(values, gain, bias):
    mean_val = jnp.mean(values, axis=-1, keepdims=True)
    centered = values - mean_val
    variance = jnp.mean(centered * centered, axis=-1, keepdims=True)
    inverse = lax.rsqrt(variance + EPS)
    normed = centered * inverse
    return (normed * gain + bias, normed, inverse)


def norm_back(grad_in, normed, inverse, gain):
    scaled = grad_in * gain
    return inverse * (
        scaled
        - jnp.mean(scaled, axis=-1, keepdims=True)
        - normed * jnp.mean(scaled * normed, axis=-1, keepdims=True)
    )


def head_split(block_rows, seq_count, row_count):
    return block_rows.reshape(seq_count, row_count, HEADS, HD)


def attend(q_heads, q_seg, k_full, v_full, seg_all, block, score_scale):
    seq_count, row_count = (q_heads.shape[0], q_heads.shape[1])
    block_count = k_full.shape[1] // block

    def attend_step(carry, index):
        row_total, value_sum = carry
        start = index * block
        k_part = head_split(lax.dynamic_slice_in_dim(k_full, start, block, 1), seq_count, block)
        v_part = head_split(lax.dynamic_slice_in_dim(v_full, start, block, 1), seq_count, block)
        seg_part = lax.dynamic_slice_in_dim(seg_all, start, block, 1)
        raw = (
            jnp.einsum("sqhd,skhd->shqk", q_heads, k_part, preferred_element_type=jnp.float32)
            * score_scale
        )
        same_doc = q_seg[:, None, :, None] == seg_part[:, None, None, :]
        expo = jnp.where(same_doc, jnp.exp(raw), 0.0)
        row_total = row_total + jnp.sum(expo, axis=-1)
        value_sum = value_sum + jnp.einsum(
            "shqk,skhd->sqhd", expo.astype(jnp.bfloat16), v_part, preferred_element_type=jnp.float32
        )
        return ((row_total, value_sum), None)

    start_carry = (
        jnp.zeros((seq_count, HEADS, row_count), jnp.float32),
        jnp.zeros((seq_count, row_count, HEADS, HD), jnp.float32),
    )
    final, unused = lax.scan(attend_step, start_carry, jnp.arange(block_count, dtype=jnp.int32))
    return final


def back_keys(q_heads, g_heads, delta, q_seg, k_full, v_full, seg_all, block, score_scale):
    seq_count, row_count = (q_heads.shape[0], q_heads.shape[1])
    full_len = k_full.shape[1]
    block_count = full_len // block

    def back_step(carry, index):
        start = index * block
        k_part = head_split(lax.dynamic_slice_in_dim(k_full, start, block, 1), seq_count, block)
        v_part = head_split(lax.dynamic_slice_in_dim(v_full, start, block, 1), seq_count, block)
        seg_part = lax.dynamic_slice_in_dim(seg_all, start, block, 1)
        raw = (
            jnp.einsum("sqhd,skhd->shqk", q_heads, k_part, preferred_element_type=jnp.float32)
            * score_scale
        )
        same_doc = q_seg[:, None, :, None] == seg_part[:, None, None, :]
        expo = jnp.where(same_doc, jnp.exp(raw), 0.0)
        prob_grad = jnp.einsum(
            "sqhd,skhd->shqk", g_heads, v_part, preferred_element_type=jnp.float32
        )
        d_score = (expo * (prob_grad - delta[..., None])).astype(jnp.bfloat16)
        q_grad = carry[0] + jnp.einsum(
            "shqk,skhd->sqhd", d_score, k_part, preferred_element_type=jnp.float32
        )
        k_grad = (
            jnp.einsum("shqk,sqhd->skhd", d_score, q_heads, preferred_element_type=jnp.float32)
            * score_scale
        )
        v_grad = jnp.einsum(
            "shqk,sqhd->skhd",
            expo.astype(jnp.bfloat16),
            g_heads,
            preferred_element_type=jnp.float32,
        )
        k_store = lax.dynamic_update_slice_in_dim(
            carry[1], k_grad.reshape(seq_count, block, HEADS * HD), start, 1
        )
        v_store = lax.dynamic_update_slice_in_dim(
            carry[2], v_grad.reshape(seq_count, block, HEADS * HD), start, 1
        )
        return ((q_grad, k_store, v_store), None)

    q_zero = jnp.zeros((seq_count, row_count, HEADS, HD), jnp.float32)
    kv_zero = jnp.zeros((seq_count, full_len, HEADS * HD), jnp.float32)
    start_carry = (q_zero, kv_zero, kv_zero)
    final, unused = lax.scan(back_step, start_carry, jnp.arange(block_count, dtype=jnp.int32))
    return (final[0] * score_scale,) + tuple(final[1:])


def local(
    tokens,
    segments,
    positions,
    cotangent,
    w_qkv,
    w_out,
    w_gate,
    w_up,
    w_down,
    ln1_gain,
    ln1_bias,
    ln2_gain,
    ln2_bias,
):
    seq_count, row_count, model_width = tokens.shape
    score_scale = HD ** (-0.5)
    q_seg = lax.dynamic_slice_in_dim(segments, lax.axis_index("seq") * row_count, row_count, 1)
    gathered = (
        lax.all_gather(w_qkv, "shard", axis=0, tiled=True),
        lax.all_gather(w_out, "shard", axis=0, tiled=True),
        lax.all_gather(w_gate, "shard", axis=0, tiled=True),
        lax.all_gather(w_up, "shard", axis=0, tiled=True),
        lax.all_gather(w_down, "shard", axis=0, tiled=True),
        lax.all_gather(ln1_gain, "shard", axis=0, tiled=True),
        lax.all_gather(ln1_bias, "shard", axis=0, tiled=True),
        lax.all_gather(ln2_gain, "shard", axis=0, tiled=True),
        lax.all_gather(ln2_bias, "shard", axis=0, tiled=True),
    )
    full_qkv, full_out, full_gate, full_up, full_down, gain_one, bias_one, gain_two, bias_two = (
        gathered
    )
    cos_b, sin_b = rope_tables(positions)
    qkv_all = jnp.einsum("scd,de->sce", tokens, full_qkv, preferred_element_type=jnp.float32)
    q_heads = rotate(
        head_split(qkv_all[..., :model_width], seq_count, row_count), cos_b, sin_b
    ).astype(jnp.bfloat16)
    k_heads = rotate(
        head_split(qkv_all[..., model_width : 2 * model_width], seq_count, row_count), cos_b, sin_b
    ).astype(jnp.bfloat16)
    v_heads = head_split(qkv_all[..., 2 * model_width :], seq_count, row_count).astype(jnp.bfloat16)
    k_local = k_heads.reshape(seq_count, row_count, model_width)
    v_local = v_heads.reshape(seq_count, row_count, model_width)
    k_full, v_full = (
        lax.all_gather(k_local, "seq", axis=1, tiled=True),
        lax.all_gather(v_local, "seq", axis=1, tiled=True),
    )
    row_total, value_sum = attend(q_heads, q_seg, k_full, v_full, segments, row_count, score_scale)
    denom = jnp.transpose(row_total, (0, 2, 1))[..., None]
    attn_out = value_sum / denom
    joined = attn_out.reshape(seq_count, row_count, model_width).astype(jnp.bfloat16)
    tokens_f = tokens.astype(jnp.float32)
    h_one = tokens_f + jnp.einsum(
        "sci,io->sco", joined, full_out, preferred_element_type=jnp.float32
    )
    x_one, normed_one, inverse_one = norm_fwd(
        h_one, gain_one.astype(jnp.float32), bias_one.astype(jnp.float32)
    )
    x_low = x_one.astype(jnp.bfloat16)
    gate_pre = jnp.einsum("scd,df->scf", x_low, full_gate, preferred_element_type=jnp.float32)
    up_pre = jnp.einsum("scd,df->scf", x_low, full_up, preferred_element_type=jnp.float32)
    sigma = jax.nn.sigmoid(gate_pre)
    smooth = gate_pre * sigma
    hidden = (smooth * up_pre).astype(jnp.bfloat16)
    h_two = x_one + jnp.einsum("scf,fd->scd", hidden, full_down, preferred_element_type=jnp.float32)
    result, normed_two, inverse_two = norm_fwd(
        h_two, gain_two.astype(jnp.float32), bias_two.astype(jnp.float32)
    )
    output = result.astype(jnp.bfloat16)
    regathered = (
        lax.all_gather(w_qkv, "shard", axis=0, tiled=True),
        lax.all_gather(w_out, "shard", axis=0, tiled=True),
        lax.all_gather(w_gate, "shard", axis=0, tiled=True),
        lax.all_gather(w_up, "shard", axis=0, tiled=True),
        lax.all_gather(w_down, "shard", axis=0, tiled=True),
        lax.all_gather(ln1_gain, "shard", axis=0, tiled=True),
        lax.all_gather(ln2_gain, "shard", axis=0, tiled=True),
    )
    back_qkv, back_out, back_gate, back_up, back_down, back_gain_one, back_gain_two = regathered
    back_k, back_v = (
        lax.all_gather(k_local, "seq", axis=1, tiled=True),
        lax.all_gather(v_local, "seq", axis=1, tiled=True),
    )
    cot_f = cotangent.astype(jnp.float32)
    grad_gain_two = jnp.sum(cot_f * normed_two, axis=(0, 1))
    grad_bias_two = jnp.sum(cot_f, axis=(0, 1))
    dh_two = norm_back(cot_f, normed_two, inverse_two, back_gain_two.astype(jnp.float32))
    dm_low = dh_two.astype(jnp.bfloat16)
    grad_down = jnp.einsum("scf,scd->fd", hidden, dm_low, preferred_element_type=jnp.float32)
    d_hidden = jnp.einsum("scd,fd->scf", dm_low, back_down, preferred_element_type=jnp.float32)
    d_up = (d_hidden * smooth).astype(jnp.bfloat16)
    d_gate = (d_hidden * up_pre * sigma * (1.0 + gate_pre * (1.0 - sigma))).astype(jnp.bfloat16)
    grad_gate = jnp.einsum("scd,scf->df", x_low, d_gate, preferred_element_type=jnp.float32)
    grad_up = jnp.einsum("scd,scf->df", x_low, d_up, preferred_element_type=jnp.float32)
    dx_one = (
        dh_two
        + jnp.einsum("scf,df->scd", d_gate, back_gate, preferred_element_type=jnp.float32)
        + jnp.einsum("scf,df->scd", d_up, back_up, preferred_element_type=jnp.float32)
    )
    grad_gain_one = jnp.sum(dx_one * normed_one, axis=(0, 1))
    grad_bias_one = jnp.sum(dx_one, axis=(0, 1))
    dh_one = norm_back(dx_one, normed_one, inverse_one, back_gain_one.astype(jnp.float32))
    d_attn = dh_one.astype(jnp.bfloat16)
    grad_out = jnp.einsum("sci,sco->io", joined, d_attn, preferred_element_type=jnp.float32)
    d_joined = jnp.einsum(
        "sco,io->sci", d_attn, back_out, preferred_element_type=jnp.float32
    ).astype(jnp.bfloat16)
    d_heads = head_split(d_joined, seq_count, row_count).astype(jnp.float32)
    g_heads = (d_heads / denom).astype(jnp.bfloat16)
    delta = jnp.transpose(jnp.sum(d_heads * attn_out, axis=-1) / denom[..., 0], (0, 2, 1))
    q_grad, k_all, v_all = back_keys(
        q_heads, g_heads, delta, q_seg, back_k, back_v, segments, row_count, score_scale
    )
    k_sum, v_sum = (
        lax.psum_scatter(k_all.astype(jnp.bfloat16), "seq", scatter_dimension=1, tiled=True).astype(
            jnp.float32
        ),
        lax.psum_scatter(v_all.astype(jnp.bfloat16), "seq", scatter_dimension=1, tiled=True).astype(
            jnp.float32
        ),
    )
    k_grad = head_split(k_sum, seq_count, row_count)
    v_grad = head_split(v_sum, seq_count, row_count)
    q_back = rotate_back(q_grad, cos_b, sin_b).reshape(seq_count, row_count, model_width)
    k_back = rotate_back(k_grad, cos_b, sin_b).reshape(seq_count, row_count, model_width)
    d_qkv = jnp.concatenate(
        [q_back, k_back, v_grad.reshape(seq_count, row_count, model_width)], axis=-1
    ).astype(jnp.bfloat16)
    grad_qkv = jnp.einsum("scd,sce->de", tokens, d_qkv, preferred_element_type=jnp.float32)
    d_tokens = dh_one + jnp.einsum(
        "sce,de->scd", d_qkv, back_qkv, preferred_element_type=jnp.float32
    )
    input_grad = d_tokens.astype(jnp.bfloat16)
    owned = (
        lax.psum_scatter(
            grad_qkv.astype(jnp.bfloat16), "shard", scatter_dimension=0, tiled=True
        ).astype(jnp.float32),
        lax.psum_scatter(
            grad_out.astype(jnp.bfloat16), "shard", scatter_dimension=0, tiled=True
        ).astype(jnp.float32),
        lax.psum_scatter(
            grad_gate.astype(jnp.bfloat16), "shard", scatter_dimension=0, tiled=True
        ).astype(jnp.float32),
        lax.psum_scatter(
            grad_up.astype(jnp.bfloat16), "shard", scatter_dimension=0, tiled=True
        ).astype(jnp.float32),
        lax.psum_scatter(
            grad_down.astype(jnp.bfloat16), "shard", scatter_dimension=0, tiled=True
        ).astype(jnp.float32),
        lax.psum_scatter(
            grad_gain_one.astype(jnp.bfloat16), "shard", scatter_dimension=0, tiled=True
        ).astype(jnp.float32),
        lax.psum_scatter(
            grad_bias_one.astype(jnp.bfloat16), "shard", scatter_dimension=0, tiled=True
        ).astype(jnp.float32),
        lax.psum_scatter(
            grad_gain_two.astype(jnp.bfloat16), "shard", scatter_dimension=0, tiled=True
        ).astype(jnp.float32),
        lax.psum_scatter(
            grad_bias_two.astype(jnp.bfloat16), "shard", scatter_dimension=0, tiled=True
        ).astype(jnp.float32),
    )
    summed = (
        lax.psum(owned[0].astype(jnp.bfloat16), "seq").astype(jnp.float32),
        lax.psum(owned[1].astype(jnp.bfloat16), "seq").astype(jnp.float32),
        lax.psum(owned[2].astype(jnp.bfloat16), "seq").astype(jnp.float32),
        lax.psum(owned[3].astype(jnp.bfloat16), "seq").astype(jnp.float32),
        lax.psum(owned[4].astype(jnp.bfloat16), "seq").astype(jnp.float32),
        lax.psum(owned[5].astype(jnp.bfloat16), "seq").astype(jnp.float32),
        lax.psum(owned[6].astype(jnp.bfloat16), "seq").astype(jnp.float32),
        lax.psum(owned[7].astype(jnp.bfloat16), "seq").astype(jnp.float32),
        lax.psum(owned[8].astype(jnp.bfloat16), "seq").astype(jnp.float32),
    )
    return (
        output,
        input_grad,
        summed[0],
        summed[1],
        summed[2],
        summed[3],
        summed[4],
        summed[5],
        summed[6],
        summed[7],
        summed[8],
    )


def solution(mesh):
    in_specs = (
        P("shard", "seq", None),
        P("shard", None),
        P("shard", "seq"),
        P("shard", "seq", None),
        P("shard", None),
        P("shard", None),
        P("shard", None),
        P("shard", None),
        P("shard", None),
        P("shard"),
        P("shard"),
        P("shard"),
        P("shard"),
    )
    out_specs = (
        P("shard", "seq", None),
        P("shard", "seq", None),
        P("shard", None),
        P("shard", None),
        P("shard", None),
        P("shard", None),
        P("shard", None),
        P("shard"),
        P("shard"),
        P("shard"),
        P("shard"),
    )
    return jax.shard_map(local, mesh=mesh, in_specs=in_specs, out_specs=out_specs, check_vma=False)
```

profile of v0, /device:TPU:20, one launch (start us, length us, event | category | flops | bytes accessed | tf_op | source)
XLA Modules:
  0.0 2134.9 jit_solution(6114114731520905912)
XLA Ops:
  8.0 33.4 %all-gather.8.cloned.1.call-done = bf16[768,2304]{1,0:T(8,128)(2,1)} async-done(((bf16[192,2304]{1,0:T(8,128)(2,1)}), bf16[768,2304]{1,0:T(8,128)(2,1)}) %all-gather.8.cloned.1.call-update) | async-done | bytes 3538960 | tf_op jit(solution)/shard_map/all_gather | solution.py:160
  84.0 143.0 %all-gather.12.cloned.1.call-done = bf16[2,4096,768]{2,1,0:T(8,128)(2,1)} async-done(((bf16[2,512,768]{2,1,0:T(8,128)(2,1)}), bf16[2,4096,768]{2,1,0:T(8,128)(2,1)}) %all-gather.12.cloned.1.call-update) | async-done | bytes 12582928 | tf_op jit(solution)/shard_map/all_gather | solution.py:186
  227.0 16.1 copy.69
  243.1 160.8 %all-gather.10.cloned.1.call-done = bf16[2,4096,768]{1,2,0:T(8,128)(2,1)} async-done(((bf16[2,512,768]{1,2,0:T(8,128)(2,1)}), bf16[2,4096,768]{1,2,0:T(8,128)(2,1)}) %all-gather.10.cloned.1.call-update) | async-done | bytes 12582928 | tf_op jit(solution)/shard_map/all_gather | solution.py:185
  403.9 237.1 %while.28 = (s32[]{:T(128)}, f32[2,12,512]{2,1,0:T(8,128)S(1)}, f32[2,512,12,64]{1,3,2,0:T(8,128)}, s32[2,512]{1,0:T(2,128)S(1)}, s32[8]{0:T(128)S(1)}, /*index=...) while((s32[]{:T(128)}, f32[2,12,512]{2,1,0:T(8,128)S(1)}, ...), condition=%wide.region_2.3_spmd.clone, body=%wide.region_0.2_spmd.clone.sunk | while | flops 1650470912 | bytes 71516400 | solution.py:89
  408.6 11.4 fusion.117
  420.0 12.5 bitcast_add_fusion.4
  437.2 11.4 fusion.117
  448.6 13.5 bitcast_add_fusion.4
  466.7 12.3 fusion.117
  479.0 13.5 bitcast_add_fusion.4
  497.2 11.6 fusion.117
  508.7 14.6 bitcast_add_fusion.4
  528.1 11.5 fusion.117
  539.5 13.4 bitcast_add_fusion.4
  557.5 11.4 fusion.117
  568.9 13.4 bitcast_add_fusion.4
  586.9 11.4 fusion.117
  598.3 13.4 bitcast_add_fusion.4
  616.3 11.4 fusion.117
  627.7 13.4 bitcast_add_fusion.4
  650.1 10.8 fusion.31
  660.9 13.7 multiply_convert_fusion.2
  674.6 9.2 fusion.65
  690.3 18.8 multiply_convert_fusion.1
  709.1 10.4 fusion.25
  719.6 10.4 multiply_reduce_fusion
  754.8 533.9 %while.29 = (s32[]{:T(128)}, f32[2,512,12,64]{1,3,2,0:T(8,128)}, bf16[2,4096,768]{1,2,0:T(8,128)(2,1)}, bf16[2,4096,768]{2,1,0:T(8,128)(2,1)}, s32[8]{0:T(128)S(...) while((s32[]{:T(128)}, f32[2,512,12,64]{1,3,2,0:T(8,128)}, ...), condition=%wide.region_13.14_spmd.clone, body=%wide.region_12.13_spmd.clone.sunk | while | flops 4080533504 | bytes 159449392 | solution.py:137
  759.6 10.1 fusion.128
  771.5 15.9 fusion.129
  806.3 11.7 fusion.130
  825.5 10.1 fusion.128
  837.4 15.9 fusion.129
  873.1 11.7 fusion.130
  892.3 10.1 fusion.128
  904.2 15.9 fusion.129
  939.9 11.7 fusion.130
  959.1 10.1 fusion.128
  971.1 15.9 fusion.129
  1006.7 11.7 fusion.130
  1026.0 10.1 fusion.128
  1038.0 15.9 fusion.129
  1073.6 11.7 fusion.130
  1092.8 10.1 fusion.128
  1104.8 15.9 fusion.129
  1140.4 11.7 fusion.130
  1159.6 10.1 fusion.128
  1171.6 15.9 fusion.129
  1207.3 11.7 fusion.130
  1226.5 10.1 fusion.128
  1238.4 15.9 fusion.129
  1274.1 11.7 fusion.130
  1292.9 203.3 %reduce-scatter.10.cloned.1.call-done = bf16[2,512,768]{1,2,0:T(8,128)(2,1)} async-done(((bf16[2,4096,768]{1,2,0:T(8,128)(2,1)}), bf16[2,512,768]{1,2,0:T(8,128)(2,1)}) %reduce-scatter.10.cloned.1.call-update) | async-done | bytes 1572880 | tf_op jit(solution)/shard_map/reduce_scatter | solution.py:255
  1503.6 202.7 %reduce-scatter.12.cloned.1.call-done = bf16[2,512,768]{2,1,0:T(8,128)(2,1)} async-done(((bf16[2,4096,768]{2,1,0:T(8,128)(2,1)}), bf16[2,512,768]{2,1,0:T(8,128)(2,1)}) %reduce-scatter.12.cloned.1.call-update) | async-done | bytes 1572880 | tf_op jit(solution)/shard_map/reduce_scatter | solution.py:258
  1722.9 9.4 bitcast_convert_fusion.2
  1733.7 10.2 bitcast_convert_fusion.1
  1745.3 9.8 bitcast_convert_fusion
  1760.0 26.5 %reduce-scatter.14.cloned.1.call-done = bf16[192,768]{1,0:T(8,128)(2,1)} async-done(((bf16[768,768]{1,0:T(8,128)(2,1)}), bf16[192,768]{1,0:T(8,128)(2,1)}) %reduce-scatter.14.cloned.1.call-update) | async-done | bytes 294928 | tf_op jit(solution)/shard_map/reduce_scatter | solution.py:278
  1786.4 50.4 %reduce-scatter.16.cloned.1.call-done = bf16[192,3072]{1,0:T(8,128)(2,1)} async-done(((bf16[768,3072]{1,0:T(8,128)(2,1)}), bf16[192,3072]{1,0:T(8,128)(2,1)}) %reduce-scatter.16.cloned.1.call-update) | async-done | bytes 1179664 | tf_op jit(solution)/shard_map/reduce_scatter | solution.py:281
  1836.8 50.5 %reduce-scatter.18.cloned.1.call-done = bf16[192,3072]{1,0:T(8,128)(2,1)} async-done(((bf16[768,3072]{1,0:T(8,128)(2,1)}), bf16[192,3072]{1,0:T(8,128)(2,1)}) %reduce-scatter.18.cloned.1.call-update) | async-done | bytes 1179664 | tf_op jit(solution)/shard_map/reduce_scatter | solution.py:284
  1887.4 50.4 %reduce-scatter.20.cloned.1.call-done = bf16[768,768]{1,0:T(8,128)(2,1)} async-done(((bf16[3072,768]{1,0:T(8,128)(2,1)}), bf16[768,768]{1,0:T(8,128)(2,1)}) %reduce-scatter.20.cloned.1.call-update) | async-done | bytes 1179664 | tf_op jit(solution)/shard_map/reduce_scatter | solution.py:287
  1940.6 10.2 all-reduce.10
  1951.1 17.3 all-reduce.8
  1980.4 139.0 %all-reduce.14.cloned.1.call-done = (bf16[192,2304]{0,1:T(8,128)(2,1)}, bf16[192,768]{1,0:T(8,128)(2,1)}, bf16[192,3072]{1,0:T(8,128)(2,1)}, bf16[192,3072]{1,0:T(8,128)(2,1)}, bf16[768,768]{1,0:T(8,128)(2,1)}) async-done(((bf16[192,2304]{0,1:T(8,128)(2,1)}, bf16[192,768]{1,0:T(8,128)(2,1)}, bf16[192,3072]{1,0:T(8,128)(2,1)}, bf16[192,3072]{1,0:T(8,128)(2,1)}, bf16[768,768]{1,0:T(8,128)(2,1)}), ...) | async-done | bytes 4718608 | tf_op jit(solution)/shard_map/psum | solution.py:304
  (372 shorter events, 399.8 us)
Async XLA Ops:
  7.2 34.2 %all-gather.8.cloned.1.call-start = ((), (), s32[]{:S(2)}) async-start(), calls=%async_computation.7 | async-start | bytes 4423680 | tf_op jit(solution)/shard_map/all_gather | solution.py:160
  7.9 219.1 %all-gather.12.cloned.1.call-start = ((), (), s32[]{:S(2)}) async-start(), calls=%async_computation.9 | async-start | bytes 14155776 | tf_op jit(solution)/shard_map/all_gather | solution.py:186
  47.6 3.6 copy-start.16
  52.5 351.4 %all-gather.10.cloned.1.call-start = ((), (), s32[]{:S(2)}) async-start(), calls=%async_computation.8 | async-start | bytes 14155776 | tf_op jit(solution)/shard_map/all_gather | solution.py:185
  53.2 12.9 copy-start.27
  53.2 12.9 copy-start.29
  71.3 2.7 copy-start.46
  71.3 3.9 copy-start.47
  71.3 4.2 copy-start.48
  71.3 4.4 copy-start.49
  71.3 12.5 copy-start.17
  71.3 12.5 copy-start.18
  71.4 572.7 %all-gather.14.cloned.1.call-start = ((), (), s32[]{:S(2)}) async-start(), calls=%async_computation.10 | async-start | bytes 1474560 | tf_op jit(solution)/shard_map/all_gather | solution.py:161
  71.9 578.2 %all-gather.16.cloned.1.call-start = ((), (), s32[]{:S(2)}) async-start(), calls=%async_computation.11 | async-start | bytes 5898240 | tf_op jit(solution)/shard_map/all_gather | solution.py:162
  72.5 588.4 %all-gather.18.cloned.1.call-start = ((), (), s32[]{:S(2)}) async-start(), calls=%async_computation.12 | async-start | bytes 5898240 | tf_op jit(solution)/shard_map/all_gather | solution.py:163
  73.1 601.5 %all-gather.20.cloned.1.call-start = ((), (), s32[]{:S(2)}) async-start(), calls=%async_computation.13 | async-start | bytes 5898240 | tf_op jit(solution)/shard_map/all_gather | solution.py:164
  73.9 1422.3 %reduce-scatter.10.cloned.1.call-start = ((), (), s32[]{:S(2)}) async-start(), calls=%async_computation.14 | async-start | bytes 14155776 | tf_op jit(solution)/shard_map/reduce_scatter | solution.py:255
  406.2 2.3 copy-start.4
  434.8 2.3 copy-start.4
  464.4 2.3 copy-start.4
  494.8 2.3 copy-start.4
  525.7 2.4 copy-start.4
  555.2 2.3 copy-start.4
  584.6 2.3 copy-start.4
  614.0 2.3 copy-start.4
  641.1 6.9 copy-start.2
  644.0 4.0 copy-start.24
  650.1 10.8 copy-start.22
  683.9 35.6 %copy-start.5 = (f32[2,512,768]{2,1,0:T(8,128)}, f32[2,512,768]{2,1,0:T(8,128)S(1)}, u32[]{:S(2)}) copy-start(f32[2,512,768]{2,1,0:T(8,128)S(1)} %get-tuple-element.392) | copy-start | bytes 9437188
  683.9 2.5 copy-start.9
  683.9 2.5 copy-start.38
  683.9 35.6 %copy-start.36 = (f32[2,512]{1,0:T(2,128)}, f32[2,512]{1,0:T(2,128)S(1)}, u32[]{:S(2)}) copy-start(f32[2,512]{1,0:T(2,128)S(1)} %broadcast_multiply_fusion.5) | copy-start | bytes 12292
  686.4 33.1 %copy-start.40 = (f32[2,512]{1,0:T(2,128)}, f32[2,512]{1,0:T(2,128)S(1)}, u32[]{:S(2)}) copy-start(f32[2,512]{1,0:T(2,128)S(1)} %add_rsqrt_fusion) | copy-start | bytes 12292
  709.1 10.4 copy-start.8
  709.1 10.4 copy-start.10
  709.1 10.4 copy-start.51
  730.0 2.6 copy-start.31
  735.7 3.7 copy-start.1
  749.5 5.4 copy-start.3
  804.1 2.1 copy-start.26
  870.9 2.1 copy-start.26
  1288.8 417.6 %reduce-scatter.12.cloned.1.call-start = ((), (), s32[]{:S(2)}) async-start(), calls=%async_computation.15 | async-start | bytes 14155776 | tf_op jit(solution)/shard_map/reduce_scatter | solution.py:258
  1289.5 468.1 %reduce-scatter.22.cloned.1.call-start = ((), (), s32[]{:S(2)}) async-start(), calls=%async_computation.20 | async-start | bytes 4423680
  1292.9 205.2 %copy-start.15 = (f32[2,512,12,64]{1,3,2,0:T(8,128)S(1)}, f32[2,512,12,64]{1,3,2,0:T(8,128)}, u32[]{:S(2)}) copy-start(f32[2,512,12,64]{1,3,2,0:T(8,128)} %broadcast_multiply_fusion) | copy-start | bytes 9437188
  1292.9 205.2 %copy-start.28 = (f32[2,512,32]{1,2,0:T(8,128)S(1)}, f32[2,512,32]{1,2,0:T(8,128)}, u32[]{:S(2)}) copy-start(f32[2,512,32]{1,2,0:T(8,128)} %copy-done.27) | copy-start | bytes 393220
  1292.9 205.2 %copy-start.30 = (f32[2,512,32]{1,2,0:T(8,128)S(1)}, f32[2,512,32]{1,2,0:T(8,128)}, u32[]{:S(2)}) copy-start(f32[2,512,32]{1,2,0:T(8,128)} %copy-done.29) | copy-start | bytes 393220
  1717.1 69.3 %reduce-scatter.14.cloned.1.call-start = ((), (), s32[]{:S(2)}) async-start(), calls=%async_computation.16 | async-start | bytes 1474560 | tf_op jit(solution)/shard_map/reduce_scatter | solution.py:278
  1722.8 114.0 %reduce-scatter.16.cloned.1.call-start = ((), (), s32[]{:S(2)}) async-start(), calls=%async_computation.17 | async-start | bytes 5898240 | tf_op jit(solution)/shard_map/reduce_scatter | solution.py:281
  1732.3 155.1 %reduce-scatter.18.cloned.1.call-start = ((), (), s32[]{:S(2)}) async-start(), calls=%async_computation.18 | async-start | bytes 5898240 | tf_op jit(solution)/shard_map/reduce_scatter | solution.py:284
  1743.9 193.9 %reduce-scatter.20.cloned.1.call-start = ((), (), s32[]{:S(2)}) async-start(), calls=%async_computation.19 | async-start | bytes 5898240 | tf_op jit(solution)/shard_map/reduce_scatter | solution.py:287
  1755.1 364.3 %all-reduce.14.cloned.1.call-start = ((), (), s32[]{:S(2)}) async-start(), calls=%async_computation.21 | async-start | bytes 10027008 | tf_op jit(solution)/shard_map/psum | solution.py:304
  1937.8 2.8 copy-start.42
  1937.8 2.8 copy-start.44
  1937.8 2.8 copy-start.45
  1937.8 32.9 %copy-start.6 = (f32[2,512,768]{2,1,0:T(8,128)S(1)}, f32[2,512,768]{2,1,0:T(8,128)}, u32[]{:S(2)}) copy-start(f32[2,512,768]{2,1,0:T(8,128)} %copy-done.5) | copy-start | bytes 9437188
  1937.8 32.9 %copy-start.37 = (f32[2,512]{1,0:T(2,128)S(1)}, f32[2,512]{1,0:T(2,128)}, u32[]{:S(2)}) copy-start(f32[2,512]{1,0:T(2,128)} %copy-done.36) | copy-start | bytes 12292
  1937.8 32.9 %copy-start.39 = (f32[768]{0:T(1024)S(1)}, f32[768]{0:T(1024)}, u32[]{:S(2)}) copy-start(f32[768]{0:T(1024)} %convert_element_type.173) | copy-start | bytes 9220
  1937.8 32.9 %copy-start.41 = (f32[2,512]{1,0:T(2,128)S(1)}, f32[2,512]{1,0:T(2,128)}, u32[]{:S(2)}) copy-start(f32[2,512]{1,0:T(2,128)} %copy-done.40) | copy-start | bytes 12292
  1968.4 4.0 copy-start.14
  1968.4 4.0 copy-start.21
  2119.5 2.6 copy-start.35
  2119.5 3.5 copy-start.34
  2119.5 5.2 copy-start.33
  2123.0 3.3 copy-start.32
  (24 other events, 40.3 us)
Sparse Core Ops, SparseCore 0:
  9.5 31.7 all-gather.7
  52.7 174.2 all-gather.11
  229.6 174.2 all-gather.9
  405.3 17.4 all-gather.13
  424.2 37.4 all-gather.15
  463.1 37.4 all-gather.17
  502.1 37.4 all-gather.19
  1288.9 207.2 reduce-scatter.9
  1499.8 206.5 reduce-scatter.11
  1717.2 40.3 reduce-scatter.21
  1760.8 25.6 reduce-scatter.13
  1788.8 47.9 reduce-scatter.15
  1839.4 47.9 reduce-scatter.17
  1889.8 47.9 reduce-scatter.19
  1942.4 176.9 all-reduce.13
where the time goes:
time: 2150 us; the launch traced here: 2130 us
  waiting for transfers between devices  1070 us (50%)
  matrix products  776 us (36%)
  local copies, waits for them, and re-layouts  180 us (8%)
  other arithmetic  50 us (2%)
  blocking collectives  34 us (2%)
    reduce_scatter x1, waiting for transfers between devices, local(): lax.psum_scatter(k_all.astype(jnp.bfloat16), 'seq', scatter_dimension=1,...  203 us
    reduce_scatter x1, waiting for transfers between devices, local(): lax.psum_scatter(v_all.astype(jnp.bfloat16), 'seq', scatter_dimension=1,...  203 us
    all_gather x1, waiting for transfers between devices, local(): lax.all_gather(k_local, 'seq', axis=1, tiled=True)  161 us
    all_gather x1, waiting for transfers between devices, local(): lax.all_gather(v_local, 'seq', axis=1, tiled=True)  143 us
    psum x1, waiting for transfers between devices, local(): lax.psum(owned[0].astype(jnp.bfloat16), 'seq').astype(jnp.float32)  139 us
    dot_general x8, matrix products, back_step(): jnp.einsum('sqhd,skhd->shqk', g_heads, v_part, preferred_element_type=jnp...  127 us
    dot_general x8, matrix products, attend_step(): jnp.einsum('shqk,skhd->sqhd', expo.astype(jnp.bfloat16), v_part, preferre...  108 us
    dot_general x8, matrix products, back_step(): jnp.einsum('shqk,sqhd->skhd', expo.astype(jnp.bfloat16), g_heads, preferr...  93.2 us
  transfers between devices with their start and end apart: 15, of which 11 were waited for; matrix products, arithmetic and copies ran while one was open for 17% of the time, Pallas kernels for 0%

commit v1 on v0

--- a/solution.py
+++ b/solution.py
@@ -1,8 +1,11 @@
+import functools
 import math
 
 import jax
 import jax.numpy as jnp
 from jax import lax
+from jax.experimental import pallas as pl
+from jax.experimental.pallas import tpu as pltpu
 from jax.sharding import PartitionSpec as P
 
 HEADS = 12
@@ -326,6 +329,310 @@
     )
 
 
+SEQS_HELD = 2
+LANES = 128
+LOG2E = 1.4426950408889634
+LN2 = 0.6931471805599453
+FAR = 2.0**30
+F32 = jnp.float32
+BF16 = jnp.bfloat16
+VMEM_LIMIT = 60 * 1024 * 1024
+
+
+def key_ranges(seg_row, rows, window, align):
+    length = seg_row.shape[0]
+    first = seg_row[::rows]
+    last = seg_row[rows - 1 :: rows]
+    low = jnp.sum((seg_row[None, :] < first[:, None]).astype(jnp.int32), axis=1)
+    high = jnp.sum((seg_row[None, :] <= last[:, None]).astype(jnp.int32), axis=1)
+    low = low // align * align
+    count = (high - low + window - 1) // window
+    low = jnp.minimum(low, length - count * window)
+    return low.astype(jnp.int32), count.astype(jnp.int32)
+
+
+def attend_kernel(window, align, low_ref, count_ref, q_ref, k_ref, v_ref, sum_ref):
+    block = pl.program_id(0)
+    low = low_ref[block]
+    sum_ref[...] = jnp.zeros_like(sum_ref)
+
+    def step(index, carry):
+        start = pl.multiple_of(low + index * window, align)
+        for head in range(q_ref.shape[0]):
+            k_part = k_ref[head, pl.ds(start, window), :]
+            v_part = v_ref[head, pl.ds(start, window), :]
+            score = lax.dot_general(
+                q_ref[head], k_part, (((1,), (1,)), ((), ())), preferred_element_type=F32
+            )
+            expo = jnp.exp2(score).astype(BF16)
+            sum_ref[head] += jnp.dot(expo, v_part, preferred_element_type=F32)
+        return carry
+
+    lax.fori_loop(0, count_ref[block], step, 0)
+
+
+def attend_heads(seg_row, q_ext, k_ext, v_ext, rows=512, window=1024, align=16):
+    heads, length, lanes = q_ext.shape
+    low, count = key_ranges(seg_row, rows, window, align)
+    whole = pl.BlockSpec((heads, length, lanes), lambda i, *_: (0, 0, 0))
+    part = pl.BlockSpec((heads, rows, lanes), lambda i, *_: (0, i, 0))
+    return pl.pallas_call(
+        functools.partial(attend_kernel, window, align),
+        out_shape=jax.ShapeDtypeStruct((heads, length, lanes), F32),
+        grid_spec=pltpu.PrefetchScalarGridSpec(
+            num_scalar_prefetch=2,
+            grid=(length // rows,),
+            in_specs=[part, whole, whole],
+            out_specs=part,
+        ),
+        compiler_params=pltpu.CompilerParams(vmem_limit_bytes=VMEM_LIMIT),
+        cost_estimate=pl.CostEstimate(
+            flops=heads * length * length * 4 * lanes // 2,
+            bytes_accessed=heads * length * lanes * 10,
+            transcendentals=heads * length * length // 2,
+        ),
+        name="attend_heads",
+    )(low, count, q_ext, k_ext, v_ext)
+
+
+def attend_back_kernel(
+    window, align, low_ref, count_ref, q_ref, g_ref, qt_ref, gt_ref, k_ref, v_ref, dq_ref, dkt_ref, dvt_ref
+):
+    block = pl.program_id(0)
+
+    @pl.when(block == 0)
+    def _():
+        dkt_ref[...] = jnp.zeros_like(dkt_ref)
+        dvt_ref[...] = jnp.zeros_like(dvt_ref)
+
+    dq_ref[...] = jnp.zeros_like(dq_ref)
+    low = low_ref[block]
+    by_lanes = (((1,), (1,)), ((), ()))
+
+    def step(index, carry):
+        start = pl.multiple_of(low + index * window, align)
+        for head in range(q_ref.shape[0]):
+            k_part = k_ref[head, pl.ds(start, window), :]
+            v_part = v_ref[head, pl.ds(start, window), :]
+            score = lax.dot_general(q_ref[head], k_part, by_lanes, preferred_element_type=F32)
+            slope = lax.dot_general(g_ref[head], v_part, by_lanes, preferred_element_type=F32)
+            expo = jnp.exp2(score)
+            d_score = (expo * slope).astype(BF16)
+            expo = expo.astype(BF16)
+            dq_ref[head] += jnp.dot(d_score, k_part, preferred_element_type=F32)
+            dvt_ref[head, :, pl.ds(start, window)] += jnp.dot(gt_ref[head], expo, preferred_element_type=F32)
+            dkt_ref[head, :, pl.ds(start, window)] += jnp.dot(qt_ref[head], d_score, preferred_element_type=F32)
+        return carry
+
+    lax.fori_loop(0, count_ref[block], step, 0)
+
+
+def attend_back_heads(seg_row, q_ext, k_ext, v_ext, g_ext, rows=512, window=512, align=128):
+    heads, length, lanes = q_ext.shape
+    low, count = key_ranges(seg_row, rows, window, align)
+    q_turned = jnp.swapaxes(q_ext[:, :, :HD], 1, 2)
+    g_turned = jnp.swapaxes(g_ext[:, :, :HD], 1, 2)
+    whole = pl.BlockSpec((heads, length, lanes), lambda i, *_: (0, 0, 0))
+    part = pl.BlockSpec((heads, rows, lanes), lambda i, *_: (0, i, 0))
+    turned_part = pl.BlockSpec((heads, HD, rows), lambda i, *_: (0, 0, i))
+    turned = pl.BlockSpec((heads, HD, length), lambda i, *_: (0, 0, 0))
+    return pl.pallas_call(
+        functools.partial(attend_back_kernel, window, align),
+        out_shape=(
+            jax.ShapeDtypeStruct((heads, length, lanes), F32),
+            jax.ShapeDtypeStruct((heads, HD, length), F32),
+            jax.ShapeDtypeStruct((heads, HD, length), F32),
+        ),
+        grid_spec=pltpu.PrefetchScalarGridSpec(
+            num_scalar_prefetch=2,
+            grid=(length // rows,),
+            in_specs=[part, part, turned_part, turned_part, whole, whole],
+            out_specs=(part, turned, turned),
+        ),
+        compiler_params=pltpu.CompilerParams(vmem_limit_bytes=VMEM_LIMIT),
+        cost_estimate=pl.CostEstimate(
+            flops=heads * length * length * 10 * lanes // 2,
+            bytes_accessed=heads * length * lanes * 20,
+            transcendentals=heads * length * length // 2,
+        ),
+        name="attend_back_heads",
+    )(low, count, q_ext, g_ext, q_turned, g_turned, k_ext, v_ext)
+
+
+def document_places(seg_row):
+    length = seg_row.shape[0]
+    ids = jnp.arange(LANES - HD, dtype=jnp.int32)
+    starts = jnp.sum((seg_row[None, :] < ids[:, None]).astype(jnp.int32), axis=1)
+    same = seg_row[:, None] == ids[None, :]
+    start = jnp.sum(jnp.where(same, starts[None, :], 0), axis=1)
+    return same, jnp.arange(length, dtype=jnp.int32) - start
+
+
+def by_group(block_rows, groups):
+    seqs, rows, width = block_rows.shape
+    split = block_rows.reshape(seqs, rows, groups, width // groups)
+    return jnp.transpose(split, (0, 2, 1, 3)).reshape(seqs * groups, rows, width // groups)
+
+
+def from_group(blocks, groups):
+    devices, rows, width = blocks.shape
+    split = blocks.reshape(devices // groups, groups, rows, width)
+    return jnp.transpose(split, (0, 2, 1, 3)).reshape(devices // groups, rows, groups * width)
+
+
+def exchange(blocks):
+    return lax.all_to_all(blocks, "seq", 0, 0, tiled=True)
+
+
+def local_heads(
+    seq_size,
+    tokens,
+    segments,
+    positions,
+    cotangent,
+    w_qkv,
+    w_out,
+    w_gate,
+    w_up,
+    w_down,
+    ln1_gain,
+    ln1_bias,
+    ln2_gain,
+    ln2_bias,
+):
+    seq_count, row_count, model_width = tokens.shape
+    groups = seq_size // seq_count
+    held = HEADS // groups
+    length = row_count * seq_size
+    score_scale = HD ** (-0.5)
+    my_seq = lax.axis_index("seq") // groups
+    seg_row = lax.dynamic_index_in_dim(segments, my_seq, 0, keepdims=False)
+
+    def gather(shard):
+        return lax.all_gather(shard, "shard", axis=0, tiled=True)
+
+    full_qkv = gather(w_qkv)
+    norms = gather(jnp.stack([ln1_gain, ln1_bias, ln2_gain, ln2_bias], axis=1)).astype(F32)
+    gain_one, bias_one, gain_two, bias_two = (norms[:, n] for n in range(4))
+    full_out, full_gate, full_up, full_down = (gather(w) for w in (w_out, w_gate, w_up, w_down))
+
+    cos_b, sin_b = rope_tables(positions)
+    qkv_all = jnp.einsum("scd,de->sce", tokens, full_qkv, preferred_element_type=F32)
+    q_heads = rotate(head_split(qkv_all[..., :model_width], seq_count, row_count), cos_b, sin_b)
+    k_heads = rotate(
+        head_split(qkv_all[..., model_width : 2 * model_width], seq_count, row_count), cos_b, sin_b
+    )
+    q_low = (q_heads * (score_scale * LOG2E)).astype(BF16).reshape(seq_count, row_count, model_width)
+    k_low = k_heads.astype(BF16).reshape(seq_count, row_count, model_width)
+    v_low = qkv_all[..., 2 * model_width :].astype(BF16)
+    sent = jnp.concatenate([by_group(part, groups) for part in (q_low, k_low, v_low)], axis=-1)
+    taken = exchange(sent).reshape(length, 3, held, HD)
+
+    same, place = document_places(seg_row)
+    own = jnp.broadcast_to(same.astype(BF16), (held, length, LANES - HD))
+    other = jnp.broadcast_to(jnp.where(same, 0.0, -FAR).astype(BF16), (held, length, LANES - HD))
+    ones = jnp.ones((held, length, LANES - HD), BF16)
+    q_own, k_own, v_own = (jnp.transpose(taken[:, n], (1, 0, 2)) for n in range(3))
+    q_ext = jnp.concatenate([q_own, own], axis=-1)
+    k_ext = jnp.concatenate([k_own, other], axis=-1)
+    v_ext = jnp.concatenate([v_own, ones], axis=-1)
+    sums = attend_heads(seg_row, q_ext, k_ext, v_ext)
+    total = sums[..., HD : HD + 1]
+    o_own = sums[..., :HD] / total
+    joined_own = jnp.transpose(o_own, (1, 0, 2)).astype(BF16).reshape(seq_size, row_count, held * HD)
+    joined = from_group(exchange(joined_own), groups)
+
+    tokens_f = tokens.astype(F32)
+    h_one = tokens_f + jnp.einsum("sci,io->sco", joined, full_out, preferred_element_type=F32)
+    x_one, normed_one, inverse_one = norm_fwd(h_one, gain_one, bias_one)
+    x_low = x_one.astype(BF16)
+    gate_pre = jnp.einsum("scd,df->scf", x_low, full_gate, preferred_element_type=F32)
+    up_pre = jnp.einsum("scd,df->scf", x_low, full_up, preferred_element_type=F32)
+    sigma = jax.nn.sigmoid(gate_pre)
+    smooth = gate_pre * sigma
+    hidden = (smooth * up_pre).astype(BF16)
+    h_two = x_one + jnp.einsum("scf,fd->scd", hidden, full_down, preferred_element_type=F32)
+    result, normed_two, inverse_two = norm_fwd(h_two, gain_two, bias_two)
+    output = result.astype(BF16)
+
+    cot_f = cotangent.astype(F32)
+    grad_gain_two = jnp.sum(cot_f * normed_two, axis=(0, 1))
+    grad_bias_two = jnp.sum(cot_f, axis=(0, 1))
+    dh_two = norm_back(cot_f, normed_two, inverse_two, gain_two)
+    dm_low = dh_two.astype(BF16)
+    d_hidden = jnp.einsum("scd,fd->scf", dm_low, full_down, preferred_element_type=F32)
+    d_up = (d_hidden * smooth).astype(BF16)
+    d_gate = (d_hidden * up_pre * sigma * (1.0 + gate_pre * (1.0 - sigma))).astype(BF16)
+    dx_one = (
+        dh_two
+        + jnp.einsum("scf,df->scd", d_gate, full_gate, preferred_element_type=F32)
+        + jnp.einsum("scf,df->scd", d_up, full_up, preferred_element_type=F32)
+    )
+    grad_gain_one = jnp.sum(dx_one * normed_one, axis=(0, 1))
+    grad_bias_one = jnp.sum(dx_one, axis=(0, 1))
+    dh_one = norm_back(dx_one, normed_one, inverse_one, gain_one)
+    d_attn = dh_one.astype(BF16)
+    d_joined = jnp.einsum("sco,io->sci", d_attn, full_out, preferred_element_type=F32).astype(BF16)
+
+    grad_down = jnp.einsum("scf,scd->fd", hidden, dm_low, preferred_element_type=F32).astype(BF16)
+    grad_gate = jnp.einsum("scd,scf->df", x_low, d_gate, preferred_element_type=F32).astype(BF16)
+    grad_up = jnp.einsum("scd,scf->df", x_low, d_up, preferred_element_type=F32).astype(BF16)
+    grad_out = jnp.einsum("sci,sco->io", joined, d_attn, preferred_element_type=F32).astype(BF16)
+    grad_norms = jnp.stack([grad_gain_one, grad_bias_one, grad_gain_two, grad_bias_two], axis=1)
+
+    def reduce_shards(partial):
+        return lax.psum_scatter(partial, "shard", scatter_dimension=0, tiled=True)
+
+    d_joined, grad_down, grad_gate, grad_up, grad_out = lax.optimization_barrier(
+        (d_joined, grad_down, grad_gate, grad_up, grad_out)
+    )
+    owned = [reduce_shards(g) for g in (grad_out, grad_gate, grad_up, grad_down)]
+
+    dout = exchange(by_group(d_joined, groups)).reshape(length, held, HD)
+    dout = jnp.transpose(dout, (1, 0, 2)).astype(F32)
+    g_low = (dout / total).astype(BF16)
+    delta = -jnp.sum(dout * o_own, axis=-1, keepdims=True) / total
+    d_high = delta.astype(BF16)
+    d_mid = (delta - d_high.astype(F32)).astype(BF16)
+    d_small = (delta - d_high.astype(F32) - d_mid.astype(F32)).astype(BF16)
+    g_ext = jnp.concatenate(
+        [g_low, d_high, d_mid, d_small, jnp.zeros((held, length, LANES - HD - 3), BF16)], axis=-1
+    )
+    dq, dk_turned, dv_turned = attend_back_heads(seg_row, q_ext, k_ext, v_ext, g_ext)
+
+    cos_f, sin_f = (t[0] for t in rope_tables(place[None]))
+    dq_own = jnp.transpose(dq[..., :HD], (1, 0, 2)) * score_scale
+    dk_own = jnp.transpose(dk_turned, (2, 0, 1)) * LN2
+    dv_own = jnp.transpose(dv_turned, (2, 0, 1))
+    d_parts = [
+        part.astype(BF16).reshape(seq_size, row_count, held * HD)
+        for part in (rotate_back(dq_own, cos_f, sin_f), rotate_back(dk_own, cos_f, sin_f), dv_own)
+    ]
+    d_taken = exchange(jnp.concatenate(d_parts, axis=-1))
+    d_split = d_taken.reshape(seq_count, groups, row_count, 3, held * HD)
+    d_qkv = jnp.transpose(d_split, (0, 2, 3, 1, 4)).reshape(seq_count, row_count, 3 * model_width)
+    grad_qkv = jnp.einsum("scd,sce->de", tokens, d_qkv, preferred_element_type=F32).astype(BF16)
+    d_tokens = dh_one + jnp.einsum("sce,de->scd", d_qkv, full_qkv, preferred_element_type=F32)
+    input_grad = d_tokens.astype(BF16)
+
+    grad_out, grad_gate, grad_up, grad_down = (lax.psum(g, "seq").astype(F32) for g in owned)
+    grad_qkv = lax.psum(reduce_shards(grad_qkv), "seq").astype(F32)
+    norm_sums = lax.psum(reduce_shards(grad_norms), "seq")
+    return (
+        output,
+        input_grad,
+        grad_qkv,
+        grad_out,
+        grad_gate,
+        grad_up,
+        grad_down,
+        norm_sums[:, 0],
+        norm_sums[:, 1],
+        norm_sums[:, 2],
+        norm_sums[:, 3],
+    )
+
+
 def solution(mesh):
     in_specs = (
         P("shard", "seq", None),
@@ -355,4 +662,6 @@
         P("shard"),
         P("shard"),
     )
-    return jax.shard_map(local, mesh=mesh, in_specs=in_specs, out_specs=out_specs, check_vma=False)
+    heads_split = mesh.shape["seq"] % SEQS_HELD == 0 and HEADS % (mesh.shape["seq"] // SEQS_HELD) == 0
+    body = functools.partial(local_heads, mesh.shape["seq"]) if heads_split else local
+    return jax.shard_map(body, mesh=mesh, in_specs=in_specs, out_specs=out_specs, check_vma=False)

time: 2150 us -> 1170 us (0.54)
  matrix products: 776 us -> 130 us
  waiting for transfers between devices: 1070 us -> 575 us
  Pallas kernels: 0 us -> 107 us
  blocking collectives: 34 us -> 120 us
  local copies, waits for them, and re-layouts: 180 us -> 137 us
  starting transfers between devices: 1.06 us -> 24 us
    dot_general x71 -> x15, matrix products: 776 us -> 130 us  [the longest x1 19 us: local_heads(): jnp.einsum('scd,fd->scf', dm_low, full_down, preferred_element_type=F32)]
    reduce_scatter x6 -> x4, waiting for transfers between devices: 584 us -> 178 us  [reduce_shards(): return lax.psum_scatter(partial, 'shard', scatter_dimension=0, tiled=True)]
    all_gather x7 -> x5, waiting for transfers between devices: 337 us -> 30.7 us  [gather(): return lax.all_gather(shard, 'shard', axis=0, tiled=True)]
    all_to_all x0 -> x3, waiting for transfers between devices: none -> 144 us  [exchange(): return lax.all_to_all(blocks, 'seq', 0, 0, tiled=True)]
    pallas_call x0 -> x2, Pallas kernels: none -> 107 us  [the longest x1 73.3 us: attend_back_heads(): pl.pallas_call(functools.partial(attend_back_kernel, window, align), out_...]
    all_to_all x0 -> x1, blocking collectives: none -> 98.6 us  [exchange(): return lax.all_to_all(blocks, 'seq', 0, 0, tiled=True)]
    dynamic_slice x49 -> x1, local copies, waits for them, and re-layouts: 66.2 us -> 0.02 us  [local_heads(): seg_row = lax.dynamic_index_in_dim(segments, my_seq, 0, keepdims=False)]
    unnamed x16 -> x14, waiting for transfers between devices: 6.24 us -> 66.8 us
  transfers between devices with their start and end apart: 15 -> 15, of which waited for: 11 -> 11; matrix products, arithmetic and copies ran while one was open for 17% -> 13% of each run, Pallas kernels for 0% -> 3%
where the time goes in v1:
time: 1170 us; the launch traced here: 1150 us
  waiting for transfers between devices  575 us (49%)
  local copies, waits for them, and re-layouts  137 us (12%)
  matrix products  130 us (11%)
  blocking collectives  120 us (10%)
  Pallas kernels  107 us (9%)
  other arithmetic  45.3 us (4%)
  starting transfers between devices  24 us (2%)
  between operations  15.2 us (1%)
    reduce_scatter x4, waiting for transfers between devices, reduce_shards(): return lax.psum_scatter(partial, 'shard', scatter_dimension=0, tiled=True)  178 us
    psum x1, waiting for transfers between devices, local_heads(): grad_qkv = lax.psum(reduce_shards(grad_qkv), 'seq').astype(F32)  156 us
    all_to_all x3, waiting for transfers between devices, exchange(): return lax.all_to_all(blocks, 'seq', 0, 0, tiled=True)  144 us
    all_to_all x1, blocking collectives, exchange(): return lax.all_to_all(blocks, 'seq', 0, 0, tiled=True)  98.6 us
    pallas_call x1, Pallas kernels, attend_back_heads(): pl.pallas_call(functools.partial(attend_back_kernel, window, align), out_...  73.3 us
    unnamed x14, waiting for transfers between devices  66.8 us
    unnamed x90, local copies, waits for them, and re-layouts  50.2 us
    pallas_call x1, Pallas kernels, attend_heads(): pl.pallas_call(functools.partial(attend_kernel, window, align), out_shape...  34.1 us
  transfers between devices with their start and end apart: 15, of which 11 were waited for; matrix products, arithmetic and copies ran while one was open for 13% of the time, Pallas kernels for 3%

profile of v1, /device:TPU:20, one launch (start us, length us, event | category | flops | bytes accessed | tf_op | source)
XLA Modules:
  0.0 1153.1 jit_solution(899286470189944371)
XLA Ops:
  10.7 30.7 %all-gather.7.cloned.1.call-done = bf16[768,2304]{1,0:T(8,128)(2,1)} async-done(((bf16[192,2304]{1,0:T(8,128)(2,1)}), bf16[768,2304]{1,0:T(8,128)(2,1)}) %all-gather.7.cloned.1.call-update) | async-done | bytes 3538960 | tf_op jit(solution)/shard_map/all_gather | solution.py:512
  41.4 10.0 fusion.52
  54.4 6.2 fusion.48
  60.6 2.4 copy.116
  63.0 3.5 copy.117
  66.6 2.9 multiply_subtract_fusion
  71.1 2.4 pad_maximum_fusion
  73.5 6.0 all-to-all-start
  83.3 2.7 select_convert_fusion
  86.0 95.1 %all-to-all-done = bf16[8,512,576]{1,2,0:T(8,128)(2,1)} async-done(((bf16[8,512,576]{1,2,0:T(8,128)(2,1)}), bf16[8,512,576]{1,2,0:T(8,128)(2,1)}, u32[]{:S(2)}, u32[]{:S(2)}) %all-to-all-start) | async-done | bytes 4718624 | tf_op jit(solution)/shard_map/all_to_all | solution.py:484
  181.1 7.2 copy.119
  188.2 8.3 reshape.219
  196.5 4.7 slice_bitcast_fusion.1
  201.6 2.8 copy.123.q_ref
  204.4 4.1 copy.153
  208.5 3.1 copy.154
  211.6 2.4 concatenate.45.v_ref
  215.8 3.4 pad_maximum_fusion.3.k_ref
  219.2 34.1 %attend_heads.1 = f32[3,4096,128]{2,1,0:T(8,128)} custom-call(s32[8]{0:T(128)} %get-tuple-element.149.low_ref, s32[8]{0:T(128)} %get-tuple-element.150.count_ref, bf16[3,4096,128]{2,1,0:T(8,128)(2,1)} %copy.123.q_ref, bf16[3,4096,128]{2,1,0:T(8,128)(2,1)} %pad_maximum_fusion.3.k_ref, bf16[3,4096,128]{2,1,0:T(8,128)(2,1)} %concatenate.45.v_ref), custom_call_target="tpu_custom_call" | custom-call | flops 12884901888 | bytes 15728640 | tf_op jit(solution)/shard_map/attend_heads/pallas_call | solution.py:379
  253.3 7.2 slice.158
  260.5 4.4 copy.156
  264.9 6.0 copy.152
  273.6 10.5 all-to-all-start.1
  284.8 5.2 all-gather
  290.2 24.4 %all-to-all-done.1 = bf16[8,512,192]{1,2,0:T(8,128)(2,1)S(1)} async-done(((bf16[8,512,192]{1,2,0:T(8,128)(2,1)}), bf16[8,512,192]{1,2,0:T(8,128)(2,1)S(1)}, u32[]{:S(2)}, u32[]{:S(2)}) %all-to-all-start.1) | async-done | bytes 1572896 | tf_op jit(solution)/shard_map/all_to_all | solution.py:484
  315.7 3.8 fusion.53
  321.7 10.4 fusion.11
  332.1 13.6 %multiply_convert_fusion.2 = (bf16[2,512,3072]{2,1,0:T(8,128)(2,1)}, f32[2,512,3072]{2,1,0:T(8,128)}) fusion(f32[2,512,3072]{2,1,0:T(8,128)} %fusion.11, bf16[2,512,768]{2,1,0:T(8,128)(2,1)} %fusion.31, bf16[768,3072]{1,0:T(8,128)(2,1)} %all-gather.13.cloned.1.call-done), kind=kOutput, calls=%fused_computation.2 | convolution fusion | flops 4850712576 | bytes 37748736 | tf_op jit(solution)/shard_map/scd,df->scf/dot_general | solution.py:550
  345.7 8.8 fusion.54
  362.6 7.0 bitcast_convert_fusion.2
  369.5 19.0 %multiply_convert_fusion.1 = (bf16[2,512,3072]{2,1,0:T(8,128)(2,1)}, bf16[2,512,3072]{2,1,0:T(8,128)(2,1)}) fusion(f32[2,512,3072]{2,1,0:T(8,128)} %fusion.11, f32[2,512,3072]{2,1,0:T(8,128)} %get-tuple-element.158, bf16[2,512,768]{2,1,0:T(8,128)(2,1)} %copy-done.19, bf16[3072,768]{1,0:T(8,128)(2,1)} %all-gather.15.cloned.1.call-done), kind=kOutput, calls=%fused_computation.1 | convolution fusion | flops 4872732672 | bytes 44040192 | tf_op jit(solution)/shard_map/scd,fd->scf/dot_general | solution.py:563
  388.5 9.1 bitcast_convert_fusion.1
  397.6 9.2 bitcast_convert_fusion
  406.9 8.7 fusion.5
  415.6 10.5 multiply_reduce_fusion
  428.9 2.4 bitcast_convert_fusion.4
  431.3 3.3 convolution_convert_fusion
  435.5 2.3 copy.132
  437.7 7.0 all-to-all-start.2
  446.4 2.8 multiply_cosine_fusion
  449.2 4.4 copy.155
  453.7 24.3 %all-to-all-done.2 = bf16[8,512,192]{1,2,0:T(8,128)(2,1)S(1)} async-done(((bf16[8,512,192]{1,2,0:T(8,128)(2,1)}), bf16[8,512,192]{1,2,0:T(8,128)(2,1)S(1)}, u32[]{:S(2)}, u32[]{:S(2)}) %all-to-all-start.2) | async-done | bytes 1572896 | tf_op jit(solution)/shard_map/all_to_all | solution.py:484
  478.0 2.6 copy.133
  480.6 2.9 reshape.227
  483.5 3.8 fusion.29
  490.1 15.1 %concatenate.47 = bf16[3,4096,128]{1,2,0:T(8,128)(2,1)S(1)} concatenate(bf16[3,4096,64]{1,2,0:T(8,128)(2,1)} %get-tuple-element.128, bf16[3,4096,1]{1,2,0:T(2,128)(2,1)S(1)} %get-tuple-element.140, bf16[3,4096,1]{1,2,0:T(2,128)(2,1)S(1)} %get-tuple-element.139, bf16[3,4096,1]{1,2,0:T(2,128)(2,1)S(1)} %get-tuple-element.101, bf16[3,4096,61]{1,2,0:T(8,128)(2,1)} %broadcast_in_dim.30), dimensions={2} | concatenate | bytes 6291456 | tf_op jit(solution)/shard_map/concatenate | solution.py:598
  505.2 2.8 copy.135.g_ref
  508.0 73.3 %attend_back_heads.1 = (f32[3,4096,128]{2,1,0:T(8,128)}, f32[3,64,4096]{2,1,0:T(8,128)}, f32[3,64,4096]{2,1,0:T(8,128)}) custom-call(s32[8]{0:T(128)} %get-tuple-element.103.low_ref, s32[8]{0:T(128)} %get-tuple-element.104.count_ref, bf16[3,4096,128]{2,1,0:T(8,128)(2,1)} %copy.123.q_ref, bf16[3,4096,128]{2,1,0:T(8,128)(2,1)} %copy.135.g_ref, ...), custom_call_target="tpu_custom_call" | custom-call | flops 32212254720 | bytes 31457280 | tf_op jit(solution)/shard_map/attend_back_heads/pallas_call | solution.py:439
  581.3 7.0 copy.136
  588.4 2.3 fusion.25
  598.5 98.6 %all_to_all.20 = bf16[8,512,576]{1,2,0:T(8,128)(2,1)S(1)} all-to-all(bf16[8,512,576]{1,2,0:T(8,128)(2,1)S(1)} %pad_maximum_fusion.1), channel_id=1, replica_groups=mesh['seq'=8,'shard'=4] {'seq'}, dimensions={0} | all-to-all | bytes 9437184 | tf_op jit(solution)/shard_map/all_to_all | solution.py:484
  699.7 5.2 fusion.13
  704.9 5.8 copy.148
  714.7 37.2 %reduce-scatter.19.cloned.1.call-done = bf16[192,2304]{1,0:T(8,128)(2,1)} async-done(((bf16[768,2304]{1,0:T(8,128)(2,1)}), bf16[192,2304]{1,0:T(8,128)(2,1)}) %reduce-scatter.19.cloned.1.call-update) | async-done | bytes 884752
  751.9 2.3 copy.149
  754.2 26.4 %reduce-scatter.11.cloned.1.call-done = bf16[192,768]{1,0:T(8,128)(2,1)} async-done(((bf16[768,768]{1,0:T(8,128)(2,1)}), bf16[192,768]{1,0:T(8,128)(2,1)}) %reduce-scatter.11.cloned.1.call-update) | async-done | bytes 294928 | tf_op jit(solution)/shard_map/reduce_scatter | solution.py:584
  780.7 50.5 %reduce-scatter.13.cloned.1.call-done = bf16[192,3072]{1,0:T(8,128)(2,1)} async-done(((bf16[768,3072]{1,0:T(8,128)(2,1)}), bf16[192,3072]{1,0:T(8,128)(2,1)}) %reduce-scatter.13.cloned.1.call-update) | async-done | bytes 1179664 | tf_op jit(solution)/shard_map/reduce_scatter | solution.py:584
  831.2 50.5 %reduce-scatter.15.cloned.1.call-done = bf16[192,3072]{1,0:T(8,128)(2,1)} async-done(((bf16[768,3072]{1,0:T(8,128)(2,1)}), bf16[192,3072]{1,0:T(8,128)(2,1)}) %reduce-scatter.15.cloned.1.call-update) | async-done | bytes 1179664 | tf_op jit(solution)/shard_map/reduce_scatter | solution.py:584
  881.7 50.4 %reduce-scatter.17.cloned.1.call-done = bf16[768,768]{1,0:T(8,128)(2,1)} async-done(((bf16[3072,768]{1,0:T(8,128)(2,1)}), bf16[768,768]{1,0:T(8,128)(2,1)}) %reduce-scatter.17.cloned.1.call-update) | async-done | bytes 1179664 | tf_op jit(solution)/shard_map/reduce_scatter | solution.py:584
  932.2 23.9 %reduce-scatter.21.cloned.1.call-done = f32[192,4]{1,0:T(8,128)} async-done(((f32[768,4]{1,0:T(8,128)}), f32[192,4]{1,0:T(8,128)}) %reduce-scatter.21.cloned.1.call-update) | async-done | bytes 3088
  957.0 15.9 %psum.47 = f32[192,4]{0,1:T(4,128)S(1)} all-reduce(f32[192,4]{0,1:T(4,128)S(1)} %copy.151), channel_id=1, replica_groups=mesh['seq'=8,'shard'=4] {'seq'}, use_global_device_ids=true, to_apply=%region_28.29 | all-reduce | flops 768 | bytes 6144 | tf_op jit(solution)/shard_map/psum | solution.py:620
  973.5 8.5 add_convert_fusion
  982.0 155.6 %all-reduce.4.cloned.1.call-done = (bf16[192,2304]{0,1:T(8,128)(2,1)}, bf16[192,768]{1,0:T(8,128)(2,1)}, bf16[192,3072]{1,0:T(8,128)(2,1)}, bf16[192,3072]{1,0:T(8,128)(2,1)}, bf16[768,768]{1,0:T(8,128)(2,1)}) async-done(((bf16[192,2304]{0,1:T(8,128)(2,1)}, bf16[192,768]{1,0:T(8,128)(2,1)}, bf16[192,3072]{1,0:T(8,128)(2,1)}, bf16[192,3072]{1,0:T(8,128)(2,1)}, bf16[768,768]{1,0:T(8,128)(2,1)}), ...) | async-done | bytes 4718608 | tf_op jit(solution)/shard_map/psum | solution.py:619
  1137.6 2.6 copy.142
  (183 shorter events, 58.5 us)
Async XLA Ops:
  7.2 72.9 %copy-start = (s32[2,4096]{1,0:T(2,128)S(1)}, s32[2,4096]{1,0:T(2,128)}, u32[]{:S(2)}) copy-start(s32[2,4096]{1,0:T(2,128)} %param.14) | copy-start | bytes 98308
  7.2 34.2 %all-gather.7.cloned.1.call-start = ((), (), s32[]{:S(2)}) async-start(), calls=%async_computation.10 | async-start | bytes 4423680 | tf_op jit(solution)/shard_map/all_gather | solution.py:512
  7.9 282.2 %all-gather.9.cloned.1.call-start = ((), (), s32[]{:S(2)}) async-start(), calls=%async_computation.11 | async-start | bytes 1474560 | tf_op jit(solution)/shard_map/all_gather | solution.py:512
  8.7 313.1 %all-gather.11.cloned.1.call-start = ((), (), s32[]{:S(2)}) async-start(), calls=%async_computation.12 | async-start | bytes 5898240 | tf_op jit(solution)/shard_map/all_gather | solution.py:512
  9.4 0.7 copy-start.28
  69.5 1.6 copy-start.6
  73.5 107.6 %all-to-all-start = ((bf16[8,512,576]{1,2,0:T(8,128)(2,1)}), bf16[8,512,576]{1,2,0:T(8,128)(2,1)}, u32[]{:S(2)}, u32[]{:S(2)}) async-start(bf16[8,512,576]{1,2,0:T(8,128)(2,1)} %pad_maximum_fusion), calls=%async_computation | async-start | bytes 9437184 | tf_op jit(solution)/shard_map/all_to_all | solution.py:484
  79.5 252.7 %all-gather.13.cloned.1.call-start = ((), (), s32[]{:S(2)}) async-start(), calls=%async_computation.13 | async-start | bytes 5898240 | tf_op jit(solution)/shard_map/all_gather | solution.py:512
  80.1 108.1 %copy-start.23 = (s32[1,4096]{1,0:T(1,128)}, s32[1,4096]{1,0:T(1,128)S(1)}, u32[]{:S(2)}) copy-start(s32[1,4096]{1,0:T(1,128)S(1)} %constant_dynamic-slice_fusion) | copy-start | bytes 49156
  211.5 2.4 copy-start.10
  213.9 1.9 copy-start.5
  264.9 6.1 copy-start.4
  271.9 12.8 %copy-start.32 = (bf16[192]{0:T(256)(128)(2,1)S(1)}, bf16[192]{0:T(256)(128)(2,1)}, u32[]{:S(2)}) copy-start(bf16[192]{0:T(256)(128)(2,1)} %param.22) | copy-start | bytes 1156
  271.9 12.8 %copy-start.33 = (bf16[192]{0:T(256)(128)(2,1)S(1)}, bf16[192]{0:T(256)(128)(2,1)}, u32[]{:S(2)}) copy-start(bf16[192]{0:T(256)(128)(2,1)} %param.23) | copy-start | bytes 1156
  271.9 12.8 %copy-start.34 = (bf16[192]{0:T(256)(128)(2,1)S(1)}, bf16[192]{0:T(256)(128)(2,1)}, u32[]{:S(2)}) copy-start(bf16[192]{0:T(256)(128)(2,1)} %param.24) | copy-start | bytes 1156
  272.0 12.8 %copy-start.35 = (bf16[192]{0:T(256)(128)(2,1)S(1)}, bf16[192]{0:T(256)(128)(2,1)}, u32[]{:S(2)}) copy-start(bf16[192]{0:T(256)(128)(2,1)} %param.25) | copy-start | bytes 1156
  273.6 40.9 %all-to-all-start.1 = ((bf16[8,512,192]{1,2,0:T(8,128)(2,1)}), bf16[8,512,192]{1,2,0:T(8,128)(2,1)S(1)}, u32[]{:S(2)}, u32[]{:S(2)}) async-start(bf16[8,512,192]{1,2,0:T(8,128)(2,1)} %copy.126), calls=%async_computation.1 | async-start | bytes 3145728 | tf_op jit(solution)/shard_map/all_to_all | solution.py:484
  284.1 61.6 %all-gather.15.cloned.1.call-start = ((), (), s32[]{:S(2)}) async-start(), calls=%async_computation.14 | async-start | bytes 5898240 | tf_op jit(solution)/shard_map/all_gather | solution.py:512
  314.6 1.1 copy-start.17
  354.5 4.8 copy-start.2
  354.5 2.5 copy-start.7
  357.0 5.5 slice-start
  359.2 3.3 slice-start.1
  361.4 1.1 copy-start.19
  406.8 8.8 copy-start.3
  406.9 8.8 copy-start.8
  426.2 2.7 copy-start.18
  427.2 1.7 copy-start.13
  428.9 2.4 copy-start.31
  435.4 9.2 copy-start.24
  435.4 11.0 copy-start.29
  437.7 40.3 %all-to-all-start.2 = ((bf16[8,512,192]{1,2,0:T(8,128)(2,1)}), bf16[8,512,192]{1,2,0:T(8,128)(2,1)S(1)}, u32[]{:S(2)}, u32[]{:S(2)}) async-start(bf16[8,512,192]{1,2,0:T(8,128)(2,1)} %copy.132), calls=%async_computation.2 | async-start | bytes 3145728 | tf_op jit(solution)/shard_map/all_to_all | solution.py:484
  444.7 307.2 %reduce-scatter.19.cloned.1.call-start = ((), (), s32[]{:S(2)}) async-start(), calls=%async_computation.19 | async-start | bytes 4423680
  588.4 2.8 copy-start.12
  591.4 1.9 copy-start.11
  593.3 1.0 copy-start.15
  593.3 1.2 copy-start.16
  697.0 2.6 copy-start.30
  697.5 2.1 copy-start.9
  710.7 70.0 %reduce-scatter.11.cloned.1.call-start = ((), (), s32[]{:S(2)}) async-start(), calls=%async_computation.15 | async-start | bytes 1474560 | tf_op jit(solution)/shard_map/reduce_scatter | solution.py:584
  711.4 119.8 %reduce-scatter.13.cloned.1.call-start = ((), (), s32[]{:S(2)}) async-start(), calls=%async_computation.16 | async-start | bytes 5898240 | tf_op jit(solution)/shard_map/reduce_scatter | solution.py:584
  712.2 169.6 %reduce-scatter.15.cloned.1.call-start = ((), (), s32[]{:S(2)}) async-start(), calls=%async_computation.17 | async-start | bytes 5898240 | tf_op jit(solution)/shard_map/reduce_scatter | solution.py:584
  712.9 0.7 copy-start.27
  712.9 0.7 copy-start.26
  712.9 219.2 %reduce-scatter.17.cloned.1.call-start = ((), (), s32[]{:S(2)}) async-start(), calls=%async_computation.18 | async-start | bytes 5898240 | tf_op jit(solution)/shard_map/reduce_scatter | solution.py:584
  713.5 242.5 %reduce-scatter.21.cloned.1.call-start = ((), (), s32[]{:S(2)}) async-start(), calls=%async_computation.20 | async-start | bytes 491520
  714.6 258.9 %copy-start.14 = (f32[2,512,768]{2,1,0:T(8,128)S(1)}, f32[2,512,768]{2,1,0:T(8,128)}, u32[]{:S(2)}) copy-start(f32[2,512,768]{2,1,0:T(8,128)} %copy-done.13) | copy-start | bytes 9437188
  714.6 423.0 %all-reduce.4.cloned.1.call-start = ((), (), s32[]{:S(2)}) async-start(), calls=%async_computation.21 | async-start | bytes 10027008 | tf_op jit(solution)/shard_map/psum | solution.py:619
  1137.6 2.6 copy-start.25
  1137.6 3.5 copy-start.22
  1137.6 5.2 copy-start.21
  1141.1 3.3 copy-start.20
  1142.8 3.3 copy-start.1
Sparse Core Ops, SparseCore 0:
  9.6 31.7 all-gather.6
  42.9 17.4 all-gather.8
  61.9 37.4 all-gather.10
  100.8 37.4 all-gather.12
  286.2 37.4 all-gather.14
  710.8 41.0 reduce-scatter.18
  755.0 25.5 reduce-scatter.10
  783.2 47.9 reduce-scatter.12
  833.7 47.9 reduce-scatter.14
  884.1 47.9 reduce-scatter.16
  935.2 20.8 reduce-scatter.20
  960.7 176.8 all-reduce.3

commit v2 on v1

--- a/solution.py
+++ b/solution.py
@@ -330,6 +330,8 @@
 
 
 SEQS_HELD = 2
+SEQ_SIZE = 8
+GROUPS = 4
 LANES = 128
 LOG2E = 1.4426950408889634
 LN2 = 0.6931471805599453
@@ -337,21 +339,202 @@
 F32 = jnp.float32
 BF16 = jnp.bfloat16
 VMEM_LIMIT = 60 * 1024 * 1024
-
-
-def key_ranges(seg_row, rows, window, align):
-    length = seg_row.shape[0]
+BY_MESH = pl.DeviceIdType.MESH
+BY_LANES = (((1,), (1,)), ((), ()))
+
+
+def flip(index, bit):
+    return index + bit - 2 * bit * lax.rem(lax.div(index, bit), 2)
+
+
+def gather_kernel(chunks, by_z, tok_ref, w_ref, all_ref, w_all_ref, send, recv, kept, w_send, w_recv):
+    me = lax.axis_index("seq")
+    shard = lax.axis_index("shard")
+    shards = w_all_ref.shape[0]
+    half = lax.div(me, GROUPS)
+    y_near, z_near, partner = flip(me, 1), flip(me, 2), flip(me, 4)
+    barrier = pltpu.get_barrier_semaphore()
+    for device in (y_near, z_near, partner):
+        pl.semaphore_signal(barrier, inc=1, device_id={"seq": device}, device_id_type=BY_MESH)
+    for step in range(1, shards):
+        pl.semaphore_signal(
+            barrier, inc=1, device_id={"shard": lax.rem(shard + step, shards)}, device_id_type=BY_MESH
+        )
+    pl.semaphore_wait(barrier, 2 + shards)
+
+    part = tok_ref.shape[1] // chunks
+    started = []
+
+    def go(source, target, slot, device):
+        copy = pltpu.make_async_remote_copy(
+            src_ref=source,
+            dst_ref=target,
+            send_sem=send.at[slot],
+            recv_sem=recv.at[slot],
+            device_id={"seq": device},
+            device_id_type=BY_MESH,
+        )
+        copy.start()
+        started.append(copy)
+        return copy
+
+    def rows(chunk):
+        return pl.ds(chunk * part, part)
+
+    def relay(piece, chunk, slot, device):
+        return go(all_ref.at[piece, rows(chunk)], all_ref.at[piece, rows(chunk)], slot * chunks + chunk, device)
+
+    def own(which, chunk, slot, device):
+        return go(tok_ref.at[which, rows(chunk)], all_ref.at[me, rows(chunk)], slot * chunks + chunk, device)
+
+    crossing = [own(1 - half, chunk, 0, partner) for chunk in range(chunks)]
+    own_y, own_z = [], []
+    for chunk in range(chunks):
+        own_y.append(own(half, chunk, 1, y_near))
+        own_z.append(own(half, chunk, 2, z_near))
+    weights = []
+    for step in range(1, shards):
+        copy = pltpu.make_async_remote_copy(
+            src_ref=w_ref,
+            dst_ref=w_all_ref.at[shard],
+            send_sem=w_send.at[step],
+            recv_sem=w_recv.at[step],
+            device_id={"shard": lax.rem(shard + step, shards)},
+            device_id_type=BY_MESH,
+        )
+        copy.start()
+        weights.append(copy)
+    keep_tok = pltpu.make_async_copy(tok_ref.at[half], all_ref.at[me], kept.at[0])
+    keep_tok.start()
+    keep_w = pltpu.make_async_copy(w_ref, w_all_ref.at[shard], kept.at[1])
+    keep_w.start()
+
+    cross_y, cross_z, corner = [], [], []
+    for chunk in range(chunks):
+        own_y[chunk].wait_recv()
+        if chunk < by_z:
+            corner.append(relay(y_near, chunk, 5, z_near))
+        own_z[chunk].wait_recv()
+        if chunk >= by_z:
+            corner.append(relay(z_near, chunk, 5, y_near))
+        crossing[chunk].wait_recv()
+        cross_y.append(relay(partner, chunk, 3, y_near))
+        cross_z.append(relay(partner, chunk, 4, z_near))
+    for chunk in range(chunks):
+        cross_y[chunk].wait_recv()
+        if chunk < by_z:
+            corner.append(relay(flip(y_near, 4), chunk, 6, z_near))
+        cross_z[chunk].wait_recv()
+        if chunk >= by_z:
+            corner.append(relay(flip(z_near, 4), chunk, 6, y_near))
+    for copy in corner:
+        copy.wait_recv()
+    for copy in weights:
+        copy.wait()
+    keep_tok.wait()
+    keep_w.wait()
+    for copy in started:
+        copy.wait_send()
+
+
+def gather_tokens(tokens, w_part, shards, chunks=8, by_z=3):
+    seqs, rows, width = tokens.shape
+    anywhere = pl.BlockSpec(memory_space=pl.ANY)
+    return pl.pallas_call(
+        functools.partial(gather_kernel, chunks, by_z),
+        out_shape=(
+            jax.ShapeDtypeStruct((SEQ_SIZE, rows, width), tokens.dtype),
+            jax.ShapeDtypeStruct((shards,) + w_part.shape, w_part.dtype),
+        ),
+        in_specs=[anywhere, anywhere],
+        out_specs=(anywhere, anywhere),
+        scratch_shapes=[
+            pltpu.SemaphoreType.DMA((7 * chunks,)),
+            pltpu.SemaphoreType.DMA((7 * chunks,)),
+            pltpu.SemaphoreType.DMA((2,)),
+            pltpu.SemaphoreType.DMA((shards,)),
+            pltpu.SemaphoreType.DMA((shards,)),
+        ],
+        compiler_params=pltpu.CompilerParams(collective_id=1, has_side_effects=True),
+        name="gather_tokens",
+    )(tokens, w_part)
+
+
+def project_kernel(seg_ref, place_ref, freq_ref, x_ref, w_ref, q_ref, k_ref, v_ref, turn_ref):
+    rows = x_ref.shape[1]
+    held = q_ref.shape[0]
+    lane = lax.broadcasted_iota(jnp.int32, (rows, LANES), 1)
+    seg = jnp.transpose(jnp.broadcast_to(seg_ref[0], (LANES, rows)))
+    place = jnp.transpose(jnp.broadcast_to(place_ref[0], (LANES, rows)))
+    turn = jnp.where(lane < HD, jnp.cos(place * freq_ref[...]), jnp.sin(place * freq_ref[...]))
+    turn_ref[...] = turn
+    cos_b = jnp.where(lane < HD, turn, 0.0)
+    sin_b = jnp.where(lane < HD, pltpu.roll(turn, HD, 1), 0.0)
+    sin_b = jnp.where(lane < HD // 2, -sin_b, sin_b)
+    same = seg == (lane - HD).astype(F32)
+    q_tail = jnp.where(same, 1.0, 0.0)
+    k_tail = jnp.where(same | (lane < HD), 0.0, -FAR)
+    v_tail = jnp.where(lane < HD, 0.0, 1.0)
+    scale = HD ** (-0.5) * LOG2E
+    q_cos, q_sin = cos_b * scale, sin_b * scale
+    width = held * LANES
+    for part in range(3):
+        mixed = jnp.dot(x_ref[0], w_ref[:, part * width : (part + 1) * width], preferred_element_type=F32)
+        for head in range(held):
+            value = mixed[:, head * LANES : (head + 1) * LANES]
+            if part == 0:
+                value = value * q_cos + pltpu.roll(value, HD // 2, 1) * q_sin + q_tail
+                q_ref[head] = value.astype(BF16)
+            elif part == 1:
+                value = value * cos_b + pltpu.roll(value, HD // 2, 1) * sin_b + k_tail
+                k_ref[head] = value.astype(BF16)
+            else:
+                v_ref[head] = (value + v_tail).astype(BF16)
+
+
+def project_heads(seg_row, place_row, freq, pieces, w_full, held):
+    count, rows, width = pieces.shape
+    length = count * rows
+    row_spec = pl.BlockSpec((1, 1, rows), lambda i: (i, 0, 0))
+    head_spec = pl.BlockSpec((held, rows, LANES), lambda i: (0, i, 0))
+    head_shape = jax.ShapeDtypeStruct((held, length, LANES), BF16)
+    return pl.pallas_call(
+        project_kernel,
+        out_shape=(head_shape, head_shape, head_shape, jax.ShapeDtypeStruct((length, LANES), F32)),
+        grid=(count,),
+        in_specs=[
+            row_spec,
+            row_spec,
+            pl.BlockSpec((1, LANES), lambda i: (0, 0)),
+            pl.BlockSpec((1, rows, width), lambda i: (i, 0, 0)),
+            pl.BlockSpec(w_full.shape, lambda i: (0, 0)),
+        ],
+        out_specs=(head_spec, head_spec, head_spec, pl.BlockSpec((rows, LANES), lambda i: (i, 0))),
+        compiler_params=pltpu.CompilerParams(vmem_limit_bytes=VMEM_LIMIT),
+        cost_estimate=pl.CostEstimate(
+            flops=2 * length * width * w_full.shape[1],
+            bytes_accessed=length * (width * 2 + held * LANES * 6 + LANES * 4),
+            transcendentals=length * LANES,
+        ),
+        name="project_heads",
+    )(seg_row.reshape(count, 1, rows), place_row.reshape(count, 1, rows), freq, pieces, w_full)
+
+
+def document_bounds(seg_row, rows):
     first = seg_row[::rows]
     last = seg_row[rows - 1 :: rows]
     low = jnp.sum((seg_row[None, :] < first[:, None]).astype(jnp.int32), axis=1)
     high = jnp.sum((seg_row[None, :] <= last[:, None]).astype(jnp.int32), axis=1)
-    low = low // align * align
-    count = (high - low + window - 1) // window
-    low = jnp.minimum(low, length - count * window)
-    return low.astype(jnp.int32), count.astype(jnp.int32)
-
-
-def attend_kernel(window, align, low_ref, count_ref, q_ref, k_ref, v_ref, sum_ref):
+    return low, high
+
+
+def windows(bounds, length, window, align):
+    low = bounds[0] // align * align
+    count = (bounds[1] - low + window - 1) // window
+    return jnp.minimum(low, length - count * window), count
+
+
+def attend_kernel(window, align, low_ref, count_ref, q_ref, k_ref, v_ref, sum_ref, joined_ref):
     block = pl.program_id(0)
     low = low_ref[block]
     sum_ref[...] = jnp.zeros_like(sum_ref)
@@ -361,29 +544,33 @@
         for head in range(q_ref.shape[0]):
             k_part = k_ref[head, pl.ds(start, window), :]
             v_part = v_ref[head, pl.ds(start, window), :]
-            score = lax.dot_general(
-                q_ref[head], k_part, (((1,), (1,)), ((), ())), preferred_element_type=F32
-            )
+            score = lax.dot_general(q_ref[head], k_part, BY_LANES, preferred_element_type=F32)
             expo = jnp.exp2(score).astype(BF16)
             sum_ref[head] += jnp.dot(expo, v_part, preferred_element_type=F32)
         return carry
 
     lax.fori_loop(0, count_ref[block], step, 0)
-
-
-def attend_heads(seg_row, q_ext, k_ext, v_ext, rows=512, window=1024, align=16):
+    for head in range(q_ref.shape[0]):
+        sums = sum_ref[head]
+        joined_ref[0, :, head * HD : (head + 1) * HD] = (sums[:, :HD] / sums[:, HD : HD + 1]).astype(BF16)
+
+
+def attend_heads(bounds, q_ext, k_ext, v_ext, rows, window=1024, align=16):
     heads, length, lanes = q_ext.shape
-    low, count = key_ranges(seg_row, rows, window, align)
+    low, count = windows(bounds, length, window, align)
     whole = pl.BlockSpec((heads, length, lanes), lambda i, *_: (0, 0, 0))
     part = pl.BlockSpec((heads, rows, lanes), lambda i, *_: (0, i, 0))
     return pl.pallas_call(
         functools.partial(attend_kernel, window, align),
-        out_shape=jax.ShapeDtypeStruct((heads, length, lanes), F32),
+        out_shape=(
+            jax.ShapeDtypeStruct((heads, length, lanes), F32),
+            jax.ShapeDtypeStruct((length // rows, rows, heads * HD), BF16),
+        ),
         grid_spec=pltpu.PrefetchScalarGridSpec(
             num_scalar_prefetch=2,
             grid=(length // rows,),
             in_specs=[part, whole, whole],
-            out_specs=part,
+            out_specs=(part, pl.BlockSpec((1, rows, heads * HD), lambda i, *_: (i, 0, 0))),
         ),
         compiler_params=pltpu.CompilerParams(vmem_limit_bytes=VMEM_LIMIT),
         cost_estimate=pl.CostEstimate(
@@ -396,58 +583,126 @@
 
 
 def attend_back_kernel(
-    window, align, low_ref, count_ref, q_ref, g_ref, qt_ref, gt_ref, k_ref, v_ref, dq_ref, dkt_ref, dvt_ref
+    window,
+    align,
+    low_ref,
+    count_ref,
+    q_ref,
+    sum_ref,
+    dout_ref,
+    turn_ref,
+    k_ref,
+    v_ref,
+    d_ref,
+    dq_ref,
+    dkv_ref,
+    g_ref,
+    gt_ref,
+    qt_ref,
 ):
     block = pl.program_id(0)
+    heads, rows, lanes = q_ref.shape
+    width = heads * HD
 
     @pl.when(block == 0)
     def _():
-        dkt_ref[...] = jnp.zeros_like(dkt_ref)
-        dvt_ref[...] = jnp.zeros_like(dvt_ref)
+        dkv_ref[...] = jnp.zeros_like(dkv_ref)
 
     dq_ref[...] = jnp.zeros_like(dq_ref)
+    half_lane = lax.broadcasted_iota(jnp.int32, (rows, HD), 1)
+    for head in range(heads):
+        dout = dout_ref[0, :, head * HD : (head + 1) * HD].astype(F32)
+        sums = sum_ref[head]
+        total = sums[:, HD : HD + 1]
+        g_low = dout / total
+        delta = -jnp.sum(dout * sums[:, :HD], axis=1, keepdims=True) / (total * total)
+        high = delta.astype(BF16).astype(F32)
+        middle = (delta - high).astype(BF16).astype(F32)
+        tail = jnp.where(
+            half_lane == 0,
+            high,
+            jnp.where(half_lane == 1, middle, jnp.where(half_lane == 2, delta - high - middle, 0.0)),
+        )
+        g_ext = jnp.concatenate([g_low, tail], axis=1)
+        g_ref[head] = g_ext.astype(BF16)
+        gt_ref[head] = jnp.transpose(g_ext)[:HD].astype(BF16)
+        qt_ref[head] = jnp.transpose(q_ref[head].astype(F32))[:HD].astype(BF16)
+
     low = low_ref[block]
-    by_lanes = (((1,), (1,)), ((), ()))
 
     def step(index, carry):
         start = pl.multiple_of(low + index * window, align)
-        for head in range(q_ref.shape[0]):
+        for head in range(heads):
             k_part = k_ref[head, pl.ds(start, window), :]
             v_part = v_ref[head, pl.ds(start, window), :]
-            score = lax.dot_general(q_ref[head], k_part, by_lanes, preferred_element_type=F32)
-            slope = lax.dot_general(g_ref[head], v_part, by_lanes, preferred_element_type=F32)
+            score = lax.dot_general(q_ref[head], k_part, BY_LANES, preferred_element_type=F32)
+            slope = lax.dot_general(g_ref[head], v_part, BY_LANES, preferred_element_type=F32)
             expo = jnp.exp2(score)
             d_score = (expo * slope).astype(BF16)
             expo = expo.astype(BF16)
             dq_ref[head] += jnp.dot(d_score, k_part, preferred_element_type=F32)
-            dvt_ref[head, :, pl.ds(start, window)] += jnp.dot(gt_ref[head], expo, preferred_element_type=F32)
-            dkt_ref[head, :, pl.ds(start, window)] += jnp.dot(qt_ref[head], d_score, preferred_element_type=F32)
+            dkv_ref[head, :HD, pl.ds(start, window)] += jnp.dot(qt_ref[head], d_score, preferred_element_type=F32)
+            dkv_ref[head, HD:, pl.ds(start, window)] += jnp.dot(gt_ref[head], expo, preferred_element_type=F32)
         return carry
 
     lax.fori_loop(0, count_ref[block], step, 0)
 
-
-def attend_back_heads(seg_row, q_ext, k_ext, v_ext, g_ext, rows=512, window=512, align=128):
+    lane = lax.broadcasted_iota(jnp.int32, (rows, lanes), 1)
+
+    def turn_back(value, turn):
+        swapped = jnp.where(lane < HD // 2, pltpu.roll(value, lanes - HD // 2, 1), pltpu.roll(value, HD // 2, 1))
+        sine = pltpu.roll(turn, HD, 1)
+        sine = jnp.where(lane < HD // 2, sine, -sine)
+        return (value * turn + swapped * sine)[:, :HD]
+
+    here = turn_ref[pl.ds(pl.multiple_of(block * rows, rows), rows), :]
+    for head in range(heads):
+        turned = turn_back(dq_ref[head] * HD ** (-0.5), here)
+        d_ref[block, :, head * HD : (head + 1) * HD] = turned.astype(BF16)
+
+    @pl.when(block == pl.num_programs(0) - 1)
+    def _():
+        def finish(piece, carry):
+            start = pl.multiple_of(piece * rows, rows)
+            turn = turn_ref[pl.ds(start, rows), :]
+            for head in range(heads):
+                both = jnp.transpose(dkv_ref[head, :, pl.ds(start, rows)])
+                at = width + head * HD
+                d_ref[piece, :, at : at + HD] = (turn_back(both, turn) * LN2).astype(BF16)
+                d_ref[piece, :, width + at : width + at + HD] = both[:, HD:].astype(BF16)
+            return carry
+
+        lax.fori_loop(0, d_ref.shape[0], finish, 0)
+
+
+def attend_back_heads(bounds, q_ext, k_ext, v_ext, sums, dout, turn, window=512, align=128):
     heads, length, lanes = q_ext.shape
-    low, count = key_ranges(seg_row, rows, window, align)
-    q_turned = jnp.swapaxes(q_ext[:, :, :HD], 1, 2)
-    g_turned = jnp.swapaxes(g_ext[:, :, :HD], 1, 2)
+    count_blocks, rows, width = dout.shape
+    low, count = windows(bounds, length, window, align)
     whole = pl.BlockSpec((heads, length, lanes), lambda i, *_: (0, 0, 0))
     part = pl.BlockSpec((heads, rows, lanes), lambda i, *_: (0, i, 0))
-    turned_part = pl.BlockSpec((heads, HD, rows), lambda i, *_: (0, 0, i))
-    turned = pl.BlockSpec((heads, HD, length), lambda i, *_: (0, 0, 0))
     return pl.pallas_call(
         functools.partial(attend_back_kernel, window, align),
-        out_shape=(
-            jax.ShapeDtypeStruct((heads, length, lanes), F32),
-            jax.ShapeDtypeStruct((heads, HD, length), F32),
-            jax.ShapeDtypeStruct((heads, HD, length), F32),
-        ),
+        out_shape=jax.ShapeDtypeStruct((count_blocks, rows, 3 * width), BF16),
         grid_spec=pltpu.PrefetchScalarGridSpec(
             num_scalar_prefetch=2,
-            grid=(length // rows,),
-            in_specs=[part, part, turned_part, turned_part, whole, whole],
-            out_specs=(part, turned, turned),
+            grid=(count_blocks,),
+            in_specs=[
+                part,
+                part,
+                pl.BlockSpec((1, rows, width), lambda i, *_: (i, 0, 0)),
+                pl.BlockSpec((length, lanes), lambda i, *_: (0, 0)),
+                whole,
+                whole,
+            ],
+            out_specs=pl.BlockSpec((count_blocks, rows, 3 * width), lambda i, *_: (0, 0, 0)),
+            scratch_shapes=[
+                pltpu.VMEM((heads, rows, lanes), F32),
+                pltpu.VMEM((heads, 2 * HD, length), F32),
+                pltpu.VMEM((heads, rows, lanes), BF16),
+                pltpu.VMEM((heads, HD, rows), BF16),
+                pltpu.VMEM((heads, HD, rows), BF16),
+            ],
         ),
         compiler_params=pltpu.CompilerParams(vmem_limit_bytes=VMEM_LIMIT),
         cost_estimate=pl.CostEstimate(
@@ -456,36 +711,43 @@
             transcendentals=heads * length * length // 2,
         ),
         name="attend_back_heads",
-    )(low, count, q_ext, g_ext, q_turned, g_turned, k_ext, v_ext)
+    )(low, count, q_ext, sums, dout, turn, k_ext, v_ext)
 
 
 def document_places(seg_row):
     length = seg_row.shape[0]
-    ids = jnp.arange(LANES - HD, dtype=jnp.int32)
-    starts = jnp.sum((seg_row[None, :] < ids[:, None]).astype(jnp.int32), axis=1)
-    same = seg_row[:, None] == ids[None, :]
-    start = jnp.sum(jnp.where(same, starts[None, :], 0), axis=1)
-    return same, jnp.arange(length, dtype=jnp.int32) - start
-
-
-def by_group(block_rows, groups):
+    ids = jnp.arange(LANES - HD, dtype=jnp.int32)[:, None]
+    starts = jnp.sum((seg_row[None, :] < ids).astype(jnp.int32), axis=1, keepdims=True)
+    start = jnp.sum(jnp.where(seg_row[None, :] == ids, starts, 0), axis=0)
+    return jnp.arange(length, dtype=jnp.int32) - start
+
+
+def by_group(block_rows):
     seqs, rows, width = block_rows.shape
-    split = block_rows.reshape(seqs, rows, groups, width // groups)
-    return jnp.transpose(split, (0, 2, 1, 3)).reshape(seqs * groups, rows, width // groups)
-
-
-def from_group(blocks, groups):
+    split = block_rows.reshape(seqs, rows, GROUPS, width // GROUPS)
+    return jnp.transpose(split, (0, 2, 1, 3)).reshape(seqs * GROUPS, rows, width // GROUPS)
+
+
+def from_group(blocks):
     devices, rows, width = blocks.shape
-    split = blocks.reshape(devices // groups, groups, rows, width)
-    return jnp.transpose(split, (0, 2, 1, 3)).reshape(devices // groups, rows, groups * width)
+    split = blocks.reshape(devices // GROUPS, GROUPS, rows, width)
+    return jnp.transpose(split, (0, 2, 1, 3)).reshape(devices // GROUPS, rows, GROUPS * width)
 
 
 def exchange(blocks):
     return lax.all_to_all(blocks, "seq", 0, 0, tiled=True)
 
 
+def head_columns(w_qkv, group, held):
+    depth = w_qkv.shape[0]
+    split = w_qkv.reshape(depth, 3, GROUPS, held, HD)
+    mine = lax.dynamic_index_in_dim(split, group, 2, keepdims=False)
+    second = mine * jnp.array([1, 1, 0], w_qkv.dtype)[None, :, None, None]
+    return jnp.concatenate([mine, second], axis=-1).reshape(depth, 3 * held * 2 * HD)
+
+
 def local_heads(
-    seq_size,
+    shards,
     tokens,
     segments,
     positions,
@@ -501,46 +763,28 @@
     ln2_bias,
 ):
     seq_count, row_count, model_width = tokens.shape
-    groups = seq_size // seq_count
-    held = HEADS // groups
-    length = row_count * seq_size
-    score_scale = HD ** (-0.5)
-    my_seq = lax.axis_index("seq") // groups
-    seg_row = lax.dynamic_index_in_dim(segments, my_seq, 0, keepdims=False)
+    held = HEADS // GROUPS
+    length = row_count * SEQ_SIZE
+    me = lax.axis_index("seq")
+    seg_row = lax.dynamic_index_in_dim(segments, me // GROUPS, 0, keepdims=False)
 
     def gather(shard):
         return lax.all_gather(shard, "shard", axis=0, tiled=True)
 
+    pieces, w_heads = gather_tokens(tokens, head_columns(w_qkv, me % GROUPS, held), shards)
     full_qkv = gather(w_qkv)
     norms = gather(jnp.stack([ln1_gain, ln1_bias, ln2_gain, ln2_bias], axis=1)).astype(F32)
     gain_one, bias_one, gain_two, bias_two = (norms[:, n] for n in range(4))
     full_out, full_gate, full_up, full_down = (gather(w) for w in (w_out, w_gate, w_up, w_down))
-
-    cos_b, sin_b = rope_tables(positions)
-    qkv_all = jnp.einsum("scd,de->sce", tokens, full_qkv, preferred_element_type=F32)
-    q_heads = rotate(head_split(qkv_all[..., :model_width], seq_count, row_count), cos_b, sin_b)
-    k_heads = rotate(
-        head_split(qkv_all[..., model_width : 2 * model_width], seq_count, row_count), cos_b, sin_b
-    )
-    q_low = (q_heads * (score_scale * LOG2E)).astype(BF16).reshape(seq_count, row_count, model_width)
-    k_low = k_heads.astype(BF16).reshape(seq_count, row_count, model_width)
-    v_low = qkv_all[..., 2 * model_width :].astype(BF16)
-    sent = jnp.concatenate([by_group(part, groups) for part in (q_low, k_low, v_low)], axis=-1)
-    taken = exchange(sent).reshape(length, 3, held, HD)
-
-    same, place = document_places(seg_row)
-    own = jnp.broadcast_to(same.astype(BF16), (held, length, LANES - HD))
-    other = jnp.broadcast_to(jnp.where(same, 0.0, -FAR).astype(BF16), (held, length, LANES - HD))
-    ones = jnp.ones((held, length, LANES - HD), BF16)
-    q_own, k_own, v_own = (jnp.transpose(taken[:, n], (1, 0, 2)) for n in range(3))
-    q_ext = jnp.concatenate([q_own, own], axis=-1)
-    k_ext = jnp.concatenate([k_own, other], axis=-1)
-    v_ext = jnp.concatenate([v_own, ones], axis=-1)
-    sums = attend_heads(seg_row, q_ext, k_ext, v_ext)
-    total = sums[..., HD : HD + 1]
-    o_own = sums[..., :HD] / total
-    joined_own = jnp.transpose(o_own, (1, 0, 2)).astype(BF16).reshape(seq_size, row_count, held * HD)
-    joined = from_group(exchange(joined_own), groups)
+    freqs = jnp.exp(jnp.arange(HD // 2, dtype=F32) * (-math.log(ROPE_BASE) / (HD // 2)))
+    freq = jnp.tile(freqs, LANES // (HD // 2))[None]
+    place = document_places(seg_row).astype(F32)
+    bounds = document_bounds(seg_row, row_count)
+    q_ext, k_ext, v_ext, turn = project_heads(
+        seg_row.astype(F32), place, freq, pieces, w_heads.reshape(model_width, -1), held
+    )
+    sums, joined_own = attend_heads(bounds, q_ext, k_ext, v_ext, row_count)
+    joined = from_group(exchange(joined_own))
 
     tokens_f = tokens.astype(F32)
     h_one = tokens_f + jnp.einsum("sci,io->sco", joined, full_out, preferred_element_type=F32)
@@ -588,34 +832,19 @@
     )
     owned = [reduce_shards(g) for g in (grad_out, grad_gate, grad_up, grad_down)]
 
-    dout = exchange(by_group(d_joined, groups)).reshape(length, held, HD)
-    dout = jnp.transpose(dout, (1, 0, 2)).astype(F32)
-    g_low = (dout / total).astype(BF16)
-    delta = -jnp.sum(dout * o_own, axis=-1, keepdims=True) / total
-    d_high = delta.astype(BF16)
-    d_mid = (delta - d_high.astype(F32)).astype(BF16)
-    d_small = (delta - d_high.astype(F32) - d_mid.astype(F32)).astype(BF16)
-    g_ext = jnp.concatenate(
-        [g_low, d_high, d_mid, d_small, jnp.zeros((held, length, LANES - HD - 3), BF16)], axis=-1
-    )
-    dq, dk_turned, dv_turned = attend_back_heads(seg_row, q_ext, k_ext, v_ext, g_ext)
-
-    cos_f, sin_f = (t[0] for t in rope_tables(place[None]))
-    dq_own = jnp.transpose(dq[..., :HD], (1, 0, 2)) * score_scale
-    dk_own = jnp.transpose(dk_turned, (2, 0, 1)) * LN2
-    dv_own = jnp.transpose(dv_turned, (2, 0, 1))
-    d_parts = [
-        part.astype(BF16).reshape(seq_size, row_count, held * HD)
-        for part in (rotate_back(dq_own, cos_f, sin_f), rotate_back(dk_own, cos_f, sin_f), dv_own)
-    ]
-    d_taken = exchange(jnp.concatenate(d_parts, axis=-1))
-    d_split = d_taken.reshape(seq_count, groups, row_count, 3, held * HD)
+    dout = exchange(by_group(d_joined))
+    d_heads = attend_back_heads(bounds, q_ext, k_ext, v_ext, sums, dout, turn)
+    d_heads, *owned = lax.optimization_barrier((d_heads, *owned))
+    summed = [lax.psum(g, "seq") for g in owned]
+    d_taken = exchange(d_heads)
+    d_taken, *summed = lax.optimization_barrier((d_taken, *summed))
+    d_split = d_taken.reshape(seq_count, GROUPS, row_count, 3, held * HD)
     d_qkv = jnp.transpose(d_split, (0, 2, 3, 1, 4)).reshape(seq_count, row_count, 3 * model_width)
     grad_qkv = jnp.einsum("scd,sce->de", tokens, d_qkv, preferred_element_type=F32).astype(BF16)
     d_tokens = dh_one + jnp.einsum("sce,de->scd", d_qkv, full_qkv, preferred_element_type=F32)
     input_grad = d_tokens.astype(BF16)
 
-    grad_out, grad_gate, grad_up, grad_down = (lax.psum(g, "seq").astype(F32) for g in owned)
+    grad_out, grad_gate, grad_up, grad_down = (g.astype(F32) for g in summed)
     grad_qkv = lax.psum(reduce_shards(grad_qkv), "seq").astype(F32)
     norm_sums = lax.psum(reduce_shards(grad_norms), "seq")
     return (
@@ -662,6 +891,5 @@
         P("shard"),
         P("shard"),
     )
-    heads_split = mesh.shape["seq"] % SEQS_HELD == 0 and HEADS % (mesh.shape["seq"] // SEQS_HELD) == 0
-    body = functools.partial(local_heads, mesh.shape["seq"]) if heads_split else local
+    body = functools.partial(local_heads, mesh.shape["shard"]) if mesh.shape["seq"] == SEQ_SIZE else local
     return jax.shard_map(body, mesh=mesh, in_specs=in_specs, out_specs=out_specs, check_vma=False)

time: 1170 us -> 930 us (0.79)
  waiting for transfers between devices: 575 us -> 423 us
  Pallas kernels: 107 us -> 232 us
  local copies, waits for them, and re-layouts: 137 us -> 41.7 us
  blocking collectives: 120 us -> 61.9 us
  other arithmetic: 45.3 us -> 17.1 us
  starting transfers between devices: 24 us -> 11.5 us
  matrix products: 130 us -> 118 us
    psum x0 -> x1, waiting for transfers between devices: none -> 226 us  [local_heads(): summed = [lax.psum(g, 'seq') for g in owned]]
    reduce_scatter x4, waiting for transfers between devices: 178 us -> 27.2 us  [reduce_shards(): return lax.psum_scatter(partial, 'shard', scatter_dimension=0, tiled=True)]
    all_to_all x3 -> x2, waiting for transfers between devices: 144 us -> 28.9 us  [exchange(): return lax.all_to_all(blocks, 'seq', 0, 0, tiled=True)]
    pallas_call x0 -> x2, Pallas kernels: none -> 89.8 us  [the longest x1 68.8 us: gather_tokens(): pl.pallas_call(functools.partial(gather_kernel, chunks, by_z), out_shape=...]
    psum x1, waiting for transfers between devices: 156 us -> 74.9 us  [local_heads(): grad_qkv = lax.psum(reduce_shards(grad_qkv), 'seq').astype(F32)]
    all_to_all x1, blocking collectives: 98.6 us -> 41.6 us  [exchange(): return lax.all_to_all(blocks, 'seq', 0, 0, tiled=True)]
    unnamed x90 -> x54, local copies, waits for them, and re-layouts: 50.2 us -> 19.7 us
    unnamed x14 -> x15, waiting for transfers between devices: 66.8 us -> 36.5 us
  transfers between devices with their start and end apart: 15 -> 15, of which waited for: 11 -> 7; matrix products, arithmetic and copies ran while one was open for 13% -> 8% of each run, Pallas kernels for 3% -> 25%
where the time goes in v2:
time: 930 us; the launch traced here: 920 us
  waiting for transfers between devices  423 us (45%)
  Pallas kernels  232 us (25%)
  matrix products  118 us (13%)
  blocking collectives  61.9 us (7%)
  local copies, waits for them, and re-layouts  41.7 us (4%)
  other arithmetic  17.1 us (2%)
  between operations  14.9 us (2%)
  starting transfers between devices  11.5 us (1%)
    psum x1, waiting for transfers between devices, local_heads(): summed = [lax.psum(g, 'seq') for g in owned]  226 us
    pallas_call x1, Pallas kernels, attend_back_heads(): pl.pallas_call(functools.partial(attend_back_kernel, window, align), out_...  102 us
    psum x1, waiting for transfers between devices, local_heads(): grad_qkv = lax.psum(reduce_shards(grad_qkv), 'seq').astype(F32)  74.9 us
    pallas_call x1, Pallas kernels, gather_tokens(): pl.pallas_call(functools.partial(gather_kernel, chunks, by_z), out_shape=...  68.8 us
    all_to_all x1, blocking collectives, exchange(): return lax.all_to_all(blocks, 'seq', 0, 0, tiled=True)  41.6 us
    pallas_call x1, Pallas kernels, attend_heads(): pl.pallas_call(functools.partial(attend_kernel, window, align), out_shape...  40.5 us
    unnamed x15, waiting for transfers between devices  36.5 us
    all_gather x5, waiting for transfers between devices, gather(): return lax.all_gather(shard, 'shard', axis=0, tiled=True)  29.6 us
  transfers between devices with their start and end apart: 15, of which 7 were waited for; matrix products, arithmetic and copies ran while one was open for 8% of the time, Pallas kernels for 25%

profile of v2, /device:TPU:20, one launch (start us, length us, event | category | flops | bytes accessed | tf_op | source)
XLA Modules:
  0.0 920.5 jit_solution(13766379004596434092)
XLA Ops:
  7.2 0.7 all-gather.7.cloned.1.call-update
  8.0 0.7 all-gather.9.cloned.1.call-update
  8.7 0.7 all-gather.11.cloned.1.call-update
  9.4 1.4 fusion.38
  11.0 0.6 broadcast_in_dim_tile.3.freq_ref
  11.6 0.6 copy.67
  12.4 1.0 copy.86.w_ref
  13.4 68.8 %gather_tokens.1 = (bf16[8,512,768]{2,1,0:T(8,128)(2,1)}, bf16[4,192,1152]{2,1,0:T(8,128)(2,1)}) custom-call(bf16[2,512,768]{2,1,0:T(8,128)(2,1)} %tok_ref.1, bf16[192,1152]{1,0:T(8,128)(2,1)} %copy.86.w_ref), custom_call_target="tpu_custom_call" | custom-call | tf_op jit(solution)/shard_map/gather_tokens/pallas_call | solution.py:443
  83.5 0.6 subtract_convert_fusion.place_ref
  84.1 21.0 %project_heads.1 = (bf16[3,4096,128]{2,1,0:T(8,128)(2,1)}, bf16[3,4096,128]{2,1,0:T(8,128)(2,1)}, bf16[3,4096,128]{2,1,0:T(8,128)(2,1)}, f32[4096,128]{1,0:T(8,128)}) custom-call(f32[8,1,512]{2,1,0:T(1,128)} %bitcast.112, f32[8,1,512]{2,1,0:T(1,128)} %subtract_convert_fusion.place_ref, f32[1,128]{1,0:T(1,128)} %broadcast_in_dim_tile.3.freq_ref, ...), custom_call_target="tpu_custom_call" | custom-call | flops 7247757312 | bytes 17825792 | tf_op jit(solution)/shard_map/project_heads/pallas_call | solution.py:501
  105.1 40.5 %attend_heads.1 = (f32[3,4096,128]{2,1,0:T(8,128)}, bf16[8,512,192]{2,1,0:T(8,128)(2,1)}) custom-call(s32[8]{0:T(128)} %get-tuple-element.150.low_ref, s32[8]{0:T(128)} %get-tuple-element.151.count_ref, bf16[3,4096,128]{2,1,0:T(8,128)(2,1)} %get-tuple-element.36.q_ref, bf16[3,4096,128]{2,1,0:T(8,128)(2,1)} %get-tuple-element.37.k_ref, ...), custom_call_target="tpu_custom_call" | custom-call | flops 12884901888 | bytes 15728640 | tf_op jit(solution)/shard_map/attend_heads/pallas_call | solution.py:563
  145.6 3.9 copy.69
  149.5 5.1 all-to-all-start
  155.3 5.2 all-gather
  160.7 28.9 %all-to-all-done = bf16[8,512,192]{1,2,0:T(8,128)(2,1)S(1)} async-done(((bf16[8,512,192]{1,2,0:T(8,128)(2,1)}), bf16[8,512,192]{1,2,0:T(8,128)(2,1)S(1)}, u32[]{:S(2)}, u32[]{:S(2)}) %all-to-all-start) | async-done | bytes 1572896 | tf_op jit(solution)/shard_map/all_to_all | solution.py:738
  189.6 1.1 copy-done.8
  190.7 3.8 fusion.41
  195.0 1.7 fusion.24
  196.7 10.6 %fusion.11 = f32[2,512,3072]{2,1,0:T(8,128)} fusion(bf16[2,512,768]{2,1,0:T(8,128)(2,1)} %fusion.24, bf16[768,3072]{1,0:T(8,128)(2,1)} %all-gather.9.cloned.1.call-done), kind=kOutput, calls=%fused_computation.22 | convolution fusion | flops 4831838208 | bytes 18874368 | tf_op jit(solution)/shard_map/scd,df->scf/dot_general | solution.py:793
  207.3 13.5 %multiply_convert_fusion.2 = (bf16[2,512,3072]{2,1,0:T(8,128)(2,1)}, f32[2,512,3072]{2,1,0:T(8,128)}) fusion(f32[2,512,3072]{2,1,0:T(8,128)} %fusion.11, bf16[2,512,768]{2,1,0:T(8,128)(2,1)} %fusion.24, bf16[768,3072]{1,0:T(8,128)(2,1)} %all-gather.11.cloned.1.call-done), kind=kOutput, calls=%fused_computation.2 | convolution fusion | flops 4850712576 | bytes 37748736 | tf_op jit(solution)/shard_map/scd,df->scf/dot_general | solution.py:794
  220.8 8.7 fusion.42
  230.1 2.0 copy-done.2
  232.1 1.6 fusion.22
  233.7 2.2 fusion.33
  235.9 1.1 copy-done.11
  237.1 6.9 bitcast_convert_fusion.2
  244.0 19.1 %multiply_convert_fusion.1 = (bf16[2,512,3072]{2,1,0:T(8,128)(2,1)}, bf16[2,512,3072]{2,1,0:T(8,128)(2,1)}) fusion(f32[2,512,3072]{2,1,0:T(8,128)} %fusion.11, f32[2,512,3072]{2,1,0:T(8,128)} %get-tuple-element.157, bf16[2,512,768]{2,1,0:T(8,128)(2,1)} %copy-done.11, bf16[3072,768]{1,0:T(8,128)(2,1)} %all-gather.13.cloned.1.call-done), kind=kOutput, calls=%fused_computation.1 | convolution fusion | flops 4872732672 | bytes 44040192 | tf_op jit(solution)/shard_map/scd,fd->scf/dot_general | solution.py:807
  263.1 9.2 bitcast_convert_fusion.1
  272.2 9.2 bitcast_convert_fusion
  281.4 8.7 fusion.5
  290.2 10.4 %multiply_reduce_fusion = (f32[768]{0:T(1024)S(1)}, f32[2,512]{1,0:T(2,128)S(1)}, f32[2,512]{1,0:T(2,128)S(1)}, f32[768]{0:T(1024)S(1)}, f32[2,512,768]{2,1,0:T(8,128)S(1)}) fusion(f32[2,512,768]{2,1,0:T(8,128)S(1)} %get-tuple-element.155, f32[2,512]{1,0:T(2,128)S(1)} %add_rsqrt_fusion.1, f32[2,512]{1,0:T(2,128)S(1)} %broadcast_multiply_fusion.6, ...), kind=kOutput, calls=%fused_computation.34 | convolution fusion | flops 4846776320 | bytes 25210880 | tf_op jit(solution)/shard_map/scf,df->scd/dot_general | solution.py:812
  300.7 1.0 subtract_multiply_fusion
  301.7 1.6 copy-done.6
  303.3 2.4 bitcast_convert_fusion.4
  305.7 3.3 convolution_convert_fusion
  309.7 0.7 reduce-scatter.15.cloned.1.call-update
  310.4 0.7 reduce-scatter.17.cloned.1.call-update
  311.9 2.3 copy.75
  314.2 41.6 %all_to_all.15 = bf16[8,512,192]{1,2,0:T(8,128)(2,1)S(1)} all-to-all(bf16[8,512,192]{1,2,0:T(8,128)(2,1)} %copy.75), channel_id=1, replica_groups=mesh['seq'=8,'shard'=4] {'seq'}, dimensions={0} | all-to-all | bytes 3145728 | tf_op jit(solution)/shard_map/all_to_all | solution.py:738
  355.8 2.4 copy.76.dout_ref
  358.2 102.0 %attend_back_heads.1 = bf16[8,512,576]{2,1,0:T(8,128)(2,1)} custom-call(s32[8]{0:T(128)} %get-tuple-element.130.low_ref, s32[8]{0:T(128)} %get-tuple-element.131.count_ref, bf16[3,4096,128]{2,1,0:T(8,128)(2,1)} %get-tuple-element.36.q_ref, f32[3,4096,128]{2,1,0:T(8,128)} %get-tuple-element.40.sum_ref, bf16[8,512,192]{2,1,0:T(8,128)(2,1)} %copy.76.dout_ref, ...), custom_call_target="tpu_custom_call" | custom-call | flops 32212254720 | bytes 31457280 | tf_op jit(solution)/shard_map/attend_back_heads/pallas_call | solution.py:684
  460.2 27.1 %reduce-scatter.17.cloned.1.call-done = bf16[768,768]{1,0:T(8,128)(2,1)} async-done(((bf16[3072,768]{1,0:T(8,128)(2,1)}), bf16[768,768]{1,0:T(8,128)(2,1)}) %reduce-scatter.17.cloned.1.call-update) | async-done | bytes 1179664 | tf_op jit(solution)/shard_map/reduce_scatter | solution.py:828
  487.4 7.6 copy.77
  495.0 6.0 all-to-all-start.2
  501.0 0.7 all-reduce.6.cloned.1.call-update
  501.9 0.9 copy.89
  502.9 225.8 %all-reduce.6.cloned.1.call-done = (bf16[192,768]{1,0:T(8,128)(2,1)}, bf16[192,3072]{1,0:T(8,128)(2,1)}, bf16[192,3072]{1,0:T(8,128)(2,1)}, bf16[768,768]{1,0:T(8,128)(2,1)}) async-done(((bf16[192,768]{1,0:T(8,128)(2,1)}, bf16[192,3072]{1,0:T(8,128)(2,1)}, bf16[192,3072]{1,0:T(8,128)(2,1)}, bf16[768,768]{1,0:T(8,128)(2,1)}), (bf16[192,768]{1,0:T(8,128)(2,1)}, bf16[192,3072]{1,0:T(8,128)(2,1)}, ...) | async-done | bytes 3833872 | tf_op jit(solution)/shard_map/psum | solution.py:838
  728.7 2.8 copy.78
  731.5 2.1 copy-done.4
  733.6 4.0 fusion.13
  737.6 4.0 copy.87
  742.3 10.1 %reduce-scatter.21.cloned.1.call-done = f32[192,4]{1,0:T(8,128)} async-done(((f32[768,4]{1,0:T(8,128)}), f32[192,4]{1,0:T(8,128)}) %reduce-scatter.21.cloned.1.call-update) | async-done | bytes 3088
  752.4 1.0 copy.90
  753.4 15.1 %psum.47 = f32[192,4]{0,1:T(4,128)S(1)} all-reduce(f32[192,4]{0,1:T(4,128)S(1)} %copy.90), channel_id=1, replica_groups=mesh['seq'=8,'shard'=4] {'seq'}, use_global_device_ids=true, to_apply=%region_27.28 | all-reduce | flops 768 | bytes 6144 | tf_op jit(solution)/shard_map/psum | solution.py:849
  769.1 0.9 convert_element_type.126
  769.9 1.7 convert_element_type.127
  771.6 1.7 convert_element_type.128
  773.3 1.6 convert_element_type.129
  774.9 20.6 %reduce-scatter.19.cloned.1.call-done = bf16[192,2304]{1,0:T(8,128)(2,1)} async-done(((bf16[768,2304]{1,0:T(8,128)(2,1)}), bf16[192,2304]{1,0:T(8,128)(2,1)}) %reduce-scatter.19.cloned.1.call-update) | async-done | bytes 884752
  795.4 2.6 copy.88
  798.0 29.6 %all-gather.15.cloned.1.call-done = bf16[768,2304]{1,0:T(8,128)(2,1)} async-done(((bf16[192,2304]{1,0:T(8,128)(2,1)}), bf16[768,2304]{1,0:T(8,128)(2,1)}) %all-gather.15.cloned.1.call-update) | async-done | bytes 3538960 | tf_op jit(solution)/shard_map/all_gather | solution.py:772
  827.6 8.4 add_convert_fusion
  836.1 74.9 %all-reduce.4.cloned.1.call-done = bf16[192,2304]{0,1:T(8,128)(2,1)} async-done(((bf16[192,2304]{0,1:T(8,128)(2,1)}), bf16[192,2304]{0,1:T(8,128)(2,1)}) %all-reduce.4.cloned.1.call-update) | async-done | bytes 884752 | tf_op jit(solution)/shard_map/psum | solution.py:848
  911.0 2.5 copy.80
  (108 shorter events, 6.5 us)
Async XLA Ops:
  7.2 5.1 copy-start.16
  7.2 4.4 copy-start.5
  7.2 153.5 %all-gather.7.cloned.1.call-start = ((), (), s32[]{:S(2)}) async-start(), calls=%async_computation.9 | async-start | bytes 1474560 | tf_op jit(solution)/shard_map/all_gather | solution.py:772
  7.9 188.8 %all-gather.9.cloned.1.call-start = ((), (), s32[]{:S(2)}) async-start(), calls=%async_computation.10 | async-start | bytes 5898240 | tf_op jit(solution)/shard_map/all_gather | solution.py:772
  8.7 198.6 %all-gather.11.cloned.1.call-start = ((), (), s32[]{:S(2)}) async-start(), calls=%async_computation.11 | async-start | bytes 5898240 | tf_op jit(solution)/shard_map/all_gather | solution.py:772
  145.6 9.6 %copy-start.18 = (bf16[192]{0:T(256)(128)(2,1)S(1)}, bf16[192]{0:T(256)(128)(2,1)}, u32[]{:S(2)}) copy-start(bf16[192]{0:T(256)(128)(2,1)} %param.25) | copy-start | bytes 1156
  145.6 9.6 %copy-start.19 = (bf16[192]{0:T(256)(128)(2,1)S(1)}, bf16[192]{0:T(256)(128)(2,1)}, u32[]{:S(2)}) copy-start(bf16[192]{0:T(256)(128)(2,1)} %param.24) | copy-start | bytes 1156
  145.6 9.7 %copy-start.20 = (bf16[192]{0:T(256)(128)(2,1)S(1)}, bf16[192]{0:T(256)(128)(2,1)}, u32[]{:S(2)}) copy-start(bf16[192]{0:T(256)(128)(2,1)} %param.23) | copy-start | bytes 1156
  145.6 9.7 %copy-start.21 = (bf16[192]{0:T(256)(128)(2,1)S(1)}, bf16[192]{0:T(256)(128)(2,1)}, u32[]{:S(2)}) copy-start(bf16[192]{0:T(256)(128)(2,1)} %param.22) | copy-start | bytes 1156
  149.5 40.0 %all-to-all-start = ((bf16[8,512,192]{1,2,0:T(8,128)(2,1)}), bf16[8,512,192]{1,2,0:T(8,128)(2,1)S(1)}, u32[]{:S(2)}, u32[]{:S(2)}) async-start(bf16[8,512,192]{1,2,0:T(8,128)(2,1)} %copy.69), calls=%async_computation | async-start | bytes 3145728 | tf_op jit(solution)/shard_map/all_to_all | solution.py:738
  154.6 66.2 %all-gather.13.cloned.1.call-start = ((), (), s32[]{:S(2)}) async-start(), calls=%async_computation.12 | async-start | bytes 5898240 | tf_op jit(solution)/shard_map/all_gather | solution.py:772
  155.2 305.0 %reduce-scatter.11.cloned.1.call-start = ((), (), s32[]{:S(2)}) async-start(), calls=%async_computation.13 | async-start | bytes 1474560 | tf_op jit(solution)/shard_map/reduce_scatter | solution.py:828
  189.6 1.1 copy-start.8
  229.5 4.2 copy-start
  229.6 2.5 copy-start.2
  232.1 5.0 slice-start
  233.7 3.3 slice-start.1
  235.9 1.1 copy-start.11
  281.4 8.8 copy-start.1
  281.4 8.8 copy-start.3
  300.7 2.6 copy-start.9
  301.6 1.6 copy-start.6
  303.3 2.4 copy-start.17
  309.0 151.2 %reduce-scatter.13.cloned.1.call-start = ((), (), s32[]{:S(2)}) async-start(), calls=%async_computation.14 | async-start | bytes 5898240 | tf_op jit(solution)/shard_map/reduce_scatter | solution.py:828
  309.6 150.6 %reduce-scatter.15.cloned.1.call-start = ((), (), s32[]{:S(2)}) async-start(), calls=%async_computation.15 | async-start | bytes 5898240 | tf_op jit(solution)/shard_map/reduce_scatter | solution.py:828
  310.4 177.0 %reduce-scatter.17.cloned.1.call-start = ((), (), s32[]{:S(2)}) async-start(), calls=%async_computation.16 | async-start | bytes 5898240 | tf_op jit(solution)/shard_map/reduce_scatter | solution.py:828
  495.0 233.6 %all-to-all-start.2 = ((bf16[8,512,576]{1,2,0:T(8,128)(2,1)}), bf16[8,512,576]{1,2,0:T(8,128)(2,1)}, u32[]{:S(2)}, u32[]{:S(2)}) async-start(bf16[8,512,576]{1,2,0:T(8,128)(2,1)} %copy.77), calls=%async_computation.6 | async-start | bytes 9437184 | tf_op jit(solution)/shard_map/all_to_all | solution.py:738
  501.0 227.6 %all-reduce.6.cloned.1.call-start = ((), (), s32[]{:S(2)}) async-start(), calls=%async_computation.21 | async-start | bytes 7667712 | tf_op jit(solution)/shard_map/psum | solution.py:838
  501.8 250.7 %reduce-scatter.21.cloned.1.call-start = ((), (), s32[]{:S(2)}) async-start(), calls=%async_computation.20 | async-start | bytes 491520
  502.8 292.6 %reduce-scatter.19.cloned.1.call-start = ((), (), s32[]{:S(2)}) async-start(), calls=%async_computation.19 | async-start | bytes 4423680
  728.7 4.9 copy-start.10
  731.4 2.1 copy-start.4
  741.6 27.4 %copy-start.15 = (bf16[192,768]{1,0:T(8,128)(2,1)S(1)}, bf16[192,768]{1,0:T(8,128)(2,1)}, u32[]{:S(2)}) copy-start(bf16[192,768]{1,0:T(8,128)(2,1)} %get-tuple-element.53) | copy-start | bytes 884740
  741.7 28.3 %copy-start.14 = (bf16[192,3072]{1,0:T(8,128)(2,1)S(1)}, bf16[192,3072]{1,0:T(8,128)(2,1)}, u32[]{:S(2)}) copy-start(bf16[192,3072]{1,0:T(8,128)(2,1)} %get-tuple-element.54) | copy-start | bytes 3538948
  741.7 29.9 %copy-start.13 = (bf16[192,3072]{1,0:T(8,128)(2,1)S(1)}, bf16[192,3072]{1,0:T(8,128)(2,1)}, u32[]{:S(2)}) copy-start(bf16[192,3072]{1,0:T(8,128)(2,1)} %get-tuple-element.55) | copy-start | bytes 3538948
  741.7 85.9 %all-gather.15.cloned.1.call-start = ((), (), s32[]{:S(2)}) async-start(), calls=%async_computation.17 | async-start | bytes 4423680 | tf_op jit(solution)/shard_map/all_gather | solution.py:772
  742.3 168.7 %all-reduce.4.cloned.1.call-start = ((), (), s32[]{:S(2)}) async-start(), calls=%async_computation.18 | async-start | bytes 2359296 | tf_op jit(solution)/shard_map/psum | solution.py:848
  769.9 3.3 copy-start.12
  773.3 54.3 %copy-start.7 = (f32[2,512,768]{2,1,0:T(8,128)S(1)}, f32[2,512,768]{2,1,0:T(8,128)}, u32[]{:S(2)}) copy-start(f32[2,512,768]{2,1,0:T(8,128)} %copy-done.6) | copy-start | bytes 9437188
Sparse Core Ops, SparseCore 0:
  9.6 24.8 all-gather.6
  36.0 37.4 all-gather.8
  75.1 37.4 all-gather.10
  156.7 37.9 all-gather.12
  309.1 26.6 reduce-scatter.10
  338.2 47.9 reduce-scatter.12
  388.8 47.9 reduce-scatter.14
  439.3 48.0 reduce-scatter.16
  505.9 222.7 all-reduce.5
  731.6 20.8 reduce-scatter.20
  755.0 40.3 reduce-scatter.18
  796.8 30.7 all-gather.14
  831.7 79.2 all-reduce.3

commit v3 on v2

--- a/solution.py
+++ b/solution.py
@@ -714,6 +714,254 @@
     )(low, count, q_ext, sums, dout, turn, k_ext, v_ext)
 
 
+def scatter_kernel(
+    chunks,
+    by_z,
+    part_ref,
+    dh_ref,
+    gw_ref,
+    norm_ref,
+    out_ref,
+    gw_all_ref,
+    norm_out_ref,
+    got_y,
+    got_z,
+    relay_y,
+    relay_z,
+    sent_y,
+    sent_z,
+    cross_out,
+    cross_in,
+    gw_got,
+    gw_mine,
+    gw_pair,
+    gw_final,
+    norm_got,
+    norm_sent,
+    send,
+    recv,
+    gw_send,
+    gw_recv,
+    norm_send,
+    norm_recv,
+    kept,
+):
+    me = lax.axis_index("seq")
+    shard = lax.axis_index("shard")
+    shards = gw_ref.shape[0]
+    half = lax.div(me, GROUPS)
+    y_near, z_near, partner = flip(me, 1), flip(me, 2), flip(me, 4)
+    corner = flip(y_near, 2)
+    barrier = pltpu.get_barrier_semaphore()
+    for device in (y_near, z_near, partner, corner):
+        pl.semaphore_signal(barrier, inc=1, device_id={"seq": device}, device_id_type=BY_MESH)
+    for step in range(1, shards):
+        pl.semaphore_signal(
+            barrier, inc=1, device_id={"shard": lax.rem(shard + step, shards)}, device_id_type=BY_MESH
+        )
+    pl.semaphore_wait(barrier, 3 + shards)
+
+    started = []
+
+    def go(source, target, sends, receives, slot, where):
+        copy = pltpu.make_async_remote_copy(
+            src_ref=source,
+            dst_ref=target,
+            send_sem=sends.at[slot],
+            recv_sem=receives.at[slot],
+            device_id=where,
+            device_id_type=BY_MESH,
+        )
+        copy.start()
+        started.append(copy)
+        return copy
+
+    rows = part_ref.shape[1] // chunks
+
+    def band(chunk):
+        return pl.ds(chunk * rows, rows)
+
+    def piece(device, far):
+        return flip(device, 4) if far else device
+
+    def slot(kind, far, chunk):
+        return (kind * 2 + (0 if far else 1)) * chunks + chunk
+
+    gw_one = [
+        go(
+            gw_ref.at[lax.rem(shard + step, shards)],
+            gw_got.at[step - 1],
+            gw_send,
+            gw_recv,
+            step - 1,
+            {"shard": lax.rem(shard + step, shards)},
+        )
+        for step in range(1, shards)
+    ]
+    pairs = [
+        {"shard": flip(shard, 1)},
+        {"shard": flip(shard, 2)},
+        {"seq": y_near},
+        {"seq": z_near},
+        {"seq": partner},
+    ]
+    norm_sent[0] = norm_ref[...]
+
+    from_corner, direct = {}, {}
+    for far in (True, False):
+        for chunk in range(chunks):
+            over_z = chunk < by_z
+            from_corner[far, chunk] = go(
+                part_ref.at[piece(corner, far), band(chunk)],
+                (relay_y if over_z else relay_z).at[0 if far else 1, chunk if over_z else chunk - by_z],
+                send,
+                recv,
+                slot(0, far, chunk),
+                {"seq": y_near if over_z else z_near},
+            )
+        for chunk in range(chunks):
+            over_z = chunk < by_z
+            near = y_near if over_z else z_near
+            direct[far, chunk] = go(
+                part_ref.at[piece(near, far), band(chunk)],
+                (got_y if over_z else got_z).at[0 if far else 1, band(chunk)],
+                send,
+                recv,
+                slot(1 if over_z else 2, far, chunk),
+                {"seq": near},
+            )
+
+    norm_copies = [go(norm_sent.at[0], norm_got.at[0], norm_send, norm_recv, 0, pairs[0])]
+    done_norm = 0
+
+    def norm_step(index):
+        norm_copies[index].wait_recv()
+        total = norm_sent[index] + norm_got[index]
+        if index + 1 < len(pairs):
+            norm_sent[index + 1] = total
+            norm_copies.append(
+                go(norm_sent.at[index + 1], norm_got.at[index + 1], norm_send, norm_recv, index + 1, pairs[index + 1])
+            )
+        else:
+            norm_out_ref[...] = total
+
+    relayed = {}
+
+    def relay(far, chunk):
+        over_z = chunk < by_z
+        target = z_near if over_z else y_near
+        index = chunk if over_z else chunk - by_z
+        which = 0 if far else 1
+        from_corner[far, chunk].wait_recv()
+        source = relay_y if over_z else relay_z
+        buffer = sent_y if over_z else sent_z
+        mine = part_ref[piece(target, far), band(chunk)].astype(F32)
+        buffer[which, index] = (source[which, index].astype(F32) + mine).astype(BF16)
+        relayed[far, chunk] = go(
+            buffer.at[which, index],
+            (got_z if over_z else got_y).at[which, band(chunk)],
+            send,
+            recv,
+            slot(2 if over_z else 1, far, chunk),
+            {"seq": target},
+        )
+
+    def total(far, chunk):
+        which = 0 if far else 1
+        direct[far, chunk].wait_recv()
+        relayed[far, chunk].wait_recv()
+        mine = part_ref[piece(me, far), band(chunk)].astype(F32)
+        return mine + got_y[which, band(chunk)].astype(F32) + got_z[which, band(chunk)].astype(F32)
+
+    for chunk in range(chunks):
+        relay(True, chunk)
+    norm_step(0)
+    for copy in gw_one:
+        copy.wait_recv()
+    summed = gw_ref[shard].astype(F32)
+    for step in range(1, shards):
+        summed = summed + gw_got[step - 1].astype(F32)
+    gw_mine[...] = summed.astype(BF16)
+    norm_step(1)
+    gw_two = go(gw_mine, gw_pair, gw_send, gw_recv, shards - 1, {"seq": partner})
+    crossing = []
+    for chunk in range(chunks):
+        cross_out[band(chunk)] = total(True, chunk).astype(BF16)
+        crossing.append(
+            go(cross_out.at[band(chunk)], cross_in.at[band(chunk)], send, recv, slot(3, True, chunk), {"seq": partner})
+        )
+        relay(False, chunk)
+    norm_step(2)
+    gw_two.wait_recv()
+    gw_final[...] = (gw_mine[...].astype(F32) + gw_pair[...].astype(F32)).astype(BF16)
+    norm_step(3)
+    group = lax.rem(me, GROUPS)
+    gw_three = [
+        go(gw_final, gw_all_ref.at[group], gw_send, gw_recv, shards + n, {"seq": device})
+        for n, device in enumerate((y_near, z_near, corner))
+    ]
+    keep = pltpu.make_async_copy(gw_final, gw_all_ref.at[group], kept.at[0])
+    keep.start()
+    for chunk in range(chunks):
+        out_ref[half, band(chunk)] = (total(False, chunk) + dh_ref[half, band(chunk)]).astype(BF16)
+    norm_step(4)
+    for chunk in range(chunks):
+        crossing[chunk].wait_recv()
+        other = 1 - half
+        out_ref[other, band(chunk)] = (cross_in[band(chunk)].astype(F32) + dh_ref[other, band(chunk)]).astype(BF16)
+    for copy in gw_three:
+        copy.wait_recv()
+    keep.wait()
+    for copy in started:
+        copy.wait_send()
+
+
+def scatter_gradients(partial, dh_one, grad_columns, norms, chunks=4, by_z=3):
+    _, rows, width = partial.shape
+    shards, depth, columns = grad_columns.shape
+    part = rows // chunks
+    vmem = pl.BlockSpec(memory_space=pltpu.VMEM)
+    dma = pltpu.SemaphoreType.DMA
+    return pl.pallas_call(
+        functools.partial(scatter_kernel, chunks, by_z),
+        out_shape=(
+            jax.ShapeDtypeStruct(dh_one.shape, BF16),
+            jax.ShapeDtypeStruct((GROUPS, depth, columns), BF16),
+            jax.ShapeDtypeStruct(norms.shape, F32),
+        ),
+        in_specs=[vmem] * 4,
+        out_specs=(vmem,) * 3,
+        scratch_shapes=[
+            pltpu.VMEM((2, rows, width), BF16),
+            pltpu.VMEM((2, rows, width), BF16),
+            pltpu.VMEM((2, by_z, part, width), BF16),
+            pltpu.VMEM((2, chunks - by_z, part, width), BF16),
+            pltpu.VMEM((2, by_z, part, width), BF16),
+            pltpu.VMEM((2, chunks - by_z, part, width), BF16),
+            pltpu.VMEM((rows, width), BF16),
+            pltpu.VMEM((rows, width), BF16),
+            pltpu.VMEM((shards - 1, depth, columns), BF16),
+            pltpu.VMEM((depth, columns), BF16),
+            pltpu.VMEM((depth, columns), BF16),
+            pltpu.VMEM((depth, columns), BF16),
+            pltpu.VMEM((5,) + norms.shape, F32),
+            pltpu.VMEM((5,) + norms.shape, F32),
+            dma((7 * chunks,)),
+            dma((7 * chunks,)),
+            dma((shards + 3,)),
+            dma((shards + 3,)),
+            dma((5,)),
+            dma((5,)),
+            dma((1,)),
+        ],
+        compiler_params=pltpu.CompilerParams(
+            collective_id=2, has_side_effects=True, vmem_limit_bytes=VMEM_LIMIT
+        ),
+        cost_estimate=pl.CostEstimate(flops=60 * 10**9, bytes_accessed=64 * 2**20, transcendentals=0),
+        name="scatter_gradients",
+    )(partial, dh_one, grad_columns, norms)
+
+
 def document_places(seg_row):
     length = seg_row.shape[0]
     ids = jnp.arange(LANES - HD, dtype=jnp.int32)[:, None]
@@ -772,7 +1020,6 @@
         return lax.all_gather(shard, "shard", axis=0, tiled=True)
 
     pieces, w_heads = gather_tokens(tokens, head_columns(w_qkv, me % GROUPS, held), shards)
-    full_qkv = gather(w_qkv)
     norms = gather(jnp.stack([ln1_gain, ln1_bias, ln2_gain, ln2_bias], axis=1)).astype(F32)
     gain_one, bias_one, gain_two, bias_two = (norms[:, n] for n in range(4))
     full_out, full_gate, full_up, full_down = (gather(w) for w in (w_out, w_gate, w_up, w_down))
@@ -822,31 +1069,43 @@
     grad_gate = jnp.einsum("scd,scf->df", x_low, d_gate, preferred_element_type=F32).astype(BF16)
     grad_up = jnp.einsum("scd,scf->df", x_low, d_up, preferred_element_type=F32).astype(BF16)
     grad_out = jnp.einsum("sci,sco->io", joined, d_attn, preferred_element_type=F32).astype(BF16)
-    grad_norms = jnp.stack([grad_gain_one, grad_bias_one, grad_gain_two, grad_bias_two], axis=1)
-
-    def reduce_shards(partial):
-        return lax.psum_scatter(partial, "shard", scatter_dimension=0, tiled=True)
-
-    d_joined, grad_down, grad_gate, grad_up, grad_out = lax.optimization_barrier(
-        (d_joined, grad_down, grad_gate, grad_up, grad_out)
-    )
-    owned = [reduce_shards(g) for g in (grad_out, grad_gate, grad_up, grad_down)]
+    norms_part = jnp.stack([grad_gain_one, grad_bias_one, grad_gain_two, grad_bias_two])
+    depth = model_width // shards
+    ff_blocks = grad_gate.shape[1] // model_width
+
+    def by_shard(grad):
+        split = grad.reshape(shards, -1, grad.shape[1] // model_width, model_width)
+        return jnp.transpose(split, (0, 2, 1, 3)).reshape(shards, -1, model_width)
+
+    packed = jnp.concatenate([by_shard(g) for g in (grad_gate, grad_up, grad_down, grad_out)], axis=1)
+    d_joined, packed = lax.optimization_barrier((d_joined, packed))
+    owned = lax.psum_scatter(
+        packed.reshape(-1, model_width), ("shard", "seq"), scatter_dimension=0, tiled=True
+    )
 
     dout = exchange(by_group(d_joined))
     d_heads = attend_back_heads(bounds, q_ext, k_ext, v_ext, sums, dout, turn)
-    d_heads, *owned = lax.optimization_barrier((d_heads, *owned))
-    summed = [lax.psum(g, "seq") for g in owned]
-    d_taken = exchange(d_heads)
-    d_taken, *summed = lax.optimization_barrier((d_taken, *summed))
-    d_split = d_taken.reshape(seq_count, GROUPS, row_count, 3, held * HD)
-    d_qkv = jnp.transpose(d_split, (0, 2, 3, 1, 4)).reshape(seq_count, row_count, 3 * model_width)
-    grad_qkv = jnp.einsum("scd,sce->de", tokens, d_qkv, preferred_element_type=F32).astype(BF16)
-    d_tokens = dh_one + jnp.einsum("sce,de->scd", d_qkv, full_qkv, preferred_element_type=F32)
-    input_grad = d_tokens.astype(BF16)
-
-    grad_out, grad_gate, grad_up, grad_down = (g.astype(F32) for g in summed)
-    grad_qkv = lax.psum(reduce_shards(grad_qkv), "seq").astype(F32)
-    norm_sums = lax.psum(reduce_shards(grad_norms), "seq")
+    w_own = w_heads.reshape(model_width, -1, LANES)[:, :, :HD].reshape(model_width, -1)
+    partial = jnp.einsum("prc,dc->prd", d_heads, w_own, preferred_element_type=F32).astype(BF16)
+    grad_columns = jnp.einsum("prd,prc->dc", pieces, d_heads, preferred_element_type=F32).astype(BF16)
+    partial, grad_columns, owned = lax.optimization_barrier((partial, grad_columns, owned))
+    shared = lax.all_gather(owned, "seq", axis=0, tiled=True)
+    input_grad, columns, norm_sums = scatter_gradients(
+        partial, dh_one, grad_columns.reshape(shards, depth, -1), norms_part
+    )
+    grad_qkv = jnp.transpose(columns.reshape(GROUPS, depth, 3, held * HD), (1, 2, 0, 3))
+    grad_qkv = grad_qkv.reshape(depth, 3 * model_width).astype(F32)
+
+    def taken(start, blocks):
+        rows = shared[start : start + blocks * depth].reshape(blocks, depth, model_width)
+        return jnp.transpose(rows, (1, 0, 2)).reshape(depth, blocks * model_width).astype(F32)
+
+    ff_rows = ff_blocks * depth
+    grad_gate, grad_up = taken(0, ff_blocks), taken(ff_rows, ff_blocks)
+    grad_down = shared[2 * ff_rows : 3 * ff_rows].astype(F32)
+    grad_out = taken(3 * ff_rows, 1)
+    shard = lax.axis_index("shard")
+    norm_sums = lax.dynamic_slice_in_dim(norm_sums, shard * depth, depth, 1)
     return (
         output,
         input_grad,
@@ -855,10 +1114,10 @@
         grad_gate,
         grad_up,
         grad_down,
-        norm_sums[:, 0],
-        norm_sums[:, 1],
-        norm_sums[:, 2],
-        norm_sums[:, 3],
+        norm_sums[0],
+        norm_sums[1],
+        norm_sums[2],
+        norm_sums[3],
     )
 
 
@@ -891,5 +1150,5 @@
         P("shard"),
         P("shard"),
     )
-    body = functools.partial(local_heads, mesh.shape["shard"]) if mesh.shape["seq"] == SEQ_SIZE else local
+    body = functools.partial(local_heads, mesh.shape["shard"]) if (mesh.shape["seq"], mesh.shape["shard"]) == (SEQ_SIZE, GROUPS) else local
     return jax.shard_map(body, mesh=mesh, in_specs=in_specs, out_specs=out_specs, check_vma=False)

time: 930 us -> 681 us (0.73)
  waiting for transfers between devices: 423 us -> 58.8 us
  Pallas kernels: 232 us -> 365 us
  blocking collectives: 61.9 us -> 5.19 us
  local copies, waits for them, and re-layouts: 41.7 us -> 69 us
    psum x2 -> x0, waiting for transfers between devices: 301 us -> none  [the longest x1 226 us: local_heads(): summed = [lax.psum(g, 'seq') for g in owned]]
    pallas_call x0 -> x1, Pallas kernels: none -> 132 us  [scatter_gradients(): pl.pallas_call(functools.partial(scatter_kernel, chunks, by_z), out_shape...]
    all_to_all x1 -> x0, blocking collectives: 41.6 us -> none  [exchange(): return lax.all_to_all(blocks, 'seq', 0, 0, tiled=True)]
    unnamed x15 -> x6, waiting for transfers between devices: 36.5 us -> 2.64 us
    reshape x0 -> x5, local copies, waits for them, and re-layouts: none -> 31 us  [the longest x4 28 us: by_shard(): split = grad.reshape(shards, -1, grad.shape[1] // model_width, model_width)]
    all_gather x5 -> x4, waiting for transfers between devices: 29.6 us -> 0.03 us  [gather(): return lax.all_gather(shard, 'shard', axis=0, tiled=True)]
    all_to_all x2, waiting for transfers between devices: 28.9 us -> 51.3 us  [exchange(): return lax.all_to_all(blocks, 'seq', 0, 0, tiled=True)]
    reduce_scatter x4 -> x1, waiting for transfers between devices: 27.2 us -> 4.82 us  [local_heads(): lax.psum_scatter(packed.reshape(-1, model_width), ('shard', 'seq'), scatt...]
  transfers between devices with their start and end apart: 15 -> 8, of which waited for: 7 -> 3; matrix products, arithmetic and copies ran while one was open for 8% -> 12% of each run, Pallas kernels for 25% -> 54%
where the time goes in v3:
time: 681 us; the launch traced here: 670 us
  Pallas kernels  365 us (54%)
  matrix products  119 us (17%)
  local copies, waits for them, and re-layouts  69 us (10%)
  waiting for transfers between devices  58.8 us (9%)
  other arithmetic  25.3 us (4%)
  between operations  15.1 us (2%)
  starting transfers between devices  13.1 us (2%)
    pallas_call x1, Pallas kernels, scatter_gradients(): pl.pallas_call(functools.partial(scatter_kernel, chunks, by_z), out_shape...  132 us
    pallas_call x1, Pallas kernels, attend_back_heads(): pl.pallas_call(functools.partial(attend_back_kernel, window, align), out_...  102 us
    pallas_call x1, Pallas kernels, gather_tokens(): pl.pallas_call(functools.partial(gather_kernel, chunks, by_z), out_shape=...  68.8 us
    all_to_all x2, waiting for transfers between devices, exchange(): return lax.all_to_all(blocks, 'seq', 0, 0, tiled=True)  51.3 us
    pallas_call x1, Pallas kernels, attend_heads(): pl.pallas_call(functools.partial(attend_kernel, window, align), out_shape...  40.5 us
    reshape x4, local copies, waits for them, and re-layouts, by_shard(): split = grad.reshape(shards, -1, grad.shape[1] // model_width, model_width)  28 us
    pallas_call x1, Pallas kernels, project_heads(): pl.pallas_call(project_kernel, out_shape=(head_shape, head_shape, head_sh...  21 us
    dot_general x1, matrix products, local_heads(): jnp.einsum('scd,fd->scf', dm_low, full_down, preferred_element_type=F32)  19.4 us
  transfers between devices with their start and end apart: 8, of which 3 were waited for; matrix products, arithmetic and copies ran while one was open for 12% of the time, Pallas kernels for 54%

profile of v3, /device:TPU:20, one launch (start us, length us, event | category | flops | bytes accessed | tf_op | source)
XLA Modules:
  0.0 670.3 jit_solution(13332409598230109539)
XLA Ops:
  7.2 0.7 all-gather.7.cloned.1.call-update
  8.0 0.7 all-gather.9.cloned.1.call-update
  8.7 0.7 all-gather.11.cloned.1.call-update
  9.4 1.4 fusion.33
  11.0 0.6 broadcast_in_dim_tile.3.freq_ref
  11.6 0.6 copy.89
  12.5 1.0 copy.115.w_ref
  13.4 68.8 %gather_tokens.1 = (bf16[8,512,768]{2,1,0:T(8,128)(2,1)}, bf16[4,192,1152]{2,1,0:T(8,128)(2,1)}) custom-call(bf16[2,512,768]{2,1,0:T(8,128)(2,1)} %tok_ref.1, bf16[192,1152]{1,0:T(8,128)(2,1)} %copy.115.w_ref), custom_call_target="tpu_custom_call" | custom-call | tf_op jit(solution)/shard_map/gather_tokens/pallas_call | solution.py:443
  83.0 0.5 subtract_minimum_fusion
  83.5 0.6 subtract_convert_fusion.place_ref
  84.1 21.0 %project_heads.1 = (bf16[3,4096,128]{2,1,0:T(8,128)(2,1)}, bf16[3,4096,128]{2,1,0:T(8,128)(2,1)}, bf16[3,4096,128]{2,1,0:T(8,128)(2,1)}, f32[4096,128]{1,0:T(8,128)}) custom-call(f32[8,1,512]{2,1,0:T(1,128)} %bitcast.143, f32[8,1,512]{2,1,0:T(1,128)} %subtract_convert_fusion.place_ref, f32[1,128]{1,0:T(1,128)} %broadcast_in_dim_tile.3.freq_ref, ...), custom_call_target="tpu_custom_call" | custom-call | flops 7247757312 | bytes 17825792 | tf_op jit(solution)/shard_map/project_heads/pallas_call | solution.py:501
  105.2 40.5 %attend_heads.1 = (f32[3,4096,128]{2,1,0:T(8,128)}, bf16[8,512,192]{2,1,0:T(8,128)(2,1)}) custom-call(s32[8]{0:T(128)} %get-tuple-element.80.low_ref, s32[8]{0:T(128)} %get-tuple-element.81.count_ref, bf16[3,4096,128]{2,1,0:T(8,128)(2,1)} %get-tuple-element.29.q_ref, bf16[3,4096,128]{2,1,0:T(8,128)(2,1)} %get-tuple-element.30.k_ref, ...), custom_call_target="tpu_custom_call" | custom-call | flops 12884901888 | bytes 15728640 | tf_op jit(solution)/shard_map/attend_heads/pallas_call | solution.py:563
  145.6 3.9 copy.91
  149.5 5.1 all-to-all-start
  154.6 0.6 all-gather.13.cloned.1.call-update
  155.3 5.2 all-gather
  160.7 25.7 %all-to-all-done = bf16[8,512,192]{1,2,0:T(8,128)(2,1)S(1)} async-done(((bf16[8,512,192]{1,2,0:T(8,128)(2,1)}), bf16[8,512,192]{1,2,0:T(8,128)(2,1)S(1)}, u32[]{:S(2)}, u32[]{:S(2)}) %all-to-all-start) | async-done | bytes 1572896 | tf_op jit(solution)/shard_map/all_to_all | solution.py:986
  186.4 1.1 copy-done.5
  187.6 3.8 fusion.36
  191.8 1.7 fusion.21
  193.5 10.3 %fusion.11 = f32[2,512,3072]{2,1,0:T(8,128)} fusion(bf16[2,512,768]{2,1,0:T(8,128)(2,1)} %fusion.21, bf16[768,3072]{1,0:T(8,128)(2,1)} %all-gather.9.cloned.1.call-done), kind=kOutput, calls=%fused_computation.22 | convolution fusion | flops 4831838208 | bytes 18874368 | tf_op jit(solution)/shard_map/scd,df->scf/dot_general | solution.py:1040
  203.8 13.4 %multiply_convert_fusion.2 = (bf16[2,512,3072]{2,1,0:T(8,128)(2,1)}, f32[2,512,3072]{2,1,0:T(8,128)}) fusion(f32[2,512,3072]{2,1,0:T(8,128)} %fusion.11, bf16[2,512,768]{2,1,0:T(8,128)(2,1)} %fusion.21, bf16[768,3072]{1,0:T(8,128)(2,1)} %all-gather.11.cloned.1.call-done), kind=kOutput, calls=%fused_computation.3 | convolution fusion | flops 4850712576 | bytes 37748736 | tf_op jit(solution)/shard_map/scd,df->scf/dot_general | solution.py:1041
  217.2 8.7 %fusion.37 = (f32[2,512]{1,0:T(2,128)S(1)}, f32[2,512,768]{2,1,0:T(8,128)S(1)}) fusion(bf16[2,512,3072]{2,1,0:T(8,128)(2,1)} %get-tuple-element.86, bf16[3072,768]{1,0:T(8,128)(2,1)} %all-gather.13.cloned.1.call-done, f32[768]{0:T(1024)S(1)} %get-tuple-element.55, f32[768]{0:T(1024)S(1)} %get-tuple-element.56, f32[2,512]{1,0:T(2,128)S(1)} %add_rsqrt_fusion.1, ...), kind=kOutput, calls=%fused_computation.109 | convolution fusion | flops 4836555776 | bytes 17319936 | tf_op jit(solution)/shard_map/scf,fd->scd/dot_general | solution.py:1045
  226.0 0.5 multiply_reduce_fusion.2
  226.5 2.0 copy-done.2
  228.5 2.2 fusion.19
  230.7 2.2 fusion.28
  232.9 7.0 %bitcast_convert_fusion = bf16[3072,768]{1,0:T(8,128)(2,1)} fusion(bf16[2,512,3072]{2,1,0:T(8,128)(2,1)S(1)} %bitcast.149, bf16[2,512,768]{2,1,0:T(8,128)(2,1)S(1)} %get-tuple-element.70), kind=kOutput, calls=%fused_computation.6 | convolution fusion | flops 4834197504 | bytes 12582912 | tf_op jit(solution)/shard_map/scf,scd->fd/dot_general | solution.py:1068
  239.9 19.4 %multiply_convert_fusion.1 = (bf16[2,512,3072]{2,1,0:T(8,128)(2,1)}, bf16[2,512,3072]{2,1,0:T(8,128)(2,1)}) fusion(f32[2,512,3072]{2,1,0:T(8,128)} %fusion.11, f32[2,512,3072]{2,1,0:T(8,128)} %get-tuple-element.87, bf16[2,512,768]{2,1,0:T(8,128)(2,1)} %copy-done.9, bf16[3072,768]{1,0:T(8,128)(2,1)} %all-gather.13.cloned.1.call-done), kind=kOutput, calls=%fused_computation.2 | convolution fusion | flops 4872732672 | bytes 44040192 | tf_op jit(solution)/shard_map/scd,fd->scf/dot_general | solution.py:1054
  259.3 9.3 %bitcast_convert_fusion.2 = bf16[768,3072]{1,0:T(8,128)(2,1)} fusion(bf16[2,512,768]{2,1,0:T(8,128)(2,1)} %fusion.21, bf16[2,512,3072]{2,1,0:T(8,128)(2,1)} %get-tuple-element.65), kind=kOutput, calls=%fused_computation.8 | convolution fusion | flops 4834197504 | bytes 12582912 | tf_op jit(solution)/shard_map/scd,scf->df/dot_general | solution.py:1069
  268.6 6.9 %bitcast_convert_fusion.1 = bf16[768,3072]{1,0:T(8,128)(2,1)} fusion(bf16[2,512,768]{2,1,0:T(8,128)(2,1)S(1)} %copy-done.8, bf16[2,512,3072]{2,1,0:T(8,128)(2,1)S(1)} %copy-done.19), kind=kOutput, calls=%fused_computation.7 | convolution fusion | flops 4834197504 | bytes 12582912 | tf_op jit(solution)/shard_map/scd,scf->df/dot_general | solution.py:1070
  275.5 9.7 %reshape.182 = bf16[4,192,4,768]{3,2,1,0:T(4,128)(2,1)} reshape(bf16[768,3072]{1,0:T(8,128)(2,1)} %bitcast_convert_fusion.1) | data formatting | bytes 9437184 | tf_op jit(solution)/shard_map/reshape | solution.py:1077
  285.3 5.3 copy.97
  290.6 9.7 %reshape.180 = bf16[4,192,4,768]{3,2,1,0:T(4,128)(2,1)} reshape(bf16[768,3072]{1,0:T(8,128)(2,1)} %bitcast_convert_fusion.2) | data formatting | bytes 9437184 | tf_op jit(solution)/shard_map/reshape | solution.py:1077
  300.3 3.2 copy.95
  303.5 10.1 %fusion.5 = f32[2,512,768]{2,1,0:T(8,128)} fusion(bf16[2,512,3072]{2,1,0:T(8,128)(2,1)} %get-tuple-element.66, bf16[768,3072]{1,0:T(8,128)(2,1)} %all-gather.11.cloned.1.call-done), kind=kOutput, calls=%fused_computation.16 | convolution fusion | flops 4831838208 | bytes 14155776 | tf_op jit(solution)/shard_map/scf,df->scd/dot_general | solution.py:1060
  313.6 10.8 %multiply_reduce_fusion = (f32[768]{0:T(1024)S(1)}, f32[2,512]{1,0:T(2,128)S(1)}, f32[2,512]{1,0:T(2,128)S(1)}, f32[768]{0:T(1024)S(1)}, f32[2,512,768]{2,1,0:T(8,128)S(1)}) fusion(f32[2,512,768]{2,1,0:T(8,128)S(1)} %get-tuple-element.85, f32[2,512]{1,0:T(2,128)S(1)} %add_rsqrt_fusion.1, f32[2,512]{1,0:T(2,128)S(1)} %broadcast_multiply_fusion.6, ...), kind=kOutput, calls=%fused_computation.32 | convolution fusion | flops 4846776320 | bytes 25210880 | tf_op jit(solution)/shard_map/scf,df->scd/dot_general | solution.py:1059
  324.4 1.0 subtract_multiply_fusion.dh_ref
  325.5 1.4 bitcast_convert_fusion.3
  327.2 1.8 slice-done.2
  329.3 6.9 %pad_maximum_fusion = bf16[4,2496,768]{2,1,0:T(8,128)(2,1)} fusion(bf16[4,192,768]{2,1,0:T(8,128)(2,1)S(1)} %bitcast.135, bf16[4,768,768]{2,1,0:T(8,128)(2,1)S(1)} %bitcast.126, bf16[4,768,768]{2,1,0:T(8,128)(2,1)S(1)} %bitcast.118, bf16[4,768,768]{2,1,0:T(8,128)(2,1)S(1)} %bitcast.119), kind=kLoop, calls=%fused_computation | loop fusion | flops 61341696 | bytes 30670848 | tf_op jit(solution)/shard_map/concatenate | solution.py:1080
  336.3 1.4 convolution_convert_fusion.1
  338.5 2.3 copy.99
  340.8 7.8 %all-to-all-start.1 = ((bf16[8,512,192]{1,2,0:T(8,128)(2,1)}), bf16[8,512,192]{1,2,0:T(8,128)(2,1)}, u32[]{:S(2)}, u32[]{:S(2)}) async-start(bf16[8,512,192]{1,2,0:T(8,128)(2,1)} %copy.99), calls=%async_computation.1 | async-start | bytes 3145728 | tf_op jit(solution)/shard_map/all_to_all | solution.py:986
  348.6 4.3 copy.101
  353.0 3.0 reshape.185
  356.0 25.6 %all-to-all-done.1 = bf16[8,512,192]{1,2,0:T(8,128)(2,1)} async-done(((bf16[8,512,192]{1,2,0:T(8,128)(2,1)}), bf16[8,512,192]{1,2,0:T(8,128)(2,1)}, u32[]{:S(2)}, u32[]{:S(2)}) %all-to-all-start.1) | async-done | bytes 1572896 | tf_op jit(solution)/shard_map/all_to_all | solution.py:986
  381.6 3.8 copy.100.dout_ref
  385.4 102.1 %attend_back_heads.1 = bf16[8,512,576]{2,1,0:T(8,128)(2,1)} custom-call(s32[8]{0:T(128)} %get-tuple-element.57.low_ref, s32[8]{0:T(128)} %get-tuple-element.58.count_ref, bf16[3,4096,128]{2,1,0:T(8,128)(2,1)} %get-tuple-element.29.q_ref, f32[3,4096,128]{2,1,0:T(8,128)} %get-tuple-element.33.sum_ref, bf16[8,512,192]{2,1,0:T(8,128)(2,1)} %copy.100.dout_ref, ...), custom_call_target="tpu_custom_call" | custom-call | flops 32212254720 | bytes 31457280 | tf_op jit(solution)/shard_map/attend_back_heads/pallas_call | solution.py:684
  487.5 9.8 %convolution_convert_fusion.part_ref = bf16[8,512,768]{2,1,0:T(8,128)(2,1)} fusion(bf16[8,512,576]{2,1,0:T(8,128)(2,1)} %attend_back_heads.1, bf16[768,576,1]{0,1,2:T(8,128)(2,1)S(1)} %bitcast.127), kind=kOutput, calls=%fused_computation.27 | convolution fusion | flops 3627024384 | bytes 11894784 | tf_op jit(solution)/shard_map/prc,dc->prd/dot_general | solution.py:1089
  497.3 6.9 %bitcast_convert_fusion.4 = bf16[768,576]{0,1:T(8,128)(2,1)S(1)} fusion(bf16[8,512,768]{2,1,0:T(8,128)(2,1)} %get-tuple-element.27.x_ref, bf16[8,512,576]{2,1,0:T(8,128)(2,1)S(1)} %copy-done.20), kind=kOutput, calls=%fused_computation.50 | convolution fusion | flops 3624321024 | bytes 11894784 | tf_op jit(solution)/shard_map/prd,prc->dc/dot_general | solution.py:1090
  504.2 4.8 reduce-scatter.2.cloned.1.call-done
  509.1 0.6 pad_maximum_fusion.3.norm_ref
  509.8 1.3 copy.104
  511.1 132.3 %scatter_gradients.1 = (bf16[2,512,768]{2,1,0:T(8,128)(2,1)}, bf16[4,192,576]{2,1,0:T(8,128)(2,1)}, f32[4,768]{1,0:T(4,128)}) custom-call(bf16[8,512,768]{2,1,0:T(8,128)(2,1)} %convolution_convert_fusion.part_ref, f32[2,512,768]{2,1,0:T(8,128)} %copy-done.4, bf16[4,192,576]{2,1,0:T(8,128)(2,1)} %bitcast.136, f32[4,768]{1,0:T(4,128)} %pad_maximum_fusion.3.norm_ref), custom_call_target="tpu_custom_call" | custom-call | flops 60000002048 | bytes 67108864 | tf_op jit(solution)/shard_map/scatter_gradients/pallas_call | solution.py:925
  643.3 1.5 copy.105
  644.9 2.5 copy.106
  647.4 3.7 reshape.189
  651.1 1.5 fusion.35
  652.6 3.7 slice_convert_fusion
  656.5 1.7 copy.117
  658.4 1.7 copy.116
  660.0 1.8 slice_convert_fusion.1
  661.8 1.1 copy.119
  (103 shorter events, 3.9 us)
Async XLA Ops:
  7.2 5.1 copy-start.13
  7.2 4.5 copy-start.10
  7.2 153.5 %all-gather.7.cloned.1.call-start = ((), (), s32[]{:S(2)}) async-start(), calls=%async_computation.3 | async-start | bytes 1474560 | tf_op jit(solution)/shard_map/all_gather | solution.py:1020
  7.9 185.6 %all-gather.9.cloned.1.call-start = ((), (), s32[]{:S(2)}) async-start(), calls=%async_computation.4 | async-start | bytes 5898240 | tf_op jit(solution)/shard_map/all_gather | solution.py:1020
  8.7 195.1 %all-gather.11.cloned.1.call-start = ((), (), s32[]{:S(2)}) async-start(), calls=%async_computation.5 | async-start | bytes 5898240 | tf_op jit(solution)/shard_map/all_gather | solution.py:1020
  145.6 9.6 %copy-start.15 = (bf16[192]{0:T(256)(128)(2,1)S(1)}, bf16[192]{0:T(256)(128)(2,1)}, u32[]{:S(2)}) copy-start(bf16[192]{0:T(256)(128)(2,1)} %param.22) | copy-start | bytes 1156
  145.6 9.6 %copy-start.16 = (bf16[192]{0:T(256)(128)(2,1)S(1)}, bf16[192]{0:T(256)(128)(2,1)}, u32[]{:S(2)}) copy-start(bf16[192]{0:T(256)(128)(2,1)} %param.23) | copy-start | bytes 1156
  145.6 9.7 %copy-start.17 = (bf16[192]{0:T(256)(128)(2,1)S(1)}, bf16[192]{0:T(256)(128)(2,1)}, u32[]{:S(2)}) copy-start(bf16[192]{0:T(256)(128)(2,1)} %param.24) | copy-start | bytes 1156
  145.6 9.7 %copy-start.18 = (bf16[192]{0:T(256)(128)(2,1)S(1)}, bf16[192]{0:T(256)(128)(2,1)}, u32[]{:S(2)}) copy-start(bf16[192]{0:T(256)(128)(2,1)} %param.25) | copy-start | bytes 1156
  149.5 36.9 %all-to-all-start = ((bf16[8,512,192]{1,2,0:T(8,128)(2,1)}), bf16[8,512,192]{1,2,0:T(8,128)(2,1)S(1)}, u32[]{:S(2)}, u32[]{:S(2)}) async-start(bf16[8,512,192]{1,2,0:T(8,128)(2,1)} %copy.91), calls=%async_computation | async-start | bytes 3145728 | tf_op jit(solution)/shard_map/all_to_all | solution.py:986
  154.6 62.6 %all-gather.13.cloned.1.call-start = ((), (), s32[]{:S(2)}) async-start(), calls=%async_computation.6 | async-start | bytes 5898240 | tf_op jit(solution)/shard_map/all_gather | solution.py:1020
  155.2 353.9 %reduce-scatter.2.cloned.1.call-start = ((), (), s32[]{:S(2)}) async-start(), calls=%async_computation.7 | async-start | bytes 15814656 | tf_op jit(solution)/shard_map/reduce_scatter | solution.py:1082
  186.4 1.1 copy-start.5
  226.0 4.8 copy-start
  226.0 2.5 copy-start.2
  228.5 4.4 slice-start.5
  230.7 2.2 slice-start.6
  232.9 7.0 %copy-start.9 = (bf16[2,512,768]{2,1,0:T(8,128)(2,1)}, bf16[2,512,768]{2,1,0:T(8,128)(2,1)S(1)}, u32[]{:S(2)}) copy-start(bf16[2,512,768]{2,1,0:T(8,128)(2,1)S(1)} %get-tuple-element.70) | copy-start | bytes 4718596
  259.3 9.3 %copy-start.8 = (bf16[2,512,768]{2,1,0:T(8,128)(2,1)S(1)}, bf16[2,512,768]{2,1,0:T(8,128)(2,1)}, u32[]{:S(2)}) copy-start(bf16[2,512,768]{2,1,0:T(8,128)(2,1)} %fusion.21) | copy-start | bytes 4718596
  259.3 9.3 %copy-start.19 = (bf16[2,512,3072]{2,1,0:T(8,128)(2,1)S(1)}, bf16[2,512,3072]{2,1,0:T(8,128)(2,1)}, u32[]{:S(2)}) copy-start(bf16[2,512,3072]{2,1,0:T(8,128)(2,1)} %get-tuple-element.66) | copy-start | bytes 18874372
  303.5 10.1 %copy-start.1 = (f32[2,512,768]{2,1,0:T(8,128)S(1)}, f32[2,512,768]{2,1,0:T(8,128)}, u32[]{:S(2)}) copy-start(f32[2,512,768]{2,1,0:T(8,128)} %copy-done) | copy-start | bytes 9437188
  303.5 10.1 %copy-start.3 = (bf16[2,512,768]{2,1,0:T(8,128)(2,1)S(1)}, bf16[2,512,768]{2,1,0:T(8,128)(2,1)}, u32[]{:S(2)}) copy-start(bf16[2,512,768]{2,1,0:T(8,128)(2,1)} %param.16) | copy-start | bytes 4718596
  313.6 11.8 %copy-start.6 = (bf16[8,512,192]{1,2,0:T(8,128)(2,1)S(1)}, bf16[8,512,192]{1,2,0:T(8,128)(2,1)}, u32[]{:S(2)}) copy-start(bf16[8,512,192]{1,2,0:T(8,128)(2,1)} %copy-done.5) | copy-start | bytes 4718596
  324.4 2.8 slice-start
  324.4 4.6 slice-start.2
  325.4 10.8 %copy-start.4 = (f32[2,512,768]{2,1,0:T(8,128)}, f32[2,512,768]{2,1,0:T(8,128)S(1)}, u32[]{:S(2)}) copy-start(f32[2,512,768]{2,1,0:T(8,128)S(1)} %subtract_multiply_fusion.dh_ref) | copy-start | bytes 9437188
  325.4 3.7 slice-start.1
  325.4 3.9 slice-start.3
  329.3 7.0 %copy-start.14 = (bf16[768,768]{1,0:T(8,128)(2,1)S(1)}, bf16[768,768]{1,0:T(8,128)(2,1)}, u32[]{:S(2)}) copy-start(bf16[768,768]{1,0:T(8,128)(2,1)} %all-gather.7.cloned.1.call-done) | copy-start | bytes 3538948
  340.8 40.8 %all-to-all-start.1 = ((bf16[8,512,192]{1,2,0:T(8,128)(2,1)}), bf16[8,512,192]{1,2,0:T(8,128)(2,1)}, u32[]{:S(2)}, u32[]{:S(2)}) async-start(bf16[8,512,192]{1,2,0:T(8,128)(2,1)} %copy.99), calls=%async_computation.1 | async-start | bytes 3145728 | tf_op jit(solution)/shard_map/all_to_all | solution.py:986
  348.6 304.0 %all-gather.15.cloned.1.call-start = ((), (), s32[]{:S(2)}) async-start(), calls=%async_computation.8 | async-start | bytes 4313088 | tf_op jit(solution)/shard_map/all_gather | solution.py:1092
  385.4 102.1 %slice-start.4 = ((bf16[768,9,128]{0,2,1:T(8,128)(2,1)}), bf16[768,9,64]{0,2,1:T(8,128)(2,1)S(1)}, s32[]{:S(2)}) async-start(bf16[768,9,128]{0,2,1:T(8,128)(2,1)} %reshape.185), calls=%async_computation.13 | async-start | bytes 1769472 | tf_op jit(solution)/shard_map/slice | solution.py:1088
  487.5 9.8 %copy-start.20 = (bf16[8,512,576]{2,1,0:T(8,128)(2,1)S(1)}, bf16[8,512,576]{2,1,0:T(8,128)(2,1)}, u32[]{:S(2)}) copy-start(bf16[8,512,576]{2,1,0:T(8,128)(2,1)} %attend_back_heads.1) | copy-start | bytes 14155780
  497.3 11.8 %copy-start.12 = (f32[768]{0:T(1024)S(1)}, f32[768]{0:T(1024)}, u32[]{:S(2)}) copy-start(f32[768]{0:T(1024)} %get-tuple-element.45) | copy-start | bytes 9220
  497.3 11.8 %copy-start.11 = (f32[768]{0:T(1024)S(1)}, f32[768]{0:T(1024)}, u32[]{:S(2)}) copy-start(f32[768]{0:T(1024)} %get-tuple-element.50) | copy-start | bytes 9220
  658.3 3.5 copy-start.7
Sparse Core Ops, SparseCore 0:
  9.6 24.8 all-gather.6
  36.0 37.4 all-gather.8
  75.1 37.4 all-gather.10
  156.7 37.6 all-gather.12
  337.8 171.1 reduce-scatter.1
  511.1 111.2 all-gather.14

commit v4 on v3

--- a/solution.py
+++ b/solution.py
@@ -339,6 +339,7 @@
 F32 = jnp.float32
 BF16 = jnp.bfloat16
 VMEM_LIMIT = 60 * 1024 * 1024
+FEED_LIMIT = 63 * 1024 * 1024
 BY_MESH = pl.DeviceIdType.MESH
 BY_LANES = (((1,), (1,)), ((), ()))
 
@@ -962,24 +963,268 @@
     )(partial, dh_one, grad_columns, norms)
 
 
+def feed_forward_kernel(
+    tokens_ref,
+    joined_ref,
+    cot_ref,
+    out_hbm,
+    gate_hbm,
+    up_hbm,
+    down_hbm,
+    norms_ref,
+    output_ref,
+    dout_ref,
+    dh_ref,
+    norm_sums_ref,
+    packed_ref,
+    w_out,
+    w_gate,
+    w_up,
+    w_down,
+    flow,
+    hat_one,
+    inverse_one,
+    x_low,
+    x_turned,
+    dm_low,
+    gate_kept,
+    up_kept,
+    d_gate,
+    d_up,
+    hidden_kept,
+    staged,
+    loads,
+    stores,
+):
+    seqs, rows, width = dh_ref.shape
+    shards = packed_ref.shape[0]
+    depth = width // shards
+    blocks = gate_hbm.shape[1] // width
+    weights = ((out_hbm, w_out), (gate_hbm, w_gate), (up_hbm, w_up), (down_hbm, w_down))
+    fetch = [pltpu.make_async_copy(src, dst, loads.at[n]) for n, (src, dst) in enumerate(weights)]
+    tokens_in = pltpu.make_async_copy(tokens_ref, flow, loads.at[4])
+    tokens_in.start()
+    for copy in fetch:
+        copy.start()
+    gain_one, bias_one, gain_two, bias_two = (norms_ref[n : n + 1, :] for n in range(4))
+
+    def mean(value):
+        return jnp.sum(value, axis=-1, keepdims=True) * (1.0 / width)
+
+    fetch[0].wait()
+    tokens_in.wait()
+    for seq in range(seqs):
+        h_one = flow[seq].astype(F32)
+        for group in range(GROUPS):
+            h_one = h_one + jnp.dot(
+                joined_ref[seq * GROUPS + group],
+                w_out[group * depth : (group + 1) * depth, :],
+                preferred_element_type=F32,
+            )
+        centered = h_one - mean(h_one)
+        inverse = lax.rsqrt(mean(centered * centered) + EPS)
+        normed = centered * inverse
+        hat_one[seq] = normed
+        inverse_one[seq] = inverse
+        x_one = normed * gain_one + bias_one
+        dh_ref[seq] = x_one
+        x_low[seq] = x_one.astype(BF16)
+        x_turned[:, seq * rows : (seq + 1) * rows] = jnp.transpose(x_one).astype(BF16)
+    cot_in = pltpu.make_async_copy(cot_ref, flow, loads.at[4])
+    cot_in.start()
+    for copy in fetch[1:]:
+        copy.wait()
+
+    def forward(block, carry):
+        at = pl.ds(pl.multiple_of(block * width, width), width)
+        for seq in range(seqs):
+            gate = jnp.dot(x_low[seq], w_gate[:, at], preferred_element_type=F32)
+            up = jnp.dot(x_low[seq], w_up[:, at], preferred_element_type=F32)
+            gate_kept[block, seq] = gate.astype(gate_kept.dtype)
+            up_kept[block, seq] = up.astype(up_kept.dtype)
+            hidden = (gate * jax.nn.sigmoid(gate) * up).astype(BF16)
+            dh_ref[seq] += jnp.dot(hidden, w_down[at, :], preferred_element_type=F32)
+        return carry
+
+    lax.fori_loop(0, blocks, forward, 0)
+
+    cot_in.wait()
+    gain_two_sum = jnp.zeros((1, width), F32)
+    bias_two_sum = jnp.zeros((1, width), F32)
+    for seq in range(seqs):
+        h_two = dh_ref[seq]
+        centered = h_two - mean(h_two)
+        inverse = lax.rsqrt(mean(centered * centered) + EPS)
+        normed = centered * inverse
+        cot = flow[seq].astype(F32)
+        flow[seq] = (normed * gain_two + bias_two).astype(BF16)
+        gain_two_sum = gain_two_sum + jnp.sum(cot * normed, axis=0, keepdims=True)
+        bias_two_sum = bias_two_sum + jnp.sum(cot, axis=0, keepdims=True)
+        scaled = cot * gain_two
+        dh_two = inverse * (scaled - mean(scaled) - normed * mean(scaled * normed))
+        dh_ref[seq] = dh_two
+        dm_low[seq * rows : (seq + 1) * rows, :] = dh_two.astype(BF16)
+    output_out = pltpu.make_async_copy(flow, output_ref, loads.at[4])
+    output_out.start()
+
+    def store(kind, block):
+        if kind < 2:
+            start = pl.multiple_of((kind * blocks + block) * depth, depth)
+            return [
+                pltpu.make_async_copy(
+                    staged.at[kind, pl.ds(shard * depth, depth)],
+                    packed_ref.at[shard, pl.ds(start, depth)],
+                    stores.at[kind, shard],
+                )
+                for shard in range(shards)
+            ]
+        start = 2 * blocks * depth
+        return [
+            pltpu.make_async_copy(
+                staged.at[2], packed_ref.at[block, pl.ds(start, width)], stores.at[2, 0]
+            )
+        ]
+
+    def backward(block, carry):
+        at = pl.ds(pl.multiple_of(block * width, width), width)
+        for seq in range(seqs):
+            here = slice(seq * rows, (seq + 1) * rows)
+            d_hidden = lax.dot_general(dm_low[here, :], w_down[at, :], BY_LANES, preferred_element_type=F32)
+            gate = gate_kept[block, seq].astype(F32)
+            up = up_kept[block, seq].astype(F32)
+            sigma = jax.nn.sigmoid(gate)
+            smooth = gate * sigma
+            hidden_kept[here, :] = (smooth * up).astype(BF16)
+            dg = (d_hidden * up * (sigma + smooth * (1.0 - sigma))).astype(BF16)
+            du = (d_hidden * smooth).astype(BF16)
+            d_gate[here, :] = dg
+            d_up[here, :] = du
+            dh_ref[seq] += lax.dot_general(dg, w_gate[:, at], BY_LANES, preferred_element_type=F32)
+            dh_ref[seq] += lax.dot_general(du, w_up[:, at], BY_LANES, preferred_element_type=F32)
+
+        @pl.when(block > 0)
+        def _():
+            for kind in range(3):
+                for copy in store(kind, block - 1):
+                    copy.wait()
+
+        staged[0] = jnp.dot(x_turned[...], d_gate[...], preferred_element_type=F32).astype(BF16)
+        staged[1] = jnp.dot(x_turned[...], d_up[...], preferred_element_type=F32).astype(BF16)
+        staged[2] = lax.dot_general(
+            hidden_kept[...], dm_low[...], (((0,), (0,)), ((), ())), preferred_element_type=F32
+        ).astype(BF16)
+        for kind in range(3):
+            for copy in store(kind, block):
+                copy.start()
+        return carry
+
+    lax.fori_loop(0, blocks, backward, 0)
+
+    gain_one_sum = jnp.zeros((1, width), F32)
+    bias_one_sum = jnp.zeros((1, width), F32)
+    for seq in range(seqs):
+        here = slice(seq * rows, (seq + 1) * rows)
+        dx_one = dh_ref[seq]
+        normed = hat_one[seq]
+        gain_one_sum = gain_one_sum + jnp.sum(dx_one * normed, axis=0, keepdims=True)
+        bias_one_sum = bias_one_sum + jnp.sum(dx_one, axis=0, keepdims=True)
+        scaled = dx_one * gain_one
+        dh_one = inverse_one[seq] * (scaled - mean(scaled) - normed * mean(scaled * normed))
+        dh_ref[seq] = dh_one
+        d_attn = dh_one.astype(BF16)
+        d_gate[here, :] = d_attn
+        for group in range(GROUPS):
+            dout_ref[seq * GROUPS + group] = lax.dot_general(
+                d_attn, w_out[group * depth : (group + 1) * depth, :], BY_LANES, preferred_element_type=F32
+            ).astype(BF16)
+    for kind in range(3):
+        for copy in store(kind, blocks - 1):
+            copy.wait()
+    for group in range(GROUPS):
+        grad = jnp.zeros((depth, width), F32)
+        for seq in range(seqs):
+            grad = grad + lax.dot_general(
+                joined_ref[seq * GROUPS + group],
+                d_gate[seq * rows : (seq + 1) * rows, :],
+                (((0,), (0,)), ((), ())),
+                preferred_element_type=F32,
+            )
+        staged[0, group * depth : (group + 1) * depth, :] = grad.astype(BF16)
+    last = [
+        pltpu.make_async_copy(
+            staged.at[0, pl.ds(shard * depth, depth)],
+            packed_ref.at[shard, pl.ds(3 * blocks * depth, depth)],
+            stores.at[0, shard],
+        )
+        for shard in range(shards)
+    ]
+    for copy in last:
+        copy.start()
+    norm_sums_ref[0:1, :] = gain_one_sum
+    norm_sums_ref[1:2, :] = bias_one_sum
+    norm_sums_ref[2:3, :] = gain_two_sum
+    norm_sums_ref[3:4, :] = bias_two_sum
+    for copy in last:
+        copy.wait()
+    output_out.wait()
+
+
+def feed_forward(tokens, joined, cotangent, w_out, w_gate, w_up, w_down, norms, kept=BF16):
+    seqs, rows, width = tokens.shape
+    total = seqs * rows
+    hidden = w_gate.shape[1]
+    blocks = hidden // width
+    depth = width // GROUPS
+    vmem = pl.BlockSpec(memory_space=pltpu.VMEM)
+    hbm = pl.BlockSpec(memory_space=pltpu.HBM)
+    dma = pltpu.SemaphoreType.DMA
+    return pl.pallas_call(
+        feed_forward_kernel,
+        out_shape=(
+            jax.ShapeDtypeStruct(tokens.shape, BF16),
+            jax.ShapeDtypeStruct(joined.shape, BF16),
+            jax.ShapeDtypeStruct(tokens.shape, F32),
+            jax.ShapeDtypeStruct((4, width), F32),
+            jax.ShapeDtypeStruct((GROUPS, (3 * blocks + 1) * depth, width), BF16),
+        ),
+        in_specs=[hbm, vmem, hbm, hbm, hbm, hbm, hbm, vmem],
+        out_specs=(hbm, vmem, vmem, vmem, hbm),
+        scratch_shapes=[
+            pltpu.VMEM(w_out.shape, BF16),
+            pltpu.VMEM(w_gate.shape, BF16),
+            pltpu.VMEM(w_up.shape, BF16),
+            pltpu.VMEM(w_down.shape, BF16),
+            pltpu.VMEM(tokens.shape, BF16),
+            pltpu.VMEM(tokens.shape, F32),
+            pltpu.VMEM((seqs, rows, 1), F32),
+            pltpu.VMEM(tokens.shape, BF16),
+            pltpu.VMEM((width, total), BF16),
+            pltpu.VMEM((total, width), BF16),
+            pltpu.VMEM((blocks, seqs, rows, width), kept),
+            pltpu.VMEM((blocks, seqs, rows, width), kept),
+            pltpu.VMEM((total, width), BF16),
+            pltpu.VMEM((total, width), BF16),
+            pltpu.VMEM((total, width), BF16),
+            pltpu.VMEM((3, width, width), BF16),
+            dma((5,)),
+            dma((3, GROUPS)),
+        ],
+        compiler_params=pltpu.CompilerParams(vmem_limit_bytes=FEED_LIMIT),
+        cost_estimate=pl.CostEstimate(
+            flops=6 * total * width * (3 * hidden + width),
+            bytes_accessed=2 * 2 * (3 * hidden + width) * width + 20 * total * width,
+            transcendentals=2 * total * hidden,
+        ),
+        name="feed_forward",
+    )(tokens, joined, cotangent, w_out, w_gate, w_up, w_down, norms)
+
+
 def document_places(seg_row):
     length = seg_row.shape[0]
     ids = jnp.arange(LANES - HD, dtype=jnp.int32)[:, None]
     starts = jnp.sum((seg_row[None, :] < ids).astype(jnp.int32), axis=1, keepdims=True)
     start = jnp.sum(jnp.where(seg_row[None, :] == ids, starts, 0), axis=0)
     return jnp.arange(length, dtype=jnp.int32) - start
-
-
-def by_group(block_rows):
-    seqs, rows, width = block_rows.shape
-    split = block_rows.reshape(seqs, rows, GROUPS, width // GROUPS)
-    return jnp.transpose(split, (0, 2, 1, 3)).reshape(seqs * GROUPS, rows, width // GROUPS)
-
-
-def from_group(blocks):
-    devices, rows, width = blocks.shape
-    split = blocks.reshape(devices // GROUPS, GROUPS, rows, width)
-    return jnp.transpose(split, (0, 2, 1, 3)).reshape(devices // GROUPS, rows, GROUPS * width)
 
 
 def exchange(blocks):
@@ -1020,8 +1265,7 @@
         return lax.all_gather(shard, "shard", axis=0, tiled=True)
 
     pieces, w_heads = gather_tokens(tokens, head_columns(w_qkv, me % GROUPS, held), shards)
-    norms = gather(jnp.stack([ln1_gain, ln1_bias, ln2_gain, ln2_bias], axis=1)).astype(F32)
-    gain_one, bias_one, gain_two, bias_two = (norms[:, n] for n in range(4))
+    norms = lax.all_gather(jnp.stack([ln1_gain, ln1_bias, ln2_gain, ln2_bias]), "shard", axis=1, tiled=True).astype(F32)
     full_out, full_gate, full_up, full_down = (gather(w) for w in (w_out, w_gate, w_up, w_down))
     freqs = jnp.exp(jnp.arange(HD // 2, dtype=F32) * (-math.log(ROPE_BASE) / (HD // 2)))
     freq = jnp.tile(freqs, LANES // (HD // 2))[None]
@@ -1031,59 +1275,16 @@
         seg_row.astype(F32), place, freq, pieces, w_heads.reshape(model_width, -1), held
     )
     sums, joined_own = attend_heads(bounds, q_ext, k_ext, v_ext, row_count)
-    joined = from_group(exchange(joined_own))
-
-    tokens_f = tokens.astype(F32)
-    h_one = tokens_f + jnp.einsum("sci,io->sco", joined, full_out, preferred_element_type=F32)
-    x_one, normed_one, inverse_one = norm_fwd(h_one, gain_one, bias_one)
-    x_low = x_one.astype(BF16)
-    gate_pre = jnp.einsum("scd,df->scf", x_low, full_gate, preferred_element_type=F32)
-    up_pre = jnp.einsum("scd,df->scf", x_low, full_up, preferred_element_type=F32)
-    sigma = jax.nn.sigmoid(gate_pre)
-    smooth = gate_pre * sigma
-    hidden = (smooth * up_pre).astype(BF16)
-    h_two = x_one + jnp.einsum("scf,fd->scd", hidden, full_down, preferred_element_type=F32)
-    result, normed_two, inverse_two = norm_fwd(h_two, gain_two, bias_two)
-    output = result.astype(BF16)
-
-    cot_f = cotangent.astype(F32)
-    grad_gain_two = jnp.sum(cot_f * normed_two, axis=(0, 1))
-    grad_bias_two = jnp.sum(cot_f, axis=(0, 1))
-    dh_two = norm_back(cot_f, normed_two, inverse_two, gain_two)
-    dm_low = dh_two.astype(BF16)
-    d_hidden = jnp.einsum("scd,fd->scf", dm_low, full_down, preferred_element_type=F32)
-    d_up = (d_hidden * smooth).astype(BF16)
-    d_gate = (d_hidden * up_pre * sigma * (1.0 + gate_pre * (1.0 - sigma))).astype(BF16)
-    dx_one = (
-        dh_two
-        + jnp.einsum("scf,df->scd", d_gate, full_gate, preferred_element_type=F32)
-        + jnp.einsum("scf,df->scd", d_up, full_up, preferred_element_type=F32)
-    )
-    grad_gain_one = jnp.sum(dx_one * normed_one, axis=(0, 1))
-    grad_bias_one = jnp.sum(dx_one, axis=(0, 1))
-    dh_one = norm_back(dx_one, normed_one, inverse_one, gain_one)
-    d_attn = dh_one.astype(BF16)
-    d_joined = jnp.einsum("sco,io->sci", d_attn, full_out, preferred_element_type=F32).astype(BF16)
-
-    grad_down = jnp.einsum("scf,scd->fd", hidden, dm_low, preferred_element_type=F32).astype(BF16)
-    grad_gate = jnp.einsum("scd,scf->df", x_low, d_gate, preferred_element_type=F32).astype(BF16)
-    grad_up = jnp.einsum("scd,scf->df", x_low, d_up, preferred_element_type=F32).astype(BF16)
-    grad_out = jnp.einsum("sci,sco->io", joined, d_attn, preferred_element_type=F32).astype(BF16)
-    norms_part = jnp.stack([grad_gain_one, grad_bias_one, grad_gain_two, grad_bias_two])
+    output, d_joined, dh_one, norms_part, packed = feed_forward(
+        tokens, exchange(joined_own), cotangent, full_out, full_gate, full_up, full_down, norms
+    )
     depth = model_width // shards
-    ff_blocks = grad_gate.shape[1] // model_width
-
-    def by_shard(grad):
-        split = grad.reshape(shards, -1, grad.shape[1] // model_width, model_width)
-        return jnp.transpose(split, (0, 2, 1, 3)).reshape(shards, -1, model_width)
-
-    packed = jnp.concatenate([by_shard(g) for g in (grad_gate, grad_up, grad_down, grad_out)], axis=1)
-    d_joined, packed = lax.optimization_barrier((d_joined, packed))
+    ff_blocks = full_gate.shape[1] // model_width
     owned = lax.psum_scatter(
         packed.reshape(-1, model_width), ("shard", "seq"), scatter_dimension=0, tiled=True
     )
 
-    dout = exchange(by_group(d_joined))
+    dout = exchange(d_joined)
     d_heads = attend_back_heads(bounds, q_ext, k_ext, v_ext, sums, dout, turn)
     w_own = w_heads.reshape(model_width, -1, LANES)[:, :, :HD].reshape(model_width, -1)
     partial = jnp.einsum("prc,dc->prd", d_heads, w_own, preferred_element_type=F32).astype(BF16)

time: 681 us -> 603 us (0.89)
  matrix products: 119 us -> 16.4 us
  Pallas kernels: 365 us -> 446 us
  local copies, waits for them, and re-layouts: 69 us -> 39.5 us
  other arithmetic: 25.3 us -> 8.61 us
    dot_general x12 -> x0, matrix products: 102 us -> none  [the longest x1 19.4 us: local_heads(): jnp.einsum('scd,fd->scf', dm_low, full_down, preferred_element_type=F32)]
    pallas_call x0 -> x1, Pallas kernels: none -> 70.6 us  [feed_forward(): pl.pallas_call(feed_forward_kernel, out_shape=(jax.ShapeDtypeStruct(token...]
    reshape x5 -> x0, local copies, waits for them, and re-layouts: 30.2 us -> none  [the longest x4 28 us: by_shard(): split = grad.reshape(shards, -1, grad.shape[1] // model_width, model_width)]
    pallas_call x1, Pallas kernels: 102 us -> 110 us  [attend_back_heads(): pl.pallas_call(functools.partial(attend_back_kernel, window, align), out_...]
    concatenate x2 -> x0, other arithmetic: 7.29 us -> none  [the longest x1 6.95 us: local_heads(): jnp.concatenate([by_shard(g) for g in (grad_gate, grad_up, grad_down, gra...]
  transfers between devices with their start and end apart: 8 -> 8, of which waited for: 3 -> 2; matrix products, arithmetic and copies ran while one was open for 12% -> 9% of each run, Pallas kernels for 54% -> 63%
where the time goes in v4:
time: 603 us; the launch traced here: 597 us
  Pallas kernels  446 us (74%)
  waiting for transfers between devices  53.5 us (9%)
  local copies, waits for them, and re-layouts  39.5 us (7%)
  matrix products  16.4 us (3%)
  between operations  14.6 us (2%)
  starting transfers between devices  13.1 us (2%)
  other arithmetic  8.61 us (1%)
    pallas_call x1, Pallas kernels, scatter_gradients(): pl.pallas_call(functools.partial(scatter_kernel, chunks, by_z), out_shape...  134 us
    pallas_call x1, Pallas kernels, attend_back_heads(): pl.pallas_call(functools.partial(attend_back_kernel, window, align), out_...  110 us
    pallas_call x1, Pallas kernels, feed_forward(): pl.pallas_call(feed_forward_kernel, out_shape=(jax.ShapeDtypeStruct(token...  70.6 us
    pallas_call x1, Pallas kernels, gather_tokens(): pl.pallas_call(functools.partial(gather_kernel, chunks, by_z), out_shape=...  68.8 us
    all_to_all x2, waiting for transfers between devices, exchange(): return lax.all_to_all(blocks, 'seq', 0, 0, tiled=True)  50.8 us
    pallas_call x1, Pallas kernels, attend_heads(): pl.pallas_call(functools.partial(attend_kernel, window, align), out_shape...  42.3 us
    pallas_call x1, Pallas kernels, project_heads(): pl.pallas_call(project_kernel, out_shape=(head_shape, head_shape, head_sh...  21.2 us
    all_to_all x2, starting transfers between devices, exchange(): return lax.all_to_all(blocks, 'seq', 0, 0, tiled=True)  12.9 us
  transfers between devices with their start and end apart: 8, of which 2 were waited for; matrix products, arithmetic and copies ran while one was open for 9% of the time, Pallas kernels for 63%

profile of v4, /device:TPU:20, one launch (start us, length us, event | category | flops | bytes accessed | tf_op | source)
XLA Modules:
  0.0 597.4 jit_solution(10689897030362082273)
XLA Ops:
  7.2 0.0 copy-start.3
  7.2 0.0 copy-start.2
  7.2 0.0 all-gather.7.cloned.1.call-start
  7.2 0.7 all-gather.7.cloned.1.call-update
  7.9 0.0 all-gather.9.cloned.1.call-start
  8.0 0.7 all-gather.9.cloned.1.call-update
  8.7 0.0 copy-start.4
  8.7 0.0 all-gather.11.cloned.1.call-start
  8.7 0.7 all-gather.11.cloned.1.call-update
  9.4 0.0 all-gather.13.cloned.1.call-start
  9.5 0.5 all-gather.13.cloned.1.call-update
  10.0 0.0 copy-done.3
  10.0 0.6 fusion.2
  10.7 0.1 slice.34
  10.8 0.1 slice.33
  10.9 0.6 broadcast_in_dim_tile.3.freq_ref
  11.5 0.0 copy-done.2
  11.5 0.6 copy.66
  12.1 0.1 broadcast_multiply_fusion
  12.2 0.1 pad_maximum_fusion
  12.3 1.0 copy.83.w_ref
  13.3 68.8 %gather_tokens.1 = (bf16[8,512,768]{2,1,0:T(8,128)(2,1)}, bf16[4,192,1152]{2,1,0:T(8,128)(2,1)}) custom-call(bf16[2,512,768]{2,1,0:T(8,128)(2,1)} %tokens_ref.1, bf16[192,1152]{1,0:T(8,128)(2,1)} %copy.83.w_ref), custom_call_target="tpu_custom_call" | custom-call | tf_op jit(solution)/shard_map/gather_tokens/pallas_call | solution.py:444
  82.1 0.2 convert_reduce_fusion.1
  82.3 0.2 convert_reduce_fusion
  82.5 0.2 select_reduce_fusion
  82.8 0.5 subtract_minimum_fusion
  83.3 0.6 subtract_convert_fusion.place_ref
  84.0 21.2 %project_heads.1 = (bf16[3,4096,128]{2,1,0:T(8,128)(2,1)}, bf16[3,4096,128]{2,1,0:T(8,128)(2,1)}, bf16[3,4096,128]{2,1,0:T(8,128)(2,1)}, f32[4096,128]{1,0:T(8,128)}) custom-call(f32[8,1,512]{2,1,0:T(1,128)} %bitcast.65, f32[8,1,512]{2,1,0:T(1,128)} %subtract_convert_fusion.place_ref, f32[1,128]{1,0:T(1,128)} %broadcast_in_dim_tile.3.freq_ref, ...), custom_call_target="tpu_custom_call" | custom-call | flops 7247757312 | bytes 17825792 | tf_op jit(solution)/shard_map/project_heads/pallas_call | solution.py:502
  105.1 42.3 %attend_heads.1 = (f32[3,4096,128]{2,1,0:T(8,128)}, bf16[8,512,192]{2,1,0:T(8,128)(2,1)}) custom-call(s32[8]{0:T(128)} %get-tuple-element.66.low_ref, s32[8]{0:T(128)} %get-tuple-element.67.count_ref, bf16[3,4096,128]{2,1,0:T(8,128)(2,1)} %get-tuple-element.32.q_ref, bf16[3,4096,128]{2,1,0:T(8,128)(2,1)} %get-tuple-element.33.k_ref, ...), custom_call_target="tpu_custom_call" | custom-call | flops 12884901888 | bytes 15728640 | tf_op jit(solution)/shard_map/attend_heads/pallas_call | solution.py:564
  147.4 3.9 copy.68
  151.3 5.2 all-to-all-start
  156.7 5.4 all-gather
  162.1 0.7 reshape.124
  162.8 25.0 %all-to-all-done = bf16[8,512,192]{1,2,0:T(8,128)(2,1)S(1)} async-done(((bf16[8,512,192]{1,2,0:T(8,128)(2,1)}), bf16[8,512,192]{1,2,0:T(8,128)(2,1)S(1)}, u32[]{:S(2)}, u32[]{:S(2)}) %all-to-all-start) | async-done | bytes 1572896 | tf_op jit(solution)/shard_map/all_to_all | solution.py:1231
  187.8 2.4 copy.70.joined_ref
  190.2 0.0 all-gather.13.cloned.1.call-done.down_hbm
  190.2 70.6 %feed_forward.1 = (bf16[2,512,768]{2,1,0:T(8,128)(2,1)}, bf16[8,512,192]{2,1,0:T(8,128)(2,1)}, f32[2,512,768]{2,1,0:T(8,128)}, f32[4,768]{1,0:T(4,128)}, bf16[4,2496,768]{2,1,0:T(8,128)(2,1)}) custom-call(bf16[2,512,768]{2,1,0:T(8,128)(2,1)} %tokens_ref.1, bf16[8,512,192]{2,1,0:T(8,128)(2,1)} %copy.70.joined_ref, bf16[2,512,768]{2,1,0:T(8,128)(2,1)} %cot_ref.1, ...), custom_call_target="tpu_custom_call" | custom-call | flops 47110422528 | bytes 46399488 | tf_op jit(solution)/shard_map/feed_forward/pallas_call | solution.py:1181
  260.9 0.0 copy-start
  260.9 0.0 reduce-scatter.2.cloned.1.call-update
  260.9 1.6 copy-done
  262.5 2.2 copy.71
  264.7 7.7 %all-to-all-start.1 = ((bf16[8,512,192]{1,2,0:T(8,128)(2,1)}), bf16[8,512,192]{1,2,0:T(8,128)(2,1)}, u32[]{:S(2)}, u32[]{:S(2)}) async-start(bf16[8,512,192]{1,2,0:T(8,128)(2,1)} %copy.71), calls=%async_computation.1 | async-start | bytes 3145728 | tf_op jit(solution)/shard_map/all_to_all | solution.py:1231
  272.4 4.3 copy.73
  276.6 3.0 reshape.112
  279.7 25.8 %all-to-all-done.1 = bf16[8,512,192]{1,2,0:T(8,128)(2,1)} async-done(((bf16[8,512,192]{1,2,0:T(8,128)(2,1)}), bf16[8,512,192]{1,2,0:T(8,128)(2,1)}, u32[]{:S(2)}, u32[]{:S(2)}) %all-to-all-start.1) | async-done | bytes 1572896 | tf_op jit(solution)/shard_map/all_to_all | solution.py:1231
  305.5 3.8 copy.72.dout_ref
  309.3 109.5 %attend_back_heads.1 = bf16[8,512,576]{2,1,0:T(8,128)(2,1)} custom-call(s32[8]{0:T(128)} %get-tuple-element.51.low_ref, s32[8]{0:T(128)} %get-tuple-element.52.count_ref, bf16[3,4096,128]{2,1,0:T(8,128)(2,1)} %get-tuple-element.32.q_ref, f32[3,4096,128]{2,1,0:T(8,128)} %get-tuple-element.37.sum_ref, bf16[8,512,192]{2,1,0:T(8,128)(2,1)} %copy.72.dout_ref, ...), custom_call_target="tpu_custom_call" | custom-call | flops 32212254720 | bytes 31457280 | tf_op jit(solution)/shard_map/attend_back_heads/pallas_call | solution.py:685
  418.8 9.5 %convolution_convert_fusion.part_ref = bf16[8,512,768]{2,1,0:T(8,128)(2,1)} fusion(bf16[8,512,576]{2,1,0:T(8,128)(2,1)} %attend_back_heads.1, bf16[768,576,1]{0,1,2:T(8,128)(2,1)S(1)} %bitcast.52), kind=kOutput, calls=%fused_computation | convolution fusion | flops 3627024384 | bytes 11894784 | tf_op jit(solution)/shard_map/prc,dc->prd/dot_general | solution.py:1290
  428.3 6.9 %bitcast_convert_fusion = bf16[768,576]{0,1:T(8,128)(2,1)S(1)} fusion(bf16[8,512,768]{2,1,0:T(8,128)(2,1)} %get-tuple-element.30.x_ref, bf16[8,512,576]{2,1,0:T(8,128)(2,1)S(1)} %copy-done.9), kind=kOutput, calls=%fused_computation.3 | convolution fusion | flops 3624321024 | bytes 11894784 | tf_op jit(solution)/shard_map/prd,prc->dc/dot_general | solution.py:1291
  435.2 0.0 reduce-scatter.2.cloned.1.call-done
  435.2 0.0 all-gather.15.cloned.1.call-update
  435.3 1.5 copy.76
  436.8 133.8 %scatter_gradients.1 = (bf16[2,512,768]{2,1,0:T(8,128)(2,1)}, bf16[4,192,576]{2,1,0:T(8,128)(2,1)}, f32[4,768]{1,0:T(4,128)}) custom-call(bf16[8,512,768]{2,1,0:T(8,128)(2,1)} %convolution_convert_fusion.part_ref, f32[2,512,768]{2,1,0:T(8,128)} %get-tuple-element.42.dh_ref, bf16[4,192,576]{2,1,0:T(8,128)(2,1)} %bitcast.58, f32[4,768]{1,0:T(4,128)} %get-tuple-element.44.norm_ref), custom_call_target="tpu_custom_call" | custom-call | flops 60000002048 | bytes 67108864 | tf_op jit(solution)/shard_map/scatter_gradients/pallas_call | solution.py:926
  570.6 1.5 copy.77
  572.2 2.5 copy.78
  574.7 3.7 reshape.116
  578.4 1.5 fusion.3
  579.9 3.7 slice_convert_fusion
  583.6 0.2 convert_bitcast_fusion
  583.8 1.7 copy.85
  585.4 0.2 convert_bitcast_fusion.1
  585.7 1.7 copy.84
  587.3 1.8 slice_convert_fusion.1
  589.1 1.1 copy.87
  (30 shorter events, 0.1 us)
Async XLA Ops:
  7.2 2.9 copy-start.3
  7.2 4.3 copy-start.2
  7.2 183.0 %all-gather.7.cloned.1.call-start = ((), (), s32[]{:S(2)}) async-start(), calls=%async_computation.3 | async-start | bytes 1474560 | tf_op jit(solution)/shard_map/all_gather | solution.py:1265
  7.9 182.3 %all-gather.9.cloned.1.call-start = ((), (), s32[]{:S(2)}) async-start(), calls=%async_computation.4 | async-start | bytes 5898240 | tf_op jit(solution)/shard_map/all_gather | solution.py:1265
  8.7 3.4 copy-start.4
  8.7 181.5 %all-gather.11.cloned.1.call-start = ((), (), s32[]{:S(2)}) async-start(), calls=%async_computation.5 | async-start | bytes 5898240 | tf_op jit(solution)/shard_map/all_gather | solution.py:1265
  9.4 180.8 %all-gather.13.cloned.1.call-start = ((), (), s32[]{:S(2)}) async-start(), calls=%async_computation.6 | async-start | bytes 5898240 | tf_op jit(solution)/shard_map/all_gather | solution.py:1265
  151.3 5.3 copy-start.5
  151.3 5.3 copy-start.6
  151.3 5.3 copy-start.7
  151.3 5.3 copy-start.8
  151.3 36.5 %all-to-all-start = ((bf16[8,512,192]{1,2,0:T(8,128)(2,1)}), bf16[8,512,192]{1,2,0:T(8,128)(2,1)S(1)}, u32[]{:S(2)}, u32[]{:S(2)}) async-start(bf16[8,512,192]{1,2,0:T(8,128)(2,1)} %copy.68), calls=%async_computation | async-start | bytes 3145728 | tf_op jit(solution)/shard_map/all_to_all | solution.py:1231
  156.6 278.7 %reduce-scatter.2.cloned.1.call-start = ((), (), s32[]{:S(2)}) async-start(), calls=%async_computation.7 | async-start | bytes 15814656 | tf_op jit(solution)/shard_map/reduce_scatter | solution.py:1283
  260.9 1.6 copy-start
  264.7 40.8 %all-to-all-start.1 = ((bf16[8,512,192]{1,2,0:T(8,128)(2,1)}), bf16[8,512,192]{1,2,0:T(8,128)(2,1)}, u32[]{:S(2)}, u32[]{:S(2)}) async-start(bf16[8,512,192]{1,2,0:T(8,128)(2,1)} %copy.71), calls=%async_computation.1 | async-start | bytes 3145728 | tf_op jit(solution)/shard_map/all_to_all | solution.py:1231
  272.4 307.5 %all-gather.15.cloned.1.call-start = ((), (), s32[]{:S(2)}) async-start(), calls=%async_computation.8 | async-start | bytes 4313088 | tf_op jit(solution)/shard_map/all_gather | solution.py:1293
  309.3 109.5 %slice-start = ((bf16[768,9,128]{0,2,1:T(8,128)(2,1)}), bf16[768,9,64]{0,2,1:T(8,128)(2,1)S(1)}, s32[]{:S(2)}) async-start(bf16[768,9,128]{0,2,1:T(8,128)(2,1)} %reshape.112), calls=%async_computation.9 | async-start | bytes 1769472 | tf_op jit(solution)/shard_map/slice | solution.py:1289
  418.8 9.5 %copy-start.9 = (bf16[8,512,576]{2,1,0:T(8,128)(2,1)S(1)}, bf16[8,512,576]{2,1,0:T(8,128)(2,1)}, u32[]{:S(2)}) copy-start(bf16[8,512,576]{2,1,0:T(8,128)(2,1)} %attend_back_heads.1) | copy-start | bytes 14155780
  585.6 3.5 copy-start.1
Sparse Core Ops, SparseCore 0:
  9.6 24.8 all-gather.6
  36.0 37.4 all-gather.8
  75.1 37.4 all-gather.10
  113.9 37.4 all-gather.12
  261.0 168.7 reduce-scatter.1
  435.4 109.3 all-gather.14

commit v5 on v4

--- a/solution.py
+++ b/solution.py
@@ -344,11 +344,30 @@
 BY_LANES = (((1,), (1,)), ((), ()))
 
 
+def packed_heads(rows):
+    return rows + rows // 2
+
+
+def unpack_heads(block):
+    rows = block.shape[0] * 2 // 3
+    last = block[rows:]
+    third = jnp.concatenate([last[:, :HD], last[:, HD:]], axis=0)
+    return jnp.concatenate([block[:rows], third], axis=1)
+
+
+def pack_heads(value):
+    rows = value.shape[0]
+    third = value[:, 2 * HD :]
+    return value[:, : 2 * HD], jnp.concatenate([third[: rows // 2], third[rows // 2 :]], axis=1)
+
+
 def flip(index, bit):
     return index + bit - 2 * bit * lax.rem(lax.div(index, bit), 2)
 
 
-def gather_kernel(chunks, by_z, tok_ref, w_ref, all_ref, w_all_ref, send, recv, kept, w_send, w_recv):
+def gather_kernel(
+    chunks, by_z, tok_ref, w_ref, n_ref, place_ref, freq_ref, all_ref, w_all_ref, n_all_ref, turn_ref, send, recv, kept, w_send, w_recv
+):
     me = lax.axis_index("seq")
     shard = lax.axis_index("shard")
     shards = w_all_ref.shape[0]
@@ -405,10 +424,34 @@
         )
         copy.start()
         weights.append(copy)
+        copy = pltpu.make_async_remote_copy(
+            src_ref=n_ref,
+            dst_ref=n_all_ref.at[shard],
+            send_sem=w_send.at[shards + step],
+            recv_sem=w_recv.at[shards + step],
+            device_id={"shard": lax.rem(shard + step, shards)},
+            device_id_type=BY_MESH,
+        )
+        copy.start()
+        weights.append(copy)
+    keep_n = pltpu.make_async_copy(n_ref, n_all_ref.at[shard], kept.at[2])
+    keep_n.start()
     keep_tok = pltpu.make_async_copy(tok_ref.at[half], all_ref.at[me], kept.at[0])
     keep_tok.start()
     keep_w = pltpu.make_async_copy(w_ref, w_all_ref.at[shard], kept.at[1])
     keep_w.start()
+
+    def turn_piece(index, carry):
+        count = turn_ref.shape[0] // place_ref.shape[0]
+        lane = lax.broadcasted_iota(jnp.int32, (count, LANES), 1)
+        place = jnp.transpose(jnp.broadcast_to(place_ref[index], (LANES, count)))
+        angle = place * freq_ref[...]
+        turn_ref[pl.ds(pl.multiple_of(index * count, count), count), :] = jnp.where(
+            lane < HD, jnp.cos(angle), jnp.sin(angle)
+        )
+        return carry
+
+    lax.fori_loop(0, place_ref.shape[0], turn_piece, 0)
 
     cross_y, cross_z, corner = [], [], []
     for chunk in range(chunks):
@@ -434,41 +477,43 @@
         copy.wait()
     keep_tok.wait()
     keep_w.wait()
+    keep_n.wait()
     for copy in started:
         copy.wait_send()
 
 
-def gather_tokens(tokens, w_part, shards, chunks=8, by_z=3):
+def gather_tokens(tokens, w_part, norms, place, freq, shards, chunks=8, by_z=3):
     seqs, rows, width = tokens.shape
     anywhere = pl.BlockSpec(memory_space=pl.ANY)
+    vmem = pl.BlockSpec(memory_space=pltpu.VMEM)
     return pl.pallas_call(
         functools.partial(gather_kernel, chunks, by_z),
         out_shape=(
             jax.ShapeDtypeStruct((SEQ_SIZE, rows, width), tokens.dtype),
             jax.ShapeDtypeStruct((shards,) + w_part.shape, w_part.dtype),
+            jax.ShapeDtypeStruct((shards,) + norms.shape, norms.dtype),
+            jax.ShapeDtypeStruct((place.shape[0] * place.shape[2], LANES), F32),
         ),
-        in_specs=[anywhere, anywhere],
-        out_specs=(anywhere, anywhere),
+        in_specs=[anywhere, anywhere, anywhere, vmem, vmem],
+        out_specs=(anywhere, anywhere, anywhere, vmem),
         scratch_shapes=[
             pltpu.SemaphoreType.DMA((7 * chunks,)),
             pltpu.SemaphoreType.DMA((7 * chunks,)),
-            pltpu.SemaphoreType.DMA((2,)),
-            pltpu.SemaphoreType.DMA((shards,)),
-            pltpu.SemaphoreType.DMA((shards,)),
+            pltpu.SemaphoreType.DMA((3,)),
+            pltpu.SemaphoreType.DMA((2 * shards,)),
+            pltpu.SemaphoreType.DMA((2 * shards,)),
         ],
         compiler_params=pltpu.CompilerParams(collective_id=1, has_side_effects=True),
         name="gather_tokens",
-    )(tokens, w_part)
-
-
-def project_kernel(seg_ref, place_ref, freq_ref, x_ref, w_ref, q_ref, k_ref, v_ref, turn_ref):
+    )(tokens, w_part, norms, place, freq)
+
+
+def project_kernel(seg_ref, turn_ref, x_ref, w_ref, q_ref, k_ref, v_ref):
     rows = x_ref.shape[1]
     held = q_ref.shape[0]
     lane = lax.broadcasted_iota(jnp.int32, (rows, LANES), 1)
     seg = jnp.transpose(jnp.broadcast_to(seg_ref[0], (LANES, rows)))
-    place = jnp.transpose(jnp.broadcast_to(place_ref[0], (LANES, rows)))
-    turn = jnp.where(lane < HD, jnp.cos(place * freq_ref[...]), jnp.sin(place * freq_ref[...]))
-    turn_ref[...] = turn
+    turn = turn_ref[...]
     cos_b = jnp.where(lane < HD, turn, 0.0)
     sin_b = jnp.where(lane < HD, pltpu.roll(turn, HD, 1), 0.0)
     sin_b = jnp.where(lane < HD // 2, -sin_b, sin_b)
@@ -493,7 +538,7 @@
                 v_ref[head] = (value + v_tail).astype(BF16)
 
 
-def project_heads(seg_row, place_row, freq, pieces, w_full, held):
+def project_heads(seg_row, turn, pieces, w_full, held):
     count, rows, width = pieces.shape
     length = count * rows
     row_spec = pl.BlockSpec((1, 1, rows), lambda i: (i, 0, 0))
@@ -501,16 +546,15 @@
     head_shape = jax.ShapeDtypeStruct((held, length, LANES), BF16)
     return pl.pallas_call(
         project_kernel,
-        out_shape=(head_shape, head_shape, head_shape, jax.ShapeDtypeStruct((length, LANES), F32)),
+        out_shape=(head_shape, head_shape, head_shape),
         grid=(count,),
         in_specs=[
             row_spec,
-            row_spec,
-            pl.BlockSpec((1, LANES), lambda i: (0, 0)),
+            pl.BlockSpec((rows, LANES), lambda i: (i, 0)),
             pl.BlockSpec((1, rows, width), lambda i: (i, 0, 0)),
             pl.BlockSpec(w_full.shape, lambda i: (0, 0)),
         ],
-        out_specs=(head_spec, head_spec, head_spec, pl.BlockSpec((rows, LANES), lambda i: (i, 0))),
+        out_specs=(head_spec, head_spec, head_spec),
         compiler_params=pltpu.CompilerParams(vmem_limit_bytes=VMEM_LIMIT),
         cost_estimate=pl.CostEstimate(
             flops=2 * length * width * w_full.shape[1],
@@ -518,7 +562,7 @@
             transcendentals=length * LANES,
         ),
         name="project_heads",
-    )(seg_row.reshape(count, 1, rows), place_row.reshape(count, 1, rows), freq, pieces, w_full)
+    )(seg_row.reshape(count, 1, rows), turn, pieces, w_full)
 
 
 def document_bounds(seg_row, rows):
@@ -551,9 +595,11 @@
         return carry
 
     lax.fori_loop(0, count_ref[block], step, 0)
-    for head in range(q_ref.shape[0]):
-        sums = sum_ref[head]
-        joined_ref[0, :, head * HD : (head + 1) * HD] = (sums[:, :HD] / sums[:, HD : HD + 1]).astype(BF16)
+    rows = q_ref.shape[1]
+    parts = [sum_ref[head][:, :HD] / sum_ref[head][:, HD : HD + 1] for head in range(q_ref.shape[0])]
+    first, last = pack_heads(jnp.concatenate(parts, axis=1))
+    joined_ref[0, :rows] = first.astype(BF16)
+    joined_ref[0, rows:] = last.astype(BF16)
 
 
 def attend_heads(bounds, q_ext, k_ext, v_ext, rows, window=1024, align=16):
@@ -565,13 +611,13 @@
         functools.partial(attend_kernel, window, align),
         out_shape=(
             jax.ShapeDtypeStruct((heads, length, lanes), F32),
-            jax.ShapeDtypeStruct((length // rows, rows, heads * HD), BF16),
+            jax.ShapeDtypeStruct((length // rows, packed_heads(rows), LANES), BF16),
         ),
         grid_spec=pltpu.PrefetchScalarGridSpec(
             num_scalar_prefetch=2,
             grid=(length // rows,),
             in_specs=[part, whole, whole],
-            out_specs=(part, pl.BlockSpec((1, rows, heads * HD), lambda i, *_: (i, 0, 0))),
+            out_specs=(part, pl.BlockSpec((1, packed_heads(rows), LANES), lambda i, *_: (i, 0, 0))),
         ),
         compiler_params=pltpu.CompilerParams(vmem_limit_bytes=VMEM_LIMIT),
         cost_estimate=pl.CostEstimate(
@@ -611,8 +657,9 @@
 
     dq_ref[...] = jnp.zeros_like(dq_ref)
     half_lane = lax.broadcasted_iota(jnp.int32, (rows, HD), 1)
+    dout_all = unpack_heads(dout_ref[0].astype(F32))
     for head in range(heads):
-        dout = dout_ref[0, :, head * HD : (head + 1) * HD].astype(F32)
+        dout = dout_all[:, head * HD : (head + 1) * HD]
         sums = sum_ref[head]
         total = sums[:, HD : HD + 1]
         g_low = dout / total
@@ -678,7 +725,8 @@
 
 def attend_back_heads(bounds, q_ext, k_ext, v_ext, sums, dout, turn, window=512, align=128):
     heads, length, lanes = q_ext.shape
-    count_blocks, rows, width = dout.shape
+    count_blocks = dout.shape[0]
+    rows, width = length // count_blocks, heads * HD
     low, count = windows(bounds, length, window, align)
     whole = pl.BlockSpec((heads, length, lanes), lambda i, *_: (0, 0, 0))
     part = pl.BlockSpec((heads, rows, lanes), lambda i, *_: (0, i, 0))
@@ -691,7 +739,7 @@
             in_specs=[
                 part,
                 part,
-                pl.BlockSpec((1, rows, width), lambda i, *_: (i, 0, 0)),
+                pl.BlockSpec((1,) + dout.shape[1:], lambda i, *_: (i, 0, 0)),
                 pl.BlockSpec((length, lanes), lambda i, *_: (0, 0)),
                 whole,
                 whole,
@@ -719,12 +767,19 @@
     chunks,
     by_z,
     part_ref,
-    dh_ref,
+    dh_hbm,
     gw_ref,
     norm_ref,
-    out_ref,
+    own_ref,
+    out_hbm,
     gw_all_ref,
     norm_out_ref,
+    rows_ref,
+    mine,
+    pass_z,
+    pass_y,
+    dh_ref,
+    out_ref,
     got_y,
     got_z,
     relay_y,
@@ -745,6 +800,8 @@
     gw_recv,
     norm_send,
     norm_recv,
+    own_send,
+    own_recv,
     kept,
 ):
     me = lax.axis_index("seq")
@@ -754,13 +811,15 @@
     y_near, z_near, partner = flip(me, 1), flip(me, 2), flip(me, 4)
     corner = flip(y_near, 2)
     barrier = pltpu.get_barrier_semaphore()
-    for device in (y_near, z_near, partner, corner):
-        pl.semaphore_signal(barrier, inc=1, device_id={"seq": device}, device_id_type=BY_MESH)
+    for n in range(1, SEQ_SIZE):
+        pl.semaphore_signal(
+            barrier, inc=1, device_id={"seq": lax.rem(me + n, SEQ_SIZE)}, device_id_type=BY_MESH
+        )
     for step in range(1, shards):
         pl.semaphore_signal(
             barrier, inc=1, device_id={"shard": lax.rem(shard + step, shards)}, device_id_type=BY_MESH
         )
-    pl.semaphore_wait(barrier, 3 + shards)
+    pl.semaphore_wait(barrier, SEQ_SIZE + shards - 2)
 
     started = []
 
@@ -788,6 +847,18 @@
     def slot(kind, far, chunk):
         return (kind * 2 + (0 if far else 1)) * chunks + chunk
 
+    loads = [pltpu.make_async_copy(dh_hbm, dh_ref, kept.at[8])]
+    for which, far in enumerate((True, False)):
+        device = piece(z_near, far)
+        split = by_z * rows
+        loads += [
+            pltpu.make_async_copy(part_ref.at[device, pl.ds(0, split)], pass_z.at[which], kept.at[2 + which]),
+            pltpu.make_async_copy(
+                part_ref.at[piece(y_near, far), pl.ds(split, (chunks - by_z) * rows)], pass_y.at[which], kept.at[4 + which]
+            ),
+            pltpu.make_async_copy(part_ref.at[piece(me, far)], mine.at[which], kept.at[6 + which]),
+        ]
+
     gw_one = [
         go(
             gw_ref.at[lax.rem(shard + step, shards)],
@@ -799,17 +870,37 @@
         )
         for step in range(1, shards)
     ]
-    pairs = [
-        {"shard": flip(shard, 1)},
-        {"shard": flip(shard, 2)},
-        {"seq": y_near},
-        {"seq": z_near},
-        {"seq": partner},
+    norm_seq = [
+        go(norm_ref, norm_got.at[n], norm_send, norm_recv, n, {"seq": lax.rem(me + n + 1, SEQ_SIZE)})
+        for n in range(SEQ_SIZE - 1)
     ]
-    norm_sent[0] = norm_ref[...]
 
     from_corner, direct = {}, {}
-    for far in (True, False):
+
+    own_rows = own_ref.shape[0] // chunks
+    all_rows = own_ref.shape[0]
+
+    def own_band(device, chunk):
+        return rows_ref.at[pl.ds(device * all_rows + chunk * own_rows, own_rows)]
+
+    def spread(device, chunk, kind, where):
+        source = own_band(device, chunk)
+        return go(source, source, own_send, own_recv, kind * chunks + chunk, {"seq": where})
+
+    def spread_own(kind, where):
+        return [
+            go(
+                own_ref.at[pl.ds(chunk * own_rows, own_rows)],
+                own_band(me, chunk),
+                own_send,
+                own_recv,
+                kind * chunks + chunk,
+                {"seq": where},
+            )
+            for chunk in range(chunks)
+        ]
+
+    def send_pieces(far):
         for chunk in range(chunks):
             over_z = chunk < by_z
             from_corner[far, chunk] = go(
@@ -822,30 +913,20 @@
             )
         for chunk in range(chunks):
             over_z = chunk < by_z
-            near = y_near if over_z else z_near
             direct[far, chunk] = go(
-                part_ref.at[piece(near, far), band(chunk)],
+                part_ref.at[piece(y_near if over_z else z_near, far), band(chunk)],
                 (got_y if over_z else got_z).at[0 if far else 1, band(chunk)],
                 send,
                 recv,
                 slot(1 if over_z else 2, far, chunk),
-                {"seq": near},
+                {"seq": y_near if over_z else z_near},
             )
 
-    norm_copies = [go(norm_sent.at[0], norm_got.at[0], norm_send, norm_recv, 0, pairs[0])]
-    done_norm = 0
-
-    def norm_step(index):
-        norm_copies[index].wait_recv()
-        total = norm_sent[index] + norm_got[index]
-        if index + 1 < len(pairs):
-            norm_sent[index + 1] = total
-            norm_copies.append(
-                go(norm_sent.at[index + 1], norm_got.at[index + 1], norm_send, norm_recv, index + 1, pairs[index + 1])
-            )
-        else:
-            norm_out_ref[...] = total
-
+    send_pieces(True)
+    for copy in loads:
+        copy.start()
+    keep_rows = pltpu.make_async_copy(own_ref, rows_ref.at[pl.ds(me * all_rows, all_rows)], kept.at[1])
+    keep_rows.start()
     relayed = {}
 
     def relay(far, chunk):
@@ -856,8 +937,8 @@
         from_corner[far, chunk].wait_recv()
         source = relay_y if over_z else relay_z
         buffer = sent_y if over_z else sent_z
-        mine = part_ref[piece(target, far), band(chunk)].astype(F32)
-        buffer[which, index] = (source[which, index].astype(F32) + mine).astype(BF16)
+        passed = (pass_z if over_z else pass_y)[which, band(index)].astype(F32)
+        buffer[which, index] = (source[which, index].astype(F32) + passed).astype(BF16)
         relayed[far, chunk] = go(
             buffer.at[which, index],
             (got_z if over_z else got_y).at[which, band(chunk)],
@@ -871,31 +952,58 @@
         which = 0 if far else 1
         direct[far, chunk].wait_recv()
         relayed[far, chunk].wait_recv()
-        mine = part_ref[piece(me, far), band(chunk)].astype(F32)
-        return mine + got_y[which, band(chunk)].astype(F32) + got_z[which, band(chunk)].astype(F32)
-
+        return mine[which, band(chunk)].astype(F32) + got_y[which, band(chunk)].astype(F32) + got_z[which, band(chunk)].astype(F32)
+
+    for copy in loads:
+        copy.wait()
     for chunk in range(chunks):
         relay(True, chunk)
-    norm_step(0)
+    send_pieces(False)
+    norm_total = norm_ref[...]
+    for n, copy in enumerate(norm_seq):
+        copy.wait_recv()
+        norm_total = norm_total + norm_got[n]
+    norm_sent[...] = norm_total
     for copy in gw_one:
         copy.wait_recv()
     summed = gw_ref[shard].astype(F32)
     for step in range(1, shards):
         summed = summed + gw_got[step - 1].astype(F32)
     gw_mine[...] = summed.astype(BF16)
-    norm_step(1)
     gw_two = go(gw_mine, gw_pair, gw_send, gw_recv, shards - 1, {"seq": partner})
+    norm_shard = [
+        go(
+            norm_sent,
+            norm_got.at[SEQ_SIZE - 2 + step],
+            norm_send,
+            norm_recv,
+            SEQ_SIZE - 2 + step,
+            {"shard": lax.rem(shard + step, shards)},
+        )
+        for step in range(1, shards)
+    ]
     crossing = []
     for chunk in range(chunks):
         cross_out[band(chunk)] = total(True, chunk).astype(BF16)
         crossing.append(
             go(cross_out.at[band(chunk)], cross_in.at[band(chunk)], send, recv, slot(3, True, chunk), {"seq": partner})
         )
+    rows_cross, rows_y, rows_z = spread_own(0, partner), spread_own(1, y_near), spread_own(2, z_near)
+    for chunk in range(chunks):
         relay(False, chunk)
-    norm_step(2)
+    rows_cross_y, rows_cross_z, rows_corner = [], [], []
+    for chunk in range(chunks):
+        rows_y[chunk].wait_recv()
+        if chunk >= by_z:
+            rows_corner.append(spread(y_near, chunk, 5, z_near))
+        rows_z[chunk].wait_recv()
+        if chunk < by_z:
+            rows_corner.append(spread(z_near, chunk, 5, y_near))
+        rows_cross[chunk].wait_recv()
+        rows_cross_y.append(spread(partner, chunk, 3, y_near))
+        rows_cross_z.append(spread(partner, chunk, 4, z_near))
     gw_two.wait_recv()
     gw_final[...] = (gw_mine[...].astype(F32) + gw_pair[...].astype(F32)).astype(BF16)
-    norm_step(3)
     group = lax.rem(me, GROUPS)
     gw_three = [
         go(gw_final, gw_all_ref.at[group], gw_send, gw_recv, shards + n, {"seq": device})
@@ -904,23 +1012,42 @@
     keep = pltpu.make_async_copy(gw_final, gw_all_ref.at[group], kept.at[0])
     keep.start()
     for chunk in range(chunks):
-        out_ref[half, band(chunk)] = (total(False, chunk) + dh_ref[half, band(chunk)]).astype(BF16)
-    norm_step(4)
+        rows_cross_y[chunk].wait_recv()
+        if chunk >= by_z:
+            rows_corner.append(spread(flip(y_near, 4), chunk, 6, z_near))
+        rows_cross_z[chunk].wait_recv()
+        if chunk < by_z:
+            rows_corner.append(spread(flip(z_near, 4), chunk, 6, y_near))
+    for chunk in range(chunks):
+        out_ref[0, band(chunk)] = (total(False, chunk) + dh_ref[half, band(chunk)]).astype(BF16)
+    out_near = pltpu.make_async_copy(out_ref.at[0], out_hbm.at[half], kept.at[2])
+    out_near.start()
+    norm_total = norm_sent[...]
+    for step, copy in enumerate(norm_shard):
+        copy.wait_recv()
+        norm_total = norm_total + norm_got[SEQ_SIZE - 1 + step]
+    norm_out_ref[...] = norm_total
     for chunk in range(chunks):
         crossing[chunk].wait_recv()
         other = 1 - half
-        out_ref[other, band(chunk)] = (cross_in[band(chunk)].astype(F32) + dh_ref[other, band(chunk)]).astype(BF16)
-    for copy in gw_three:
+        out_ref[1, band(chunk)] = (cross_in[band(chunk)].astype(F32) + dh_ref[other, band(chunk)]).astype(BF16)
+    out_far = pltpu.make_async_copy(out_ref.at[1], out_hbm.at[1 - half], kept.at[3])
+    out_far.start()
+    for copy in gw_three + rows_corner:
         copy.wait_recv()
     keep.wait()
+    keep_rows.wait()
+    out_near.wait()
+    out_far.wait()
     for copy in started:
         copy.wait_send()
 
 
-def scatter_gradients(partial, dh_one, grad_columns, norms, chunks=4, by_z=3):
+def scatter_gradients(partial, dh_one, grad_columns, norms, owned, chunks=4, by_z=3):
     _, rows, width = partial.shape
     shards, depth, columns = grad_columns.shape
     part = rows // chunks
+    hbm = pl.BlockSpec(memory_space=pltpu.HBM)
     vmem = pl.BlockSpec(memory_space=pltpu.VMEM)
     dma = pltpu.SemaphoreType.DMA
     return pl.pallas_call(
@@ -929,10 +1056,16 @@
             jax.ShapeDtypeStruct(dh_one.shape, BF16),
             jax.ShapeDtypeStruct((GROUPS, depth, columns), BF16),
             jax.ShapeDtypeStruct(norms.shape, F32),
+            jax.ShapeDtypeStruct((SEQ_SIZE * owned.shape[0], width), BF16),
         ),
-        in_specs=[vmem] * 4,
-        out_specs=(vmem,) * 3,
+        in_specs=[hbm, hbm, vmem, vmem, hbm],
+        out_specs=(hbm, vmem, vmem, hbm),
         scratch_shapes=[
+            pltpu.VMEM((2, rows, width), BF16),
+            pltpu.VMEM((2, by_z * part, width), BF16),
+            pltpu.VMEM((2, (chunks - by_z) * part, width), BF16),
+            pltpu.VMEM(dh_one.shape, F32),
+            pltpu.VMEM((2, rows, width), BF16),
             pltpu.VMEM((2, rows, width), BF16),
             pltpu.VMEM((2, rows, width), BF16),
             pltpu.VMEM((2, by_z, part, width), BF16),
@@ -945,22 +1078,28 @@
             pltpu.VMEM((depth, columns), BF16),
             pltpu.VMEM((depth, columns), BF16),
             pltpu.VMEM((depth, columns), BF16),
-            pltpu.VMEM((5,) + norms.shape, F32),
-            pltpu.VMEM((5,) + norms.shape, F32),
+            pltpu.VMEM((SEQ_SIZE + shards - 2,) + norms.shape, F32),
+            pltpu.VMEM(norms.shape, F32),
             dma((7 * chunks,)),
             dma((7 * chunks,)),
             dma((shards + 3,)),
             dma((shards + 3,)),
-            dma((5,)),
-            dma((5,)),
-            dma((1,)),
+            dma((SEQ_SIZE + shards - 2,)),
+            dma((SEQ_SIZE + shards - 2,)),
+            dma((7 * chunks,)),
+            dma((7 * chunks,)),
+            dma((9,)),
         ],
         compiler_params=pltpu.CompilerParams(
             collective_id=2, has_side_effects=True, vmem_limit_bytes=VMEM_LIMIT
         ),
         cost_estimate=pl.CostEstimate(flops=60 * 10**9, bytes_accessed=64 * 2**20, transcendentals=0),
         name="scatter_gradients",
-    )(partial, dh_one, grad_columns, norms)
+    )(partial, dh_one, grad_columns, norms, owned)
+
+
+def padded_rows(blocks, depth):
+    return pl.cdiv((3 * blocks + 1) * depth, SEQ_SIZE * 16) * SEQ_SIZE * 16
 
 
 def feed_forward_kernel(
@@ -1017,7 +1156,7 @@
         h_one = flow[seq].astype(F32)
         for group in range(GROUPS):
             h_one = h_one + jnp.dot(
-                joined_ref[seq * GROUPS + group],
+                unpack_heads(joined_ref[seq * GROUPS + group]),
                 w_out[group * depth : (group + 1) * depth, :],
                 preferred_element_type=F32,
             )
@@ -1134,9 +1273,12 @@
         d_attn = dh_one.astype(BF16)
         d_gate[here, :] = d_attn
         for group in range(GROUPS):
-            dout_ref[seq * GROUPS + group] = lax.dot_general(
+            dout = lax.dot_general(
                 d_attn, w_out[group * depth : (group + 1) * depth, :], BY_LANES, preferred_element_type=F32
-            ).astype(BF16)
+            )
+            first, last = pack_heads(dout)
+            dout_ref[seq * GROUPS + group, :rows] = first.astype(BF16)
+            dout_ref[seq * GROUPS + group, rows:] = last.astype(BF16)
     for kind in range(3):
         for copy in store(kind, blocks - 1):
             copy.wait()
@@ -1144,7 +1286,7 @@
         grad = jnp.zeros((depth, width), F32)
         for seq in range(seqs):
             grad = grad + lax.dot_general(
-                joined_ref[seq * GROUPS + group],
+                unpack_heads(joined_ref[seq * GROUPS + group]),
                 d_gate[seq * rows : (seq + 1) * rows, :],
                 (((0,), (0,)), ((), ())),
                 preferred_element_type=F32,
@@ -1155,6 +1297,15 @@
             staged.at[0, pl.ds(shard * depth, depth)],
             packed_ref.at[shard, pl.ds(3 * blocks * depth, depth)],
             stores.at[0, shard],
+        )
+        for shard in range(shards)
+    ]
+    used = (3 * blocks + 1) * depth
+    rest = packed_ref.shape[1] - used
+    staged[1, :rest, :] = jnp.zeros((rest, width), BF16)
+    last += [
+        pltpu.make_async_copy(
+            staged.at[1, pl.ds(0, rest)], packed_ref.at[shard, pl.ds(used, rest)], stores.at[1, shard]
         )
         for shard in range(shards)
     ]
@@ -1185,7 +1336,7 @@
             jax.ShapeDtypeStruct(joined.shape, BF16),
             jax.ShapeDtypeStruct(tokens.shape, F32),
             jax.ShapeDtypeStruct((4, width), F32),
-            jax.ShapeDtypeStruct((GROUPS, (3 * blocks + 1) * depth, width), BF16),
+            jax.ShapeDtypeStruct((GROUPS, padded_rows(blocks, depth), width), BF16),
         ),
         in_specs=[hbm, vmem, hbm, hbm, hbm, hbm, hbm, vmem],
         out_specs=(hbm, vmem, vmem, vmem, hbm),
@@ -1219,6 +1370,51 @@
     )(tokens, joined, cotangent, w_out, w_gate, w_up, w_down, norms)
 
 
+def unpack_kernel(gate_rows, up_rows, down_rows, out_rows, columns, gate_ref, up_ref, down_ref, out_ref, qkv_ref):
+    gate_ref[...] = gate_rows[...].astype(F32)
+    up_ref[...] = up_rows[...].astype(F32)
+    down_ref[...] = down_rows[...].astype(F32)
+
+    @pl.when(pl.program_id(0) == 0)
+    def _():
+        out_ref[...] = out_rows[...].astype(F32)
+        groups, _, width = columns.shape
+        width = width // 3
+        for group in range(groups):
+            for part in range(3):
+                at = (part * groups + group) * width
+                qkv_ref[:, at : at + width] = columns[group, :, part * width : (part + 1) * width].astype(F32)
+
+
+def unpack_gradients(rows, columns, blocks):
+    groups, depth, thirds = columns.shape
+    width = rows.shape[1]
+    piece = [
+        pl.BlockSpec((depth, width), lambda i, first=first, step=step: (first + step * i, 0))
+        for first, step in ((0, 1), (blocks, 1), (2 * blocks, 1), (3 * blocks, 0))
+    ]
+    return pl.pallas_call(
+        unpack_kernel,
+        out_shape=(
+            jax.ShapeDtypeStruct((depth, blocks * width), F32),
+            jax.ShapeDtypeStruct((depth, blocks * width), F32),
+            jax.ShapeDtypeStruct((blocks * depth, width), F32),
+            jax.ShapeDtypeStruct((depth, width), F32),
+            jax.ShapeDtypeStruct((depth, groups * thirds), F32),
+        ),
+        grid=(blocks,),
+        in_specs=piece + [pl.BlockSpec(columns.shape, lambda i: (0, 0, 0))],
+        out_specs=(
+            pl.BlockSpec((depth, width), lambda i: (0, i)),
+            pl.BlockSpec((depth, width), lambda i: (0, i)),
+            pl.BlockSpec((depth, width), lambda i: (i, 0)),
+            pl.BlockSpec((depth, width), lambda i: (0, 0)),
+            pl.BlockSpec((depth, groups * thirds), lambda i: (0, 0)),
+        ),
+        name="unpack_gradients",
+    )(rows, rows, rows, rows, columns)
+
+
 def document_places(seg_row):
     length = seg_row.shape[0]
     ids = jnp.arange(LANES - HD, dtype=jnp.int32)[:, None]
@@ -1227,8 +1423,44 @@
     return jnp.arange(length, dtype=jnp.int32) - start
 
 
-def exchange(blocks):
-    return lax.all_to_all(blocks, "seq", 0, 0, tiled=True)
+def exchange_kernel(sent_ref, taken_ref, send, recv, kept):
+    me = lax.axis_index("seq")
+    barrier = pltpu.get_barrier_semaphore()
+    others = [lax.rem(me + step, SEQ_SIZE) for step in range(1, SEQ_SIZE)]
+    for device in others:
+        pl.semaphore_signal(barrier, inc=1, device_id={"seq": device}, device_id_type=BY_MESH)
+    pl.semaphore_wait(barrier, SEQ_SIZE - 1)
+    copies = []
+    for step, device in enumerate(others):
+        copy = pltpu.make_async_remote_copy(
+            src_ref=sent_ref.at[device],
+            dst_ref=taken_ref.at[me],
+            send_sem=send.at[step],
+            recv_sem=recv.at[step],
+            device_id={"seq": device},
+            device_id_type=BY_MESH,
+        )
+        copy.start()
+        copies.append(copy)
+    keep = pltpu.make_async_copy(sent_ref.at[me], taken_ref.at[me], kept)
+    keep.start()
+    keep.wait()
+    for copy in copies:
+        copy.wait()
+
+
+def exchange(blocks, collective_id):
+    hbm = pl.BlockSpec(memory_space=pltpu.HBM)
+    dma = pltpu.SemaphoreType.DMA
+    return pl.pallas_call(
+        exchange_kernel,
+        out_shape=jax.ShapeDtypeStruct(blocks.shape, blocks.dtype),
+        in_specs=[hbm],
+        out_specs=hbm,
+        scratch_shapes=[dma((SEQ_SIZE - 1,)), dma((SEQ_SIZE - 1,)), dma],
+        compiler_params=pltpu.CompilerParams(collective_id=collective_id, has_side_effects=True),
+        name="exchange",
+    )(blocks)
 
 
 def head_columns(w_qkv, group, held):
@@ -1264,19 +1496,22 @@
     def gather(shard):
         return lax.all_gather(shard, "shard", axis=0, tiled=True)
 
-    pieces, w_heads = gather_tokens(tokens, head_columns(w_qkv, me % GROUPS, held), shards)
-    norms = lax.all_gather(jnp.stack([ln1_gain, ln1_bias, ln2_gain, ln2_bias]), "shard", axis=1, tiled=True).astype(F32)
-    full_out, full_gate, full_up, full_down = (gather(w) for w in (w_out, w_gate, w_up, w_down))
     freqs = jnp.exp(jnp.arange(HD // 2, dtype=F32) * (-math.log(ROPE_BASE) / (HD // 2)))
     freq = jnp.tile(freqs, LANES // (HD // 2))[None]
-    place = document_places(seg_row).astype(F32)
+    place = document_places(seg_row).astype(F32).reshape(SEQ_SIZE, 1, row_count)
+    norm_rows = jnp.stack([ln1_gain, ln1_bias, ln2_gain, ln2_bias]).astype(F32)
+    pieces, w_heads, norms, turn = gather_tokens(
+        tokens, head_columns(w_qkv, me % GROUPS, held), norm_rows, place, freq, shards
+    )
+    norms = jnp.transpose(norms, (1, 0, 2)).reshape(4, model_width)
+    full_out, full_gate, full_up, full_down = (gather(w) for w in (w_out, w_gate, w_up, w_down))
     bounds = document_bounds(seg_row, row_count)
-    q_ext, k_ext, v_ext, turn = project_heads(
-        seg_row.astype(F32), place, freq, pieces, w_heads.reshape(model_width, -1), held
+    q_ext, k_ext, v_ext = project_heads(
+        seg_row.astype(F32), turn, pieces, w_heads.reshape(model_width, -1), held
     )
     sums, joined_own = attend_heads(bounds, q_ext, k_ext, v_ext, row_count)
     output, d_joined, dh_one, norms_part, packed = feed_forward(
-        tokens, exchange(joined_own), cotangent, full_out, full_gate, full_up, full_down, norms
+        tokens, exchange(joined_own, 3), cotangent, full_out, full_gate, full_up, full_down, norms
     )
     depth = model_width // shards
     ff_blocks = full_gate.shape[1] // model_width
@@ -1284,27 +1519,18 @@
         packed.reshape(-1, model_width), ("shard", "seq"), scatter_dimension=0, tiled=True
     )
 
-    dout = exchange(d_joined)
+    dout = exchange(d_joined, 4)
     d_heads = attend_back_heads(bounds, q_ext, k_ext, v_ext, sums, dout, turn)
-    w_own = w_heads.reshape(model_width, -1, LANES)[:, :, :HD].reshape(model_width, -1)
+    w_lanes = w_heads.reshape(model_width, -1)
+    w_own = jnp.concatenate(
+        [w_lanes[:, at : at + HD] for at in range(0, w_lanes.shape[1], LANES)], axis=1
+    )
     partial = jnp.einsum("prc,dc->prd", d_heads, w_own, preferred_element_type=F32).astype(BF16)
     grad_columns = jnp.einsum("prd,prc->dc", pieces, d_heads, preferred_element_type=F32).astype(BF16)
-    partial, grad_columns, owned = lax.optimization_barrier((partial, grad_columns, owned))
-    shared = lax.all_gather(owned, "seq", axis=0, tiled=True)
-    input_grad, columns, norm_sums = scatter_gradients(
-        partial, dh_one, grad_columns.reshape(shards, depth, -1), norms_part
-    )
-    grad_qkv = jnp.transpose(columns.reshape(GROUPS, depth, 3, held * HD), (1, 2, 0, 3))
-    grad_qkv = grad_qkv.reshape(depth, 3 * model_width).astype(F32)
-
-    def taken(start, blocks):
-        rows = shared[start : start + blocks * depth].reshape(blocks, depth, model_width)
-        return jnp.transpose(rows, (1, 0, 2)).reshape(depth, blocks * model_width).astype(F32)
-
-    ff_rows = ff_blocks * depth
-    grad_gate, grad_up = taken(0, ff_blocks), taken(ff_rows, ff_blocks)
-    grad_down = shared[2 * ff_rows : 3 * ff_rows].astype(F32)
-    grad_out = taken(3 * ff_rows, 1)
+    input_grad, columns, norm_sums, shared = scatter_gradients(
+        partial, dh_one, grad_columns.reshape(shards, depth, -1), norms_part, owned
+    )
+    grad_gate, grad_up, grad_down, grad_out, grad_qkv = unpack_gradients(shared, columns, ff_blocks)
     shard = lax.axis_index("shard")
     norm_sums = lax.dynamic_slice_in_dim(norm_sums, shard * depth, depth, 1)
     return (

time: 603 us -> 578 us (0.959)
  Pallas kernels: 446 us -> 518 us
  waiting for transfers between devices: 53.5 us -> 2.68 us
  local copies, waits for them, and re-layouts: 39.5 us -> 10.3 us
  starting transfers between devices: 13.1 us -> 0.19 us
    pallas_call x0 -> x3, Pallas kernels: none -> 78.7 us  [the longest x2 71.8 us: exchange(): pl.pallas_call(exchange_kernel, out_shape=jax.ShapeDtypeStruct(blocks.sha...]
    all_to_all x2 -> x0, waiting for transfers between devices: 50.8 us -> none  [exchange(): return lax.all_to_all(blocks, 'seq', 0, 0, tiled=True)]
    all_to_all x2 -> x0, starting transfers between devices: 12.9 us -> none  [exchange(): return lax.all_to_all(blocks, 'seq', 0, 0, tiled=True)]
    pallas_call x1, Pallas kernels: 134 us -> 122 us  [scatter_gradients(): pl.pallas_call(functools.partial(scatter_kernel, chunks, by_z), out_shape...]
    convert_element_type x7 -> x1, local copies, waits for them, and re-layouts: 11.8 us -> 1.32 us  [local_heads(): jnp.einsum('prd,prc->dc', pieces, d_heads, preferred_element_type=F32)]
    pallas_call x3 -> x0, local copies, waits for them, and re-layouts: 10.4 us -> none  [the longest x1 4.25 us: gather_tokens(): pl.pallas_call(functools.partial(gather_kernel, chunks, by_z), out_shape=...]
    pallas_call x1, Pallas kernels: 110 us -> 119 us  [attend_back_heads(): pl.pallas_call(functools.partial(attend_back_kernel, window, align), out_...]
    all_to_all x2 -> x0, local copies, waits for them, and re-layouts: 6.23 us -> none  [exchange(): return lax.all_to_all(blocks, 'seq', 0, 0, tiled=True)]
  transfers between devices with their start and end apart: 8 -> 5, of which waited for: 2 -> 0; matrix products, arithmetic and copies ran while one was open for 9% -> 5% of each run, Pallas kernels for 63% -> 56%
where the time goes in v5:
time: 578 us; the launch traced here: 567 us
  Pallas kernels  518 us (90%)
  matrix products  17.7 us (3%)
  between operations  14.3 us (2%)
  local copies, waits for them, and re-layouts  10.3 us (2%)
    pallas_call x1, Pallas kernels, scatter_gradients(): pl.pallas_call(functools.partial(scatter_kernel, chunks, by_z), out_shape...  122 us
    pallas_call x1, Pallas kernels, attend_back_heads(): pl.pallas_call(functools.partial(attend_back_kernel, window, align), out_...  119 us
    pallas_call x2, Pallas kernels, exchange(): pl.pallas_call(exchange_kernel, out_shape=jax.ShapeDtypeStruct(blocks.sha...  71.8 us
    pallas_call x1, Pallas kernels, gather_tokens(): pl.pallas_call(functools.partial(gather_kernel, chunks, by_z), out_shape=...  70.9 us
    pallas_call x1, Pallas kernels, feed_forward(): pl.pallas_call(feed_forward_kernel, out_shape=(jax.ShapeDtypeStruct(token...  70.4 us
    pallas_call x1, Pallas kernels, attend_heads(): pl.pallas_call(functools.partial(attend_kernel, window, align), out_shape...  42.3 us
    pallas_call x1, Pallas kernels, project_heads(): pl.pallas_call(project_kernel, out_shape=(head_shape, head_shape, head_sh...  15.1 us
  transfers between devices with their start and end apart: 5, of which 0 were waited for; matrix products, arithmetic and copies ran while one was open for 5% of the time, Pallas kernels for 56%

profile of v5, /device:TPU:20, one launch (start us, length us, event | category | flops | bytes accessed | tf_op | source)
XLA Modules:
  0.0 566.9 jit_solution(17638815084108004634)
XLA Ops:
  7.2 0.0 copy-start.3
  7.2 0.0 copy-start.5
  7.2 0.0 copy-start.6
  7.2 0.0 copy-start.7
  7.2 0.0 copy-start.8
  7.2 0.0 copy-start.2
  7.2 0.0 all-gather.5.cloned.1.call-start
  7.3 0.7 all-gather.5.cloned.1.call-update
  8.0 0.0 all-gather.7.cloned.1.call-start
  8.0 0.7 all-gather.7.cloned.1.call-update
  8.7 0.0 copy-start.4
  8.7 0.0 all-gather.9.cloned.1.call-start
  8.8 0.7 all-gather.9.cloned.1.call-update
  9.5 0.0 all-gather.11.cloned.1.call-start
  9.5 0.5 all-gather.11.cloned.1.call-update
  10.0 0.0 reduce-scatter.2.cloned.1.call-start
  10.1 0.0 copy-done.3
  10.1 0.6 fusion.3
  10.8 0.1 slice.46
  10.9 0.1 slice.45
  10.9 0.0 copy-done.5
  11.0 0.0 copy-done.6
  11.0 0.0 copy-done.7
  11.0 0.0 copy-done.8
  11.0 0.6 broadcast_in_dim_tile.3.freq_ref
  11.6 0.0 copy-done.2
  11.6 0.6 copy.42
  12.2 0.0 copy-done.4
  12.3 0.1 broadcast_multiply_fusion
  12.3 0.1 pad_maximum_fusion
  12.5 1.0 copy.52.w_ref
  13.4 0.6 maximum_convert_fusion.n_ref
  14.0 0.2 convert_reduce_fusion
  14.3 0.2 select_reduce_fusion
  14.5 0.6 subtract_convert_fusion.place_ref
  15.1 70.9 %gather_tokens.1 = (bf16[8,512,768]{2,1,0:T(8,128)(2,1)}, bf16[4,192,1152]{2,1,0:T(8,128)(2,1)}, f32[4,4,192]{2,1,0:T(4,128)}, f32[4096,128]{1,0:T(8,128)}) custom-call(bf16[2,512,768]{2,1,0:T(8,128)(2,1)} %tokens_ref.1, bf16[192,1152]{1,0:T(8,128)(2,1)} %copy.52.w_ref, f32[4,192]{1,0:T(4,128)} %maximum_convert_fusion.n_ref, ...), custom_call_target="tpu_custom_call" | custom-call | tf_op jit(solution)/shard_map/gather_tokens/pallas_call | solution.py:489
  86.1 0.7 copy.44
  86.8 0.7 reshape.92.norms_ref
  87.5 0.2 convert_reduce_fusion.1
  87.7 0.5 subtract_minimum_fusion
  88.3 15.1 %project_heads.1 = (bf16[3,4096,128]{2,1,0:T(8,128)(2,1)}, bf16[3,4096,128]{2,1,0:T(8,128)(2,1)}, bf16[3,4096,128]{2,1,0:T(8,128)(2,1)}) custom-call(f32[8,1,512]{2,1,0:T(1,128)} %bitcast.36, f32[4096,128]{1,0:T(8,128)} %get-tuple-element.34.turn_ref, bf16[8,512,768]{2,1,0:T(8,128)(2,1)} %get-tuple-element.35.x_ref, bf16[768,1152]{1,0:T(8,128)(2,1)} %bitcast.27), custom_call_target="tpu_custom_call" | custom-call | flops 7247757312 | bytes 17825792 | tf_op jit(solution)/shard_map/project_heads/pallas_call | solution.py:547
  103.4 42.3 %attend_heads.1 = (f32[3,4096,128]{2,1,0:T(8,128)}, bf16[8,768,128]{2,1,0:T(8,128)(2,1)}) custom-call(s32[8]{0:T(128)} %get-tuple-element.80.low_ref, s32[8]{0:T(128)} %get-tuple-element.81.count_ref, bf16[3,4096,128]{2,1,0:T(8,128)(2,1)} %get-tuple-element.37.q_ref, bf16[3,4096,128]{2,1,0:T(8,128)(2,1)} %get-tuple-element.38.k_ref, ...), custom_call_target="tpu_custom_call" | custom-call | flops 12884901888 | bytes 15728640 | tf_op jit(solution)/shard_map/attend_heads/pallas_call | solution.py:610
  145.7 34.9 %exchange.2.joined_ref = bf16[8,768,128]{2,1,0:T(8,128)(2,1)} custom-call(bf16[8,768,128]{2,1,0:T(8,128)(2,1)} %get-tuple-element.40.sent_ref), custom_call_target="tpu_custom_call" | custom-call | tf_op jit(solution)/shard_map/exchange/pallas_call | solution.py:1455
  180.6 0.0 all-gather.5.cloned.1.call-done.out_hbm
  180.6 0.0 all-gather.7.cloned.1.call-done.gate_hbm
  180.6 0.0 all-gather.9.cloned.1.call-done.up_hbm
  180.7 0.0 all-gather.11.cloned.1.call-done.down_hbm
  180.7 70.4 %feed_forward.1 = (bf16[2,512,768]{2,1,0:T(8,128)(2,1)}, bf16[8,768,128]{2,1,0:T(8,128)(2,1)}, f32[2,512,768]{2,1,0:T(8,128)}, f32[4,768]{1,0:T(4,128)}, bf16[4,2560,768]{2,1,0:T(8,128)(2,1)}) custom-call(bf16[2,512,768]{2,1,0:T(8,128)(2,1)} %tokens_ref.1, bf16[8,768,128]{2,1,0:T(8,128)(2,1)} %exchange.2.joined_ref, bf16[2,512,768]{2,1,0:T(8,128)(2,1)} %cot_ref.1, ...), custom_call_target="tpu_custom_call" | custom-call | flops 47110422528 | bytes 46399488 | tf_op jit(solution)/shard_map/feed_forward/pallas_call | solution.py:1332
  251.1 0.0 copy-start
  251.1 0.0 reduce-scatter.2.cloned.1.call-update
  251.1 1.4 copy-done
  252.5 0.3 fusion.4
  252.9 0.7 concatenate.7
  253.6 36.9 %exchange.3.dout_ref = bf16[8,768,128]{2,1,0:T(8,128)(2,1)} custom-call(bf16[8,768,128]{2,1,0:T(8,128)(2,1)} %get-tuple-element.44.sent_ref), custom_call_target="tpu_custom_call" | custom-call | tf_op jit(solution)/shard_map/exchange/pallas_call | solution.py:1455
  290.5 119.3 %attend_back_heads.1 = bf16[8,512,576]{2,1,0:T(8,128)(2,1)} custom-call(s32[8]{0:T(128)} %get-tuple-element.59.low_ref, s32[8]{0:T(128)} %get-tuple-element.60.count_ref, bf16[3,4096,128]{2,1,0:T(8,128)(2,1)} %get-tuple-element.37.q_ref, f32[3,4096,128]{2,1,0:T(8,128)} %get-tuple-element.43.sum_ref, bf16[8,768,128]{2,1,0:T(8,128)(2,1)} %exchange.3.dout_ref, ...), custom_call_target="tpu_custom_call" | custom-call | flops 32212254720 | bytes 31457280 | tf_op jit(solution)/shard_map/attend_back_heads/pallas_call | solution.py:733
  409.8 8.2 %bitcast_convert_fusion = bf16[768,576]{0,1:T(8,128)(2,1)S(1)} fusion(bf16[8,512,768]{2,1,0:T(8,128)(2,1)} %get-tuple-element.35.x_ref, bf16[8,512,576]{2,1,0:T(8,128)(2,1)} %attend_back_heads.1), kind=kOutput, calls=%fused_computation.1 | convolution fusion | flops 3624321024 | bytes 11894784 | tf_op jit(solution)/shard_map/prd,prc->dc/dot_general | solution.py:1529
  418.1 1.3 copy.48
  419.4 9.5 %convolution_convert_fusion.part_ref = bf16[8,512,768]{2,1,0:T(8,128)(2,1)} fusion(bf16[8,512,576]{2,1,0:T(8,128)(2,1)} %attend_back_heads.1, bf16[768,576]{1,0:T(8,128)(2,1)S(1)} %concatenate.7), kind=kOutput, calls=%fused_computation | convolution fusion | flops 3627024384 | bytes 11894784 | tf_op jit(solution)/shard_map/prc,dc->prd/dot_general | solution.py:1528
  428.8 121.8 %scatter_gradients.1 = (bf16[2,512,768]{2,1,0:T(8,128)(2,1)}, bf16[4,192,576]{2,1,0:T(8,128)(2,1)}, f32[4,768]{1,0:T(4,128)}, bf16[2560,768]{1,0:T(8,128)(2,1)}) custom-call(bf16[8,512,768]{2,1,0:T(8,128)(2,1)} %convolution_convert_fusion.part_ref, f32[2,512,768]{2,1,0:T(8,128)} %get-tuple-element.45.dh_hbm, bf16[4,192,576]{2,1,0:T(8,128)(2,1)} %bitcast.29, ...), custom_call_target="tpu_custom_call" | custom-call | flops 60000002048 | bytes 67108864 | tf_op jit(solution)/shard_map/scatter_gradients/pallas_call | solution.py:1053
  550.6 0.0 copy-start.1
  550.7 6.9 %unpack_gradients.1 = (f32[192,3072]{1,0:T(8,128)}, f32[192,3072]{1,0:T(8,128)}, f32[768,768]{1,0:T(8,128)}, f32[192,768]{1,0:T(8,128)}, f32[192,2304]{1,0:T(8,128)}) custom-call(bf16[2560,768]{1,0:T(8,128)(2,1)} %get-tuple-element.49.gate_rows.up_rows.down_rows.out_rows, bf16[2560,768]{1,0:T(8,128)(2,1)} %get-tuple-element.49.gate_rows.up_rows.down_rows.out_rows, ...), custom_call_target="tpu_custom_call" | custom-call | tf_op jit(solution)/shard_map/unpack_gradients/pallas_call | solution.py:1396
  557.6 1.5 fusion.5
  559.1 0.0 copy-done.1
  559.1 1.1 copy.55
  (8 shorter events, 0.0 us)
Async XLA Ops:
  7.2 2.9 copy-start.3
  7.2 3.8 copy-start.5
  7.2 3.8 copy-start.6
  7.2 3.8 copy-start.7
  7.2 3.8 copy-start.8
  7.2 4.4 copy-start.2
  7.2 173.4 %all-gather.5.cloned.1.call-start = ((), (), s32[]{:S(2)}) async-start(), calls=%async_computation.1 | async-start | bytes 1474560 | tf_op jit(solution)/shard_map/all_gather | solution.py:1497
  8.0 172.7 %all-gather.7.cloned.1.call-start = ((), (), s32[]{:S(2)}) async-start(), calls=%async_computation.2 | async-start | bytes 5898240 | tf_op jit(solution)/shard_map/all_gather | solution.py:1497
  8.7 3.5 copy-start.4
  8.7 171.9 %all-gather.9.cloned.1.call-start = ((), (), s32[]{:S(2)}) async-start(), calls=%async_computation.3 | async-start | bytes 5898240 | tf_op jit(solution)/shard_map/all_gather | solution.py:1497
  9.5 171.2 %all-gather.11.cloned.1.call-start = ((), (), s32[]{:S(2)}) async-start(), calls=%async_computation.4 | async-start | bytes 5898240 | tf_op jit(solution)/shard_map/all_gather | solution.py:1497
  10.0 418.8 %reduce-scatter.2.cloned.1.call-start = ((), (), s32[]{:S(2)}) async-start(), calls=%async_computation.5 | async-start | bytes 16220160 | tf_op jit(solution)/shard_map/reduce_scatter | solution.py:1518
  251.1 1.5 copy-start
  550.6 8.4 %copy-start.1 = (bf16[2,512,768]{2,1,0:T(8,128)(2,1)S(1)}, bf16[2,512,768]{2,1,0:T(8,128)(2,1)}, u32[]{:S(2)}) copy-start(bf16[2,512,768]{2,1,0:T(8,128)(2,1)} %get-tuple-element.96) | copy-start | bytes 4718596
Sparse Core Ops, SparseCore 0:
  9.6 24.8 all-gather.4
  36.1 37.4 all-gather.6
  75.1 37.4 all-gather.8
  114.0 37.4 all-gather.10
  251.2 171.6 reduce-scatter.1
